TPU v7x, 8 devices: a whole 2x2x1 slice. The times are simulated.
8 devices in a mesh: batch: 1 (over z), dap: 8 (over y, x, core).
Axes of the slice: x: 2, y: 2, z: 1, core: 2. Of those that a mesh axis runs over, the one named last changes fastest.
Arguments:
- pair_act: bfloat16 [384, 384, 128], P(('batch', 'dap'))
- pair_mask: int32 [384, 384], P(('batch', 'dap'))
- ln_in_scale: bfloat16 [2, 128], replicated
- ln_in_bias: bfloat16 [2, 128], replicated
- w_in: bfloat16 [2, 128, 512], replicated
- b_in: bfloat16 [2, 512], replicated
- w_gate: bfloat16 [2, 128, 128], replicated
- b_gate: bfloat16 [2, 128], replicated
- ln_out_scale: bfloat16 [2, 128], replicated
- ln_out_bias: bfloat16 [2, 128], replicated
- w_out: bfloat16 [2, 128, 128], replicated
- b_out: bfloat16 [2, 128], replicated
Outputs:
- output: bfloat16 [384, 384, 128], P(('batch', 'dap'))
All inputs are finite; a program needn't handle non-finite values.
Results may differ from a plain program's by a relative error of at most 0.00746334.
Values are sent between devices in bfloat16 or wider.
A program may use at most 1 GiB of HBM per device.

v0:
```python
import jax
import jax.numpy as jnp
from jax import lax
from jax.sharding import PartitionSpec as P

LN_EPS = 1e-5


def layer_norm(values, ln_scale, offset, axis):
    values = values.astype(jnp.float32)
    mean_val = jnp.mean(values, axis=axis, keepdims=True)
    centred = values - mean_val
    var_val = jnp.mean(centred * centred, axis=axis, keepdims=True)
    return centred * lax.rsqrt(var_val + LN_EPS) * ln_scale.astype(jnp.float32) + offset.astype(jnp.float32)


def gated_side(z_norm, mask_f, w_pair, b_pair):
    hidden = w_pair.shape[1] // 2
    projected = jnp.einsum('de,ikd->eik', w_pair, z_norm, preferred_element_type=jnp.float32)
    projected = projected + b_pair.astype(jnp.float32)[:, None, None]
    return (mask_f[None] * jax.nn.sigmoid(projected[hidden:]) * projected[:hidden]).astype(jnp.bfloat16)


def finish_layer(z_rows, z_norm, a_side, b_full, ln_out_s, ln_out_b, w_gate_l, b_gate_l, w_out_l, b_out_l):
    tri_sum = jnp.einsum('cik,cjk->cij', a_side, b_full, preferred_element_type=jnp.float32)
    o_norm = layer_norm(tri_sum, ln_out_s[:, None, None], ln_out_b[:, None, None], 0).astype(jnp.bfloat16)
    update = jnp.einsum('cij,cd->ijd', o_norm, w_out_l, preferred_element_type=jnp.float32)
    update = (update + b_out_l.astype(jnp.float32)).astype(jnp.bfloat16)
    gate_val = jnp.einsum('ijd,de->ije', z_norm, w_gate_l, preferred_element_type=jnp.float32)
    gate_val = jax.nn.sigmoid(gate_val + b_gate_l.astype(jnp.float32))
    return (z_rows.astype(jnp.float32) + gate_val * update.astype(jnp.float32)).astype(jnp.bfloat16)


def solution(mesh):
    row_spec = P(('batch', 'dap'), None, None)
    mask_spec = P(('batch', 'dap'), None)
    vec_spec = P(None, None)
    mat_spec = P(None, None, None)

    def device_fn(z_rows, mask_rows, ln_in_scale, ln_in_bias, w_in, b_in, w_gate, b_gate, ln_out_scale, ln_out_bias, w_out, b_out):
        hidden = w_in.shape[2] // 4
        mask_f = mask_rows.astype(jnp.float32)
        z_cur = z_rows
        for layer_idx in range(w_in.shape[0]):
            z_norm = layer_norm(z_cur, ln_in_scale[layer_idx], ln_in_bias[layer_idx], -1).astype(jnp.bfloat16)
            a_side = gated_side(z_norm, mask_f, w_in[layer_idx, :, :2 * hidden], b_in[layer_idx, :2 * hidden])
            b_own = gated_side(z_norm, mask_f, w_in[layer_idx, :, 2 * hidden:], b_in[layer_idx, 2 * hidden:])
            b_full = lax.all_gather(b_own, 'dap', axis=1, tiled=True)
            z_cur = finish_layer(z_cur, z_norm, a_side, b_full, ln_out_scale[layer_idx], ln_out_bias[layer_idx], w_gate[layer_idx], b_gate[layer_idx], w_out[layer_idx], b_out[layer_idx])
        return z_cur

    return jax.shard_map(device_fn, mesh=mesh, in_specs=(row_spec, mask_spec, vec_spec, vec_spec, mat_spec, vec_spec, mat_spec, vec_spec, vec_spec, vec_spec, mat_spec, vec_spec), out_specs=row_spec, check_vma=False)
```

profile of v0, /device:TPU:0, one launch (start us, length us, event | category | flops | bytes accessed | tf_op | source)
XLA Modules:
  0.0 568.1 jit_solution(16365669297547257992)
XLA Ops:
  6.5 0.0 copy-start.5
  6.5 0.0 copy-start.7
  6.5 0.0 copy-start.6
  6.5 0.0 copy-start.2
  6.5 0.0 all-gather.3.cloned.1.call-start
  6.6 6.7 %copy.31 = bf16[48,384,128]{1,2,0:T(8,128)(2,1)} copy(bf16[48,384,128]{2,1,0:T(8,128)(2,1)} %param.12) | data formatting | bytes 9437184 | tf_op args[0]
  13.3 0.0 copy-start
  13.3 3.4 convert_reduce_fusion.1
  16.7 4.2 fusion.12
  21.0 0.0 copy-done.5
  21.0 0.0 copy-done.7
  21.0 0.0 copy-done.6
  21.0 0.0 copy-done.2
  21.0 0.0 copy-done
  21.0 3.4 add_bitcast_fusion.3
  24.5 0.0 copy-start.3
  24.5 8.2 %add_bitcast_fusion.2 = f32[256,48,384]{0,2,1:T(8,128)} fusion(f32[256]{0:T(256)S(1)} %bitcast.92, bf16[2,128,512]{2,1,0:T(8,128)(2,1)S(1)} %copy-done.2, bf16[48,384,128]{1,2,0:T(8,128)(2,1)S(1)} %copy-done, f32[128]{0:T(128)S(1)} %get-tuple-element.24, f32[128]{0:T(128)S(1)} %get-tuple-element.31, f32[48,384]{1,0:T(8,128)S(1)} %add_rsqrt_fusion.3, ...), kind=kOutput, calls=%fused_computation.6 | convolution fusion | flops 1226833920 | bytes 23808000 | tf_op jit(solution)/shard_map/de,ikd->eik/dot_general | solution.py:19
  32.7 0.0 copy-done.3
  32.7 12.9 %fusion.28 = (bf16[128,48,384]{0,2,1:T(8,128)(2,1)}, bf16[128,48,384]{0,2,1:T(8,128)(2,1)}) fusion(f32[256,48,384]{0,2,1:T(8,128)} %add_bitcast_fusion.2, f32[48,384]{1,0:T(8,128)S(1)} %convert_element_type.225, f32[256,48,384]{0,2,1:T(8,128)S(1)} %add_bitcast_fusion.3), kind=kLoop, calls=%fused_computation.43 | loop fusion | flops 28311552 | bytes 47259648 | tf_op jit(solution)/shard_map/convert_element_type | solution.py:21
  45.6 6.6 %copy.36 = bf16[128,48,384]{2,0,1:T(8,128)(2,1)} copy(bf16[128,48,384]{0,2,1:T(8,128)(2,1)} %get-tuple-element.7) | data formatting | bytes 9437184 | tf_op jit(solution)/shard_map/convert_element_type | solution.py:21
  52.3 0.0 copy-start.8
  52.3 0.0 copy-start.9
  52.3 0.0 copy-start.10
  52.3 0.0 copy-start.11
  52.3 0.0 all-gather.3.cloned.1.call-update
  52.3 0.6 all-gather.5.cloned.1.call-start
  52.9 7.1 %copy.37 = bf16[128,48,384]{2,1,0:T(8,128)(2,1)} copy(bf16[128,48,384]{0,2,1:T(8,128)(2,1)} %get-tuple-element.8) | data formatting | bytes 9437184 | tf_op jit(solution)/shard_map/convert_element_type | solution.py:21
  60.0 0.0 copy-done.8
  60.0 0.0 copy-done.9
  60.0 0.0 copy-done.10
  60.0 0.0 copy-done.11
  60.1 169.2 %all-gather.3.cloned.1.call-done = bf16[128,384,384]{2,0,1:T(8,128)(2,1)} async-done(((bf16[128,48,384]{2,0,1:T(8,128)(2,1)}), bf16[128,384,384]{2,0,1:T(8,128)(2,1)}) %all-gather.3.cloned.1.call-update) | async-done | bytes 37748752 | tf_op jit(solution)/shard_map/all_gather | solution.py:48
  229.3 40.3 %fusion.64 = (f32[48,384]{1,0:T(8,128)S(1)}, f32[128,48,384]{2,1,0:T(8,128)S(1)}) fusion(bf16[128,48,384]{2,1,0:T(8,128)(2,1)} %copy.37, bf16[128,384,384]{2,0,1:T(8,128)(2,1)} %all-gather.3.cloned.1.call-done), kind=kOutput, calls=%fused_computation.106 | convolution fusion | flops 1814280192 | bytes 51978240 | tf_op jit(solution)/shard_map/cik,cjk->cij/dot_general | solution.py:25
  269.7 0.0 slice-start
  269.7 1.0 multiply_reduce_fusion.1
  270.7 0.0 slice-start.1
  270.7 3.9 add_convert_fusion.3
  274.6 0.0 copy-done.4
  274.6 0.0 copy-start.12
  274.6 7.4 %fusion.40 = f32[48,384,128]{1,2,0:T(8,128)} fusion(bf16[128,48,384]{2,1,0:T(8,128)(2,1)} %add_convert_fusion.3, bf16[2,128,128]{2,1,0:T(8,128)(2,1)S(1)} %copy-done.4), kind=kOutput, calls=%fused_computation.64 | convolution fusion | flops 603979776 | bytes 14188544 | tf_op jit(solution)/shard_map/cij,cd->ijd/dot_general | solution.py:27
  282.0 0.0 slice-done
  282.0 0.0 slice-done.1
  282.0 0.0 copy-done.12
  282.0 8.6 %convert_reduce_fusion = (f32[48,384]{1,0:T(8,128)S(1)}, bf16[48,384,128]{1,2,0:T(8,128)(2,1)S(1)}) fusion(f32[48,384,128]{1,2,0:T(8,128)} %fusion.40, f32[128]{0:T(128)S(1)} %get-tuple-element.16, f32[128]{0:T(128)S(1)} %get-tuple-element.35, bf16[48,384,128]{1,2,0:T(8,128)(2,1)S(1)} %bitcast.87, f32[128]{0:T(128)S(1)} %get-tuple-element.24, ...), kind=kOutput, calls=%fused_computation.10 | convolution fusion | flops 648787968 | bytes 23848960 | tf_op jit(solution)/shard_map/ijd,de->ije/dot_general | solution.py:29
  290.7 0.0 copy-start.1
  290.7 1.8 fusion.8
  292.6 3.4 add_bitcast_fusion.1
  296.0 0.0 copy-done.1
  296.0 8.2 %add_bitcast_fusion = f32[256,48,384]{0,2,1:T(8,128)} fusion(f32[256]{0:T(256)S(1)} %bitcast.90, bf16[2,128,512]{2,1,0:T(8,128)(2,1)S(1)} %copy-done.2, bf16[48,384,128]{1,2,0:T(8,128)(2,1)S(1)} %get-tuple-element.28, f32[128]{0:T(128)S(1)} %get-tuple-element.23, f32[128]{0:T(128)S(1)} %get-tuple-element.32, f32[48,384]{1,0:T(8,128)S(1)} %add_rsqrt_fusion.1, ...), kind=kOutput, calls=%fused_computation.4 | convolution fusion | flops 1226833920 | bytes 23808000 | tf_op jit(solution)/shard_map/de,ikd->eik/dot_general | solution.py:19
  304.3 12.9 %fusion.18 = (bf16[128,48,384]{0,2,1:T(8,128)(2,1)}, bf16[128,48,384]{0,2,1:T(8,128)(2,1)}) fusion(f32[256,48,384]{0,2,1:T(8,128)} %add_bitcast_fusion, f32[48,384]{1,0:T(8,128)S(1)} %convert_element_type.225, f32[256,48,384]{0,2,1:T(8,128)S(1)} %add_bitcast_fusion.1), kind=kLoop, calls=%fused_computation.29 | loop fusion | flops 28311552 | bytes 47259648 | tf_op jit(solution)/shard_map/convert_element_type | solution.py:21
  317.1 6.6 %copy.45 = bf16[128,48,384]{2,0,1:T(8,128)(2,1)} copy(bf16[128,48,384]{0,2,1:T(8,128)(2,1)} %get-tuple-element.5) | data formatting | bytes 9437184 | tf_op jit(solution)/shard_map/convert_element_type | solution.py:21
  323.8 0.0 all-gather.5.cloned.1.call-update
  323.8 7.1 %copy.46 = bf16[128,48,384]{2,1,0:T(8,128)(2,1)} copy(bf16[128,48,384]{0,2,1:T(8,128)(2,1)} %get-tuple-element.6) | data formatting | bytes 9437184 | tf_op jit(solution)/shard_map/convert_element_type | solution.py:21
  330.9 167.0 %all-gather.5.cloned.1.call-done = bf16[128,384,384]{2,0,1:T(8,128)(2,1)} async-done(((bf16[128,48,384]{2,0,1:T(8,128)(2,1)}), bf16[128,384,384]{2,0,1:T(8,128)(2,1)}) %all-gather.5.cloned.1.call-update) | async-done | bytes 37748752 | tf_op jit(solution)/shard_map/all_gather | solution.py:48
  498.0 40.7 %fusion.65 = (f32[48,384]{1,0:T(8,128)S(1)}, f32[128,48,384]{2,1,0:T(8,128)S(1)}) fusion(bf16[128,48,384]{2,1,0:T(8,128)(2,1)} %copy.46, bf16[128,384,384]{2,0,1:T(8,128)(2,1)} %all-gather.5.cloned.1.call-done), kind=kOutput, calls=%fused_computation.107 | convolution fusion | flops 1814280192 | bytes 51978240 | tf_op jit(solution)/shard_map/cik,cjk->cij/dot_general | solution.py:25
  538.7 0.0 slice-start.2
  538.7 1.0 multiply_reduce_fusion
  539.7 0.0 slice-start.3
  539.7 3.8 add_convert_fusion.1
  543.5 3.8 fusion.38
  547.2 0.0 slice-done.2
  547.3 0.0 slice-done.3
  547.3 6.9 %fusion.17 = bf16[48,384,128]{1,2,0:T(8,128)(2,1)} fusion(bf16[48,384,128]{1,2,0:T(8,128)(2,1)S(1)} %bitcast.89, f32[48,384,128]{1,2,0:T(8,128)S(1)} %fusion.38, f32[128]{0:T(128)S(1)} %get-tuple-element.15, f32[128]{0:T(128)S(1)} %get-tuple-element.36, bf16[2,128,128]{2,1,0:T(8,128)(2,1)S(1)} %copy-done.12, f32[128]{0:T(128)S(1)} %get-tuple-element.23, ...), kind=kOutput, calls=%fused_computation.27 | convolution fusion | flops 644087808 | bytes 23775232 | tf_op jit(solution)/shard_map/ijd,de->ije/dot_general | solution.py:29
  554.2 6.6 %copy.50 = bf16[48,384,128]{2,1,0:T(8,128)(2,1)} copy(bf16[48,384,128]{1,2,0:T(8,128)(2,1)} %fusion.17) | data formatting | bytes 9437184 | tf_op jit(solution)/shard_map/convert_element_type | solution.py:31
  (16 shorter events, 0.1 us)
Async XLA Ops:
  6.5 14.4 %copy-start.5 = (bf16[2,512]{1,0:T(2,128)(2,1)S(1)}, bf16[2,512]{1,0:T(2,128)(2,1)}, u32[]{:S(2)}) copy-start(bf16[2,512]{1,0:T(2,128)(2,1)} %param.17) | copy-start | bytes 6148
  6.5 14.5 %copy-start.7 = (bf16[2,128]{1,0:T(2,128)(2,1)S(1)}, bf16[2,128]{1,0:T(2,128)(2,1)}, u32[]{:S(2)}) copy-start(bf16[2,128]{1,0:T(2,128)(2,1)} %param.14) | copy-start | bytes 1540
  6.5 14.5 %copy-start.6 = (bf16[2,128]{1,0:T(2,128)(2,1)S(1)}, bf16[2,128]{1,0:T(2,128)(2,1)}, u32[]{:S(2)}) copy-start(bf16[2,128]{1,0:T(2,128)(2,1)} %param.15) | copy-start | bytes 1540
  6.5 14.5 %copy-start.2 = (bf16[2,128,512]{2,1,0:T(8,128)(2,1)S(1)}, bf16[2,128,512]{2,1,0:T(8,128)(2,1)}, u32[]{:S(2)}) copy-start(bf16[2,128,512]{2,1,0:T(8,128)(2,1)} %param.16) | copy-start | bytes 786436
  6.5 222.8 %all-gather.3.cloned.1.call-start = ((), (), s32[]{:S(2)}) async-start(), calls=%async_computation | async-start | bytes 42467328 | tf_op jit(solution)/shard_map/all_gather | solution.py:48
  13.3 7.8 %copy-start = (bf16[48,384,128]{1,2,0:T(8,128)(2,1)S(1)}, bf16[48,384,128]{1,2,0:T(8,128)(2,1)}, u32[]{:S(2)}) copy-start(bf16[48,384,128]{1,2,0:T(8,128)(2,1)} %copy.31) | copy-start | bytes 14155780
  24.5 8.2 %copy-start.3 = (s32[48,384]{1,0:T(8,128)S(1)}, s32[48,384]{1,0:T(8,128)}, u32[]{:S(2)}) copy-start(s32[48,384]{1,0:T(8,128)} %param.13) | copy-start | bytes 221188
  52.3 7.7 %copy-start.8 = (bf16[2,128]{1,0:T(2,128)(2,1)S(1)}, bf16[2,128]{1,0:T(2,128)(2,1)}, u32[]{:S(2)}) copy-start(bf16[2,128]{1,0:T(2,128)(2,1)} %param.21) | copy-start | bytes 1540
  52.3 7.7 %copy-start.9 = (bf16[2,128]{1,0:T(2,128)(2,1)S(1)}, bf16[2,128]{1,0:T(2,128)(2,1)}, u32[]{:S(2)}) copy-start(bf16[2,128]{1,0:T(2,128)(2,1)} %param.20) | copy-start | bytes 1540
  52.3 7.8 %copy-start.10 = (bf16[2,128]{1,0:T(2,128)(2,1)S(1)}, bf16[2,128]{1,0:T(2,128)(2,1)}, u32[]{:S(2)}) copy-start(bf16[2,128]{1,0:T(2,128)(2,1)} %param.23) | copy-start | bytes 1540
  52.3 7.8 %copy-start.11 = (bf16[2,128]{1,0:T(2,128)(2,1)S(1)}, bf16[2,128]{1,0:T(2,128)(2,1)}, u32[]{:S(2)}) copy-start(bf16[2,128]{1,0:T(2,128)(2,1)} %param.19) | copy-start | bytes 1540
  52.3 445.7 %all-gather.5.cloned.1.call-start = ((), (), s32[]{:S(2)}) async-start(), calls=%async_computation.1 | async-start | bytes 42467328 | tf_op jit(solution)/shard_map/all_gather | solution.py:48
  269.7 12.4 %slice-start = ((s8[4718592]{0:T(1024)(128)(4,1)}), s8[4194304]{0:T(1024)(128)(4,1)S(1)}, s32[]{:S(2)}) async-start(s8[4718592]{0:T(1024)(128)(4,1)} %bitcast.86), calls=%async_computation.2 | async-start | bytes 8388608
  270.7 3.9 copy-start.4
  270.7 11.3 %slice-start.1 = ((s8[4718592]{0:T(1024)(128)(4,1)}), s8[524288]{0:T(1024)(128)(4,1)S(1)}, s32[]{:S(2)}) async-start(s8[4718592]{0:T(1024)(128)(4,1)} %bitcast.86), calls=%async_computation.3 | async-start | bytes 1048576
  274.6 7.5 %copy-start.12 = (bf16[2,128,128]{2,1,0:T(8,128)(2,1)S(1)}, bf16[2,128,128]{2,1,0:T(8,128)(2,1)}, u32[]{:S(2)}) copy-start(bf16[2,128,128]{2,1,0:T(8,128)(2,1)} %param.18) | copy-start | bytes 196612
  290.7 5.4 copy-start.1
  538.7 8.6 %slice-start.2 = ((s8[4718592]{0:T(1024)(128)(4,1)}), s8[4194304]{0:T(1024)(128)(4,1)S(1)}, s32[]{:S(2)}) async-start(s8[4718592]{0:T(1024)(128)(4,1)} %bitcast.88), calls=%async_computation.4 | async-start | bytes 8388608
  539.7 7.6 %slice-start.3 = ((s8[4718592]{0:T(1024)(128)(4,1)}), s8[524288]{0:T(1024)(128)(4,1)S(1)}, s32[]{:S(2)}) async-start(s8[4718592]{0:T(1024)(128)(4,1)} %bitcast.88), calls=%async_computation.5 | async-start | bytes 1048576
Sparse Core Ops, SparseCore 0:
  52.4 176.8 all-gather.2
  323.9 173.9 all-gather.4
where the time goes:
time: 576 us; the launch traced here: 568 us
  waiting for transfers between devices  336 us (58%)
  matrix products  131 us (23%)
  other arithmetic  45 us (8%)
  local copies, waits for them, and re-layouts  40.9 us (7%)
  between operations  14.2 us (2%)
    all_gather x2, waiting for transfers between devices, device_fn(): b_full = lax.all_gather(b_own, 'dap', axis=1, tiled=True)  336 us
    dot_general x2, matrix products, finish_layer(): jnp.einsum('cik,cjk->cij', a_side, b_full, preferred_element_type=jnp.flo...  81 us
    convert_element_type x4, local copies, waits for them, and re-layouts, gated_side(): (mask_f[None] * jax.nn.sigmoid(projected[hidden:]) * projected[:hidden])....  27.5 us
    convert_element_type x2, other arithmetic, gated_side(): (mask_f[None] * jax.nn.sigmoid(projected[hidden:]) * projected[:hidden])....  25.8 us
    dot_general x4, matrix products, gated_side(): jnp.einsum('de,ikd->eik', w_pair, z_norm, preferred_element_type=jnp.floa...  23.3 us
    dot_general x2, matrix products, finish_layer(): jnp.einsum('ijd,de->ije', z_norm, w_gate_l, preferred_element_type=jnp.fl...  15.5 us
  transfers between devices with their start and end apart: 2, of which 2 were waited for; matrix products, arithmetic and copies ran while one was open for 3% of the time, Pallas kernels for 0%

commit v1 on v0

v1 whole, which is shorter than its diff:
```python
import functools
import jax
import jax.numpy as jnp
from jax import lax
from jax.experimental import pallas as pl
from jax.experimental.pallas import tpu as pltpu
from jax.sharding import PartitionSpec as P

LN_EPS = 1e-5
ROWS = 16
CHUNK = 32
PITCH = 136
ROW_PITCH = 24
NT = (((1,), (1,)), ((), ()))


def norm_sublanes(x, scale, bias):
    mean = jnp.mean(x, axis=0, keepdims=True)
    xc = x - mean
    var = jnp.mean(xc * xc, axis=0, keepdims=True)
    return xc * lax.rsqrt(var + LN_EPS) * scale + bias


def project_kernel(sides, group, counts, *refs):
    sources, refs = [refs[5 * n:5 * n + 5] for n in range(len(counts))], refs[5 * len(counts):]
    bias_ref, centre, w_ref, ln_s, ln_b = refs[:5]
    outs = refs[6:6 + sides]
    proj, znt, stage = refs[6 + sides:]

    def block(z_refs, mask_ref):
        def normalise(i0):
            for h in range(group):
                z = jnp.concatenate([z_refs[t][i0 + h, 0] for t in range(4)], axis=0)
                xc = lax.dot_general(centre[...], z, NT, preferred_element_type=jnp.float32)
                for lt in range(3):
                    ls = slice(lt * 128, lt * 128 + 128)
                    x = xc[:, ls]
                    var = jnp.mean(x * x, axis=0, keepdims=True)
                    znt[h, :, ls] = (x * lax.rsqrt(var + LN_EPS) * ln_s[...] + ln_b[...]).astype(jnp.bfloat16)

        normalise(0)

        def some(g, carry):
            for h in range(group):
                proj[h] = jnp.dot(w_ref[...], znt[h], preferred_element_type=jnp.float32)
            normalise(jnp.minimum(g + 1, ROWS // group - 1) * group)
            for h in range(group):
                i = g * group + h
                for lt in range(3):
                    ls = slice(lt * 128, lt * 128 + 128)
                    m = mask_ref[i, :, ls]
                    for s in range(sides):
                        value = proj[h, s * 256:s * 256 + 128, ls] + bias_ref[s * 256:s * 256 + 128]
                        gate = proj[h, s * 256 + 128:s * 256 + 256, ls] + bias_ref[s * 256 + 128:s * 256 + 256]
                        stage[s, lt, pl.ds(i, 128, stride=ROW_PITCH), :] = (jnp.tanh(gate) + 1.0) * value * m
            return carry

        lax.fori_loop(0, ROWS // group, some, 0)

    if len(counts) == 1:
        block(sources[0][:4], sources[0][4])
    else:
        first = pl.program_id(0) < counts[0]
        pl.when(first)(lambda: block(sources[0][:4], sources[0][4]))
        pl.when(jnp.logical_not(first))(lambda: block(sources[1][:4], sources[1][4]))

    def chan(c, carry):
        for s in range(sides):
            for lt in range(3):
                outs[s][c, :, lt * 128:lt * 128 + 128] = stage[s, lt, pl.ds(pl.multiple_of(c * ROW_PITCH, 8), ROWS), :].astype(jnp.bfloat16)
        return carry

    lax.fori_loop(0, 128, chan, 0, unroll=8)


def project(sources, bias, w_t, ln_s, ln_b, centre, sides, dep, group=4):
    counts = [mask.shape[0] // ROWS for _, mask in sources]
    rows = sum(counts) * ROWS
    full = lambda *shape: pl.BlockSpec(shape, lambda r: (0,) * len(shape))
    in_specs, args, start = [], [], 0
    for (tiles, mask), count in zip(sources, counts):
        at = functools.partial(lambda lo, n, r: jnp.minimum(jnp.maximum(r - lo, 0), n - 1), start, count)
        for arr, blk in tiles:
            in_specs.append(pl.BlockSpec((ROWS, 1, 96, 128), functools.partial(lambda at, b, r: (at(r), b, 0, 0), at, blk)))
            args.append(arr)
        in_specs.append(pl.BlockSpec((ROWS, 1, 384), functools.partial(lambda at, r: (at(r), 0, 0), at)))
        args.append(mask)
        start += count
    in_specs += [full(256 * sides, 128), full(128, 128), full(256 * sides, 128), full(128, 128), full(128, 128), pl.BlockSpec(memory_space=pl.ANY)]
    return pl.pallas_call(
        functools.partial(project_kernel, sides, group, counts),
        grid=(rows // ROWS,),
        out_shape=[jax.ShapeDtypeStruct((128, rows, 384), jnp.bfloat16)] * sides,
        in_specs=in_specs,
        out_specs=[pl.BlockSpec((128, ROWS, 384), lambda r: (0, r, 0))] * sides,
        scratch_shapes=[pltpu.VMEM((group, 256 * sides, 384), jnp.float32), pltpu.VMEM((group, 128, 384), jnp.bfloat16), pltpu.VMEM((sides, 3, 128 * ROW_PITCH, 128), jnp.float32)],
        compiler_params=pltpu.CompilerParams(dimension_semantics=('arbitrary',), vmem_limit_bytes=62 * 2**20),
        cost_estimate=pl.CostEstimate(flops=rows * 384 * 128 * 512 * sides, bytes_accessed=rows * 384 * 256 * (1 + sides), transcendentals=0),
        name='project',
    )(*args, bias, centre, w_t, ln_s, ln_b, dep)


def triangle_kernel(sets, n_b, group, where_ref, *refs):
    pieces = [(s, n) for s, counts in enumerate(sets) for n in counts]
    a_refs, refs = refs[:len(pieces)], refs[len(pieces):]
    b_refs, refs = refs[:n_b], refs[n_b:]
    z_refs, refs = refs[:len(pieces)], refs[len(pieces):]
    perm_ref, w_out, b_out, w_gate, b_gate, ln_s, ln_b, in_s, in_b, centre = refs[:10]
    outs = refs[11:11 + len(sets)]
    tri, = refs[11 + len(sets):]
    step = pl.program_id(0)
    rows = sum(n for _, n in pieces)

    @pl.when(step == 0)
    def _():
        tri[:, 96:128] = jnp.zeros((rows * PITCH, 32), jnp.float32)

    def chan(cc, carry):
        a = jnp.concatenate([r[cc] for r in a_refs], axis=0)
        b = jnp.concatenate([r[cc] for r in b_refs], axis=0)
        tri[pl.ds(step * CHUNK + cc, rows, stride=PITCH), 0:96] = lax.dot_general(a, b, NT, preferred_element_type=jnp.float32)
        return carry

    lax.fori_loop(0, CHUNK, chan, 0, unroll=CHUNK)

    @pl.when(step == pl.num_programs(0) - 1)
    def _():
        row0 = 0
        done = [0] * len(sets)
        for k, (s, count) in enumerate(pieces):
            def some(i, carry, k=k, s=s, row0=row0, out0=done[s]):
                i0 = i * group
                flipped = []
                for q in range(group):
                    o = tri[pl.ds(pl.multiple_of((row0 + i0 + q) * PITCH, 8), 128), :]
                    on = norm_sublanes(o, ln_s[...], ln_b[...]).astype(jnp.bfloat16)
                    flipped.append(lax.dot_general(perm_ref[...], on, NT, preferred_element_type=jnp.float32).astype(jnp.bfloat16))
                on = jnp.concatenate(flipped, axis=0)
                u = jnp.dot(on, w_out[...], preferred_element_type=jnp.float32) + b_out[...]
                u = u.astype(jnp.bfloat16).astype(jnp.float32)
                zb = z_refs[k][pl.ds(i0, group), 0].reshape(group * 96, 128)
                xc = jnp.dot(zb, centre[...], preferred_element_type=jnp.float32)
                z = zb.astype(jnp.float32)
                var = jnp.mean(xc * xc, axis=-1, keepdims=True)
                zn = (xc * lax.rsqrt(var + LN_EPS) * in_s[...] + in_b[...]).astype(jnp.bfloat16)
                g = jnp.dot(zn, w_gate[...], preferred_element_type=jnp.float32) + b_gate[...]
                g = 0.5 * jnp.tanh(g) + 0.5
                outs[s][pl.ds(out0 + i0, group), 0] = (z + g * u).astype(jnp.bfloat16).reshape(group, 96, 128)
                return carry

            lax.fori_loop(0, count // group, some, 0)
            row0 += count
            done[s] += count


def triangle(where, sets, b_pieces, params, dep, into=None, group=16):
    flat = [p for pieces in sets for p in pieces]
    rows = sum(p[2] for p in flat)

    def tile_spec(n, rel):
        if rel is None:
            return pl.BlockSpec((n, 1, 96, 128), lambda c, w: (0, 0, 0, 0))
        return pl.BlockSpec((n, 1, 96, 128), lambda c, w: (0, w[0] ^ rel, 0, 0))

    chan_spec = lambda n, blk: pl.BlockSpec((CHUNK, n, 384), lambda c, w: (c, blk, 0))
    full = lambda *shape: pl.BlockSpec(shape, lambda c, w: (0,) * len(shape))
    in_specs = [chan_spec(p[2], p[1]) for p in flat] + [chan_spec(n, blk) for _, blk, n in b_pieces]
    in_specs += [tile_spec(p[2], p[4]) for p in flat]
    in_specs += [full(96, 128), full(128, 128), full(1, 128), full(128, 128), full(1, 128), full(128, 128), full(128, 128), full(1, 128), full(1, 128), full(128, 128)]
    in_specs.append(pl.BlockSpec(memory_space=pl.ANY))
    sizes = [[p[2] for p in pieces] for pieces in sets]
    width, out_rel, aliases = 1, None, {}
    if into is not None:
        width, out_rel = 4, into[1]
        if into[0] is not None:
            dep, aliases = into[0], {len(in_specs): 0}
    return pl.pallas_call(
        functools.partial(triangle_kernel, sizes, len(b_pieces), group),
        out_shape=[jax.ShapeDtypeStruct((sum(n), width, 96, 128), jnp.bfloat16) for n in sizes],
        input_output_aliases=aliases,
        grid_spec=pltpu.PrefetchScalarGridSpec(
            num_scalar_prefetch=1, grid=(128 // CHUNK,), in_specs=in_specs,
            out_specs=[tile_spec(sum(n), out_rel) for n in sizes],
            scratch_shapes=[pltpu.VMEM((rows * PITCH, 128), jnp.float32)]),
        compiler_params=pltpu.CompilerParams(dimension_semantics=('arbitrary',), vmem_limit_bytes=62 * 2**20),
        cost_estimate=pl.CostEstimate(flops=rows * 96 * 128 * 1800, bytes_accessed=(rows + 96) * 384 * 256, transcendentals=0),
        name='triangle',
    )(where, *[p[0] for p in flat], *[b for b, _, _ in b_pieces], *[p[3] for p in flat], *params, dep)


def solution(mesh):
    row_spec = P(('batch', 'dap'), None, None)
    mask_spec = P(('batch', 'dap'), None)
    vec_spec = P(None, None)
    mat_spec = P(None, None, None)

    def swap(x, bit):
        return lax.ppermute(x, 'dap', [(i, i ^ bit) for i in range(8)])

    def hold(x, *others):
        return lax.optimization_barrier((x,) + others)[0]

    def device_fn(z_rows, mask_rows, ln_in_scale, ln_in_bias, w_in, b_in, w_gate, b_gate, ln_out_scale, ln_out_bias, w_out, b_out):
        f32, bf16 = jnp.float32, jnp.bfloat16
        index = lax.axis_index('dap')
        chip, core = index // 2, index % 2
        z_own = z_rows.reshape(48, 4, 96, 128)
        z_xa, z_ya = swap(z_own[:32], 2), swap(z_own[:32], 4)
        z_xb, z_yb = swap(z_own[32:], 2), swap(z_own[32:], 4)
        mask_bf = mask_rows
        mask_x, mask_y = swap(mask_bf, 2), swap(mask_bf, 4)
        masks = [m.astype(f32)[:, None] for m in (mask_bf, mask_x, mask_y)]
        order = jnp.stack([chip ^ t for t in range(4)])
        masks_rel = [jnp.take(m.reshape(48, 1, 4, 96), order, axis=2).reshape(48, 1, 384) for m in masks]
        j = jnp.arange(96)
        source = jnp.where(core == 0, j, (j + 48) % 96)
        perm = (source[:, None] == jnp.arange(128)[None, :]).astype(bf16)
        eye = jnp.arange(128)[:, None] == jnp.arange(128)[None, :]
        centre = (eye.astype(f32) - 1.0 / 128).astype(bf16)
        zero = jnp.zeros((1,), jnp.int32)
        where = jnp.reshape(chip, (1,)).astype(jnp.int32)
        lanes = lambda v: jnp.broadcast_to(v.astype(f32)[:, None], (v.shape[0], 128))
        half = bf16(0.5)

        def weights(l):
            proj = (lanes(b_in[l].astype(f32) * 0.5), w_in[l].T * half, lanes(ln_in_scale[l]), lanes(ln_in_bias[l]), centre)
            tri = (perm, w_out[l], b_out[l].astype(f32)[None], w_gate[l] * half, b_gate[l].astype(f32)[None] * 0.5,
                   lanes(ln_out_scale[l]), lanes(ln_out_bias[l]), ln_in_scale[l].astype(f32)[None], ln_in_bias[l].astype(f32)[None], centre)
            return proj, tri

        (bias, w_t, ls, lb, ce), tri = weights(0)
        spread = lambda arr: [(arr, i) for i in range(4)]
        a_o, b_o = project([(spread(z_own), masks[0])], bias, w_t, ls, lb, ce, 2, perm)
        b_o2 = swap(b_o, 1)
        set_o = lambda t: [(a_o, 0, 48, z_own, t)]
        o0, = triangle(where, [set_o(0)], [(b_o, 0, 48), (b_o2, 0, 48)], tri, a_o)
        a_a, b_a = project([(spread(z_xa), masks[1][:32]), (spread(z_ya), masks[2][:32])], bias, w_t, ls, lb, ce, 2, o0)
        b_a2 = swap(b_a, 1)
        a_b, b_b = project([(spread(z_xb), masks[1][32:]), (spread(z_yb), masks[2][32:])], bias, w_t, ls, lb, ce, 2, a_a)
        b_b2 = swap(b_b, 1)
        o0s = hold(o0, z_xb, z_yb)
        x1, y2 = swap(o0s, 2), swap(o0s, 4)
        cols = lambda k: [(b_a, k, 32), (b_b, k, 16), (b_a2, k, 32), (b_b2, k, 16)]
        set_x = [(a_a, 0, 32, z_xa, 2), (a_b, 0, 16, z_xb, 2)]
        o2, x2 = triangle(where, [set_o(2), set_x], cols(1), tri, a_b)
        o3 = swap(x2, 2)
        o1, = triangle(where, [set_o(1)], cols(0), tri, o2)
        y3 = swap(o1, 4)
        set_x = [(a_a, 0, 32, z_xa, 0), (a_b, 0, 16, z_xb, 0)]
        set_y = [(a_a, 1, 32, z_ya, 0), (a_b, 1, 16, z_yb, 0)]
        x0, y0 = triangle(where, [set_x, set_y], [(b_o, 0, 48), (b_o2, 0, 48)], tri, o1)
        x3 = swap(o2, 2)
        y1 = swap(o3, 4)

        (bias, w_t, ls, lb, ce), tri = weights(1)
        tiles = lambda *arrs: [(arr, 0) for arr in arrs]
        a_o1, b_o1 = project([(tiles(o0, o1, o2, o3), masks_rel[0])], bias, w_t, ls, lb, ce, 2, x0)
        b_o12 = swap(b_o1, 1)
        set_o = lambda z: [(a_o1, 0, 48, z, None)]
        a_x1, b_x1 = project([(tiles(x0, x1, x2, x3), masks_rel[1])], bias, w_t, ls, lb, ce, 2, a_o1)
        b_x12 = swap(b_x1, 1)
        b_y1, = project([(tiles(y0, y1, y2, y3), masks_rel[2])], bias[256:], w_t[256:], ls, lb, ce, 1, a_x1)
        b_y12 = swap(b_y1, 1)
        out, = triangle(where, [set_o(o0)], [(b_o1, 0, 48), (b_o12, 0, 48)], tri, b_y1, (None, 0))
        q2, = triangle(where, [[(a_x1, 0, 48, x2, None)]], [(b_y1, 0, 48), (b_y12, 0, 48)], tri, out)
        p3 = swap(q2, 2)
        out, = triangle(where, [set_o(o2)], [(b_y1, 0, 48), (b_y12, 0, 48)], tri, q2, (out, 2))
        out, = triangle(where, [set_o(o1)], [(b_x1, 0, 48), (b_x12, 0, 48)], tri, q2, (out, 1))
        out = lax.dynamic_update_slice(out, p3, (0, chip ^ 3, 0, 0))
        return out.reshape(48, 384, 128)

    return jax.shard_map(device_fn, mesh=mesh, in_specs=(row_spec, mask_spec, vec_spec, vec_spec, mat_spec, vec_spec, mat_spec, vec_spec, vec_spec, vec_spec, mat_spec, vec_spec), out_specs=row_spec, check_vma=False)
```

time: 576 us -> 388 us (0.67); the launches traced: 568 us -> 388 us
  Pallas kernels: 0 us -> 216 us
  waiting for transfers between devices: 336 us -> 124 us
  matrix products: 131 us -> 0 us
  other arithmetic: 45 us -> 7.02 us
  local copies, waits for them, and re-layouts: 40.9 us -> 24.7 us
  starting transfers between devices: 0.6 us -> 16.2 us
  between operations: 14.2 us -> 0.35 us
    all_gather x2 -> x0, waiting for transfers between devices: 336 us -> none  [device_fn(): b_full = lax.all_gather(b_own, 'dap', axis=1, tiled=True)]
    pallas_call x0 -> x14, Pallas kernels: none -> 216 us  [the longest x8 115 us: triangle(): pl.pallas_call(functools.partial(triangle_kernel, sizes, len(b_pieces), g...]
    dot_general x10 -> x0, matrix products: 131 us -> none  [the longest x2 81 us: finish_layer(): jnp.einsum('cik,cjk->cij', a_side, b_full, preferred_element_type=jnp.flo...]
    ppermute x0 -> x19, waiting for transfers between devices: none -> 124 us  [swap(): return lax.ppermute(x, 'dap', [(i, i ^ bit) for i in range(8)])]
    convert_element_type x5 -> x0, local copies, waits for them, and re-layouts: 34.1 us -> none  [the longest x4 27.5 us: gated_side(): (mask_f[None] * jax.nn.sigmoid(projected[hidden:]) * projected[:hidden])....]
    convert_element_type x9, other arithmetic: 33.4 us -> 4.14 us  [the longest x3 1.35 us: device_fn(): v.astype(f32)[:, None]]
    ppermute x0 -> x19, starting transfers between devices: none -> 16.2 us  [swap(): return lax.ppermute(x, 'dap', [(i, i ^ bit) for i in range(8)])]
    reduce_sum x5 -> x0, other arithmetic: 11.5 us -> none  [the longest x4 8.02 us: layer_norm(): var_val = jnp.mean(centred * centred, axis=axis, keepdims=True)]
  transfers between devices with their start and end apart: 2 -> 19, of which waited for: 2 -> 8; matrix products, arithmetic and copies ran while one was open for 3% -> 5% of each run, Pallas kernels for 0% -> 41%
where the time goes in v1:
time: 388 us
  Pallas kernels  216 us (56%)
  waiting for transfers between devices  124 us (32%)
  local copies, waits for them, and re-layouts  24.7 us (6%)
  starting transfers between devices  16.2 us (4%)
  other arithmetic  7.02 us (2%)
    ppermute x19, waiting for transfers between devices, swap(): return lax.ppermute(x, 'dap', [(i, i ^ bit) for i in range(8)])  124 us
    pallas_call x8, Pallas kernels, triangle(): pl.pallas_call(functools.partial(triangle_kernel, sizes, len(b_pieces), g...  115 us
    pallas_call x6, Pallas kernels, project(): pl.pallas_call(functools.partial(project_kernel, sides, group, counts), g...  101 us
    ppermute x19, starting transfers between devices, swap(): return lax.ppermute(x, 'dap', [(i, i ^ bit) for i in range(8)])  16.2 us
    broadcast_in_dim x11, local copies, waits for them, and re-layouts, device_fn(): jnp.broadcast_to(v.astype(f32)[:, None], (v.shape[0], 128))  8.04 us
  transfers between devices with their start and end apart: 19, of which 8 were waited for; matrix products, arithmetic and copies ran while one was open for 5% of the time, Pallas kernels for 41%

profile of v1, /device:TPU:0, one launch (start us, length us, event | category | flops | bytes accessed | tf_op | source)
XLA Modules:
  0.0 388.0 jit_solution(11160988487639531307)
XLA Ops:
  0.0 0.6 add_convert_fusion.refs_6_.refs_13_.refs_11_.refs_19_.refs_15_
  0.6 0.7 fusion.refs_10_.refs_4_.refs_6_
  1.3 1.0 fusion.5
  2.4 0.7 multiply_bitcast_fusion.1.refs_7_.refs_12_
  3.1 0.8 convert_multiply_fusion
  3.9 0.9 convert_element_type.203
  4.7 0.7 broadcast_in_dim.33.refs_4_
  5.4 1.3 slice_convert_fusion.1
  6.8 0.7 broadcast_in_dim.35.refs_8_.refs_13_
  7.5 0.7 broadcast_in_dim.36.refs_9_.refs_14_
  8.2 0.8 broadcast_in_dim.34.refs_5_.refs_10_
  9.0 17.2 %project.6 = (bf16[128,48,384]{2,1,0:T(8,128)(2,1)}, bf16[128,48,384]{2,1,0:T(8,128)(2,1)}) custom-call(bf16[48,4,96,128]{3,2,1,0:T(8,128)(2,1)} %bitcast.78, bf16[48,4,96,128]{3,2,1,0:T(8,128)(2,1)} %bitcast.79, bf16[48,4,96,128]{3,2,1,0:T(8,128)(2,1)} %bitcast.80, bf16[48,4,96,128]{3,2,1,0:T(8,128)(2,1)} %bitcast.81, ...), custom_call_target="tpu_custom_call" | custom-call | flops 2415919104 | bytes 14155776 | tf_op jit(solution)/shard_map/project/pallas_call | solution.py:90
  26.2 0.9 collective-permute-start
  27.1 3.9 slice.123
  30.9 2.5 collective-permute-start.1
  33.5 1.5 collective-permute-start.3
  36.2 0.7 multiply_bitcast_fusion.2
  37.4 66.6 %collective-permute-done.2 = s32[48,384]{1,0:T(8,128)S(1)} collective-permute-done((s32[48,384]{1,0:T(8,128)S(1)}, s32[48,384]{1,0:T(8,128)S(1)}, u32[]{:S(2)}, u32[]{:S(2)}) %collective-permute-start.2) | collective-permute-done | bytes 73760 | tf_op jit(solution)/shard_map/ppermute | solution.py:198
  104.0 0.7 copy.20.refs_4_
  104.7 0.8 collective-permute-done.4
  105.5 0.7 copy.21.refs_9_
  106.1 0.7 broadcast_in_dim.37.refs_9_.refs_15_.refs_11_
  106.8 0.7 broadcast_in_dim.38.refs_10_.refs_16_.refs_12_
  107.5 12.8 %triangle.8.refs_15_.refs_0_.refs_3_ = bf16[48,1,96,128]{3,2,1,0:T(8,128)(2,1)} custom-call(s32[1]{0:T(128)} %bitcast.where_ref, bf16[128,48,384]{2,1,0:T(8,128)(2,1)} %get-tuple-element.21.refs_0_.refs_14_, bf16[128,48,384]{2,1,0:T(8,128)(2,1)} %get-tuple-element.22.refs_1_.refs_4_, bf16[128,48,384]{2,1,0:T(8,128)(2,1)} %collective-permute-done.refs_2_.refs_5_, ...), custom_call_target="tpu_custom_call" | custom-call | flops 1061683200 | bytes 14155776 | tf_op jit(solution)/shard_map/triangle/pallas_call | solution.py:177
  120.3 22.7 %project.7 = (bf16[128,64,384]{2,1,0:T(8,128)(2,1)}, bf16[128,64,384]{2,1,0:T(8,128)(2,1)}) custom-call(bf16[32,4,96,128]{3,2,1,0:T(8,128)(2,1)} %collective-permute-done.1.refs_0_.refs_1_.refs_2_.refs_3_.refs_8_.refs_6_, bf16[32,4,96,128]{3,2,1,0:T(8,128)(2,1)} %collective-permute-done.1.refs_0_.refs_1_.refs_2_.refs_3_.refs_8_.refs_6_, ...), custom_call_target="tpu_custom_call" | custom-call | flops 3221225472 | bytes 18874368 | tf_op jit(solution)/shard_map/project/pallas_call | solution.py:90
  143.1 1.5 slice.129
  144.6 1.0 collective-permute-start.5
  145.6 1.5 collective-permute-start.6
  147.1 0.6 slice.132.refs_4_
  147.7 0.6 slice.134.refs_9_
  148.4 33.0 %collective-permute-done.5.refs_0_.refs_1_.refs_2_.refs_3_.refs_9_.refs_7_ = bf16[16,4,96,128]{3,2,1,0:T(8,128)(2,1)S(1)} collective-permute-done((bf16[16,4,96,128]{3,2,1,0:T(8,128)(2,1)S(1)}, bf16[16,4,96,128]{3,2,1,0:T(8,128)(2,1)S(1)}, u32[]{:S(2)}, u32[]{:S(2)}) %collective-permute-start.5) | collective-permute-done | bytes 1572896 | tf_op jit(solution)/shard_map/ppermute | solution.py:198
  181.4 0.8 collective-permute-done.6.refs_5_.refs_6_.refs_7_.refs_8_.refs_9_
  182.6 13.1 %project.8 = (bf16[128,32,384]{2,1,0:T(8,128)(2,1)}, bf16[128,32,384]{2,1,0:T(8,128)(2,1)}) custom-call(bf16[16,4,96,128]{3,2,1,0:T(8,128)(2,1)} %copy-done, bf16[16,4,96,128]{3,2,1,0:T(8,128)(2,1)} %copy-done, bf16[16,4,96,128]{3,2,1,0:T(8,128)(2,1)} %copy-done, bf16[16,4,96,128]{3,2,1,0:T(8,128)(2,1)} %copy-done, f32[16,1,384]{2,1,0:T(1,128)} %slice.132.refs_4_, ...), custom_call_target="tpu_custom_call" | custom-call | flops 1610612736 | bytes 9437184 | tf_op jit(solution)/shard_map/project/pallas_call | solution.py:90
  195.7 6.0 %collective-permute-done.8.refs_6_.refs_4_ = bf16[128,32,384]{2,1,0:T(8,128)(2,1)} collective-permute-done((bf16[128,32,384]{2,1,0:T(8,128)(2,1)}, bf16[128,32,384]{2,1,0:T(8,128)(2,1)}, u32[]{:S(2)}, u32[]{:S(2)}) %collective-permute-start.8) | collective-permute-done | bytes 3145760 | tf_op jit(solution)/shard_map/ppermute | solution.py:198
  201.7 18.3 %triangle.9 = (bf16[48,1,96,128]{3,2,1,0:T(8,128)(2,1)}, bf16[48,1,96,128]{3,2,1,0:T(8,128)(2,1)}) custom-call(s32[1]{0:T(128)} %bitcast.where_ref, bf16[128,48,384]{2,1,0:T(8,128)(2,1)} %get-tuple-element.21.refs_0_.refs_14_, bf16[128,64,384]{2,1,0:T(8,128)(2,1)} %get-tuple-element.24.refs_15_.refs_1_.refs_0_.refs_2_, ...), custom_call_target="tpu_custom_call" | custom-call | flops 2123366400 | bytes 18874368 | tf_op jit(solution)/shard_map/triangle/pallas_call | solution.py:177
  220.0 1.0 collective-permute-start.9
  221.2 1.1 collective-permute-start.10
  222.2 1.6 collective-permute-start.14
  223.8 0.9 collective-permute-start.11
  224.7 12.8 %triangle.10.refs_20_.refs_1_.refs_3_ = bf16[48,1,96,128]{3,2,1,0:T(8,128)(2,1)} custom-call(s32[1]{0:T(128)} %bitcast.where_ref, bf16[128,48,384]{2,1,0:T(8,128)(2,1)} %get-tuple-element.21.refs_0_.refs_14_, bf16[128,64,384]{2,1,0:T(8,128)(2,1)} %get-tuple-element.23.refs_3_.refs_1_, bf16[128,32,384]{2,1,0:T(8,128)(2,1)} %get-tuple-element.25.refs_4_.refs_2_, ...), custom_call_target="tpu_custom_call" | custom-call | flops 1061683200 | bytes 14155776 | tf_op jit(solution)/shard_map/triangle/pallas_call | solution.py:177
  238.0 11.2 %collective-permute-done.9.refs_3_ = bf16[48,1,96,128]{3,2,1,0:T(8,128)(2,1)} collective-permute-done((bf16[48,1,96,128]{3,2,1,0:T(8,128)(2,1)}, bf16[48,1,96,128]{3,2,1,0:T(8,128)(2,1)}, u32[]{:S(2)}, u32[]{:S(2)}) %collective-permute-start.9) | collective-permute-done | bytes 1179680 | tf_op jit(solution)/shard_map/ppermute | solution.py:198
  249.2 1.6 collective-permute-start.13
  250.9 0.6 slice.159.refs_7_
  253.7 0.8 reshape.149.refs_4_
  254.6 0.8 reshape.150.refs_4_
  255.4 0.8 reshape.151.refs_4_
  256.2 18.3 %triangle.11 = (bf16[48,1,96,128]{3,2,1,0:T(8,128)(2,1)}, bf16[48,1,96,128]{3,2,1,0:T(8,128)(2,1)}) custom-call(s32[1]{0:T(128)} %bitcast.where_ref, bf16[128,64,384]{2,1,0:T(8,128)(2,1)} %get-tuple-element.24.refs_15_.refs_1_.refs_0_.refs_2_, bf16[128,32,384]{2,1,0:T(8,128)(2,1)} %get-tuple-element.26.refs_2_.refs_20_.refs_1_.refs_3_, ...), custom_call_target="tpu_custom_call" | custom-call | flops 2123366400 | bytes 18874368 | tf_op jit(solution)/shard_map/triangle/pallas_call | solution.py:177
  274.6 0.7 broadcast_in_dim.40.refs_8_
  275.3 0.7 broadcast_in_dim.41.refs_9_
  276.0 0.8 broadcast_in_dim.39.refs_5_
  276.8 17.4 %project.9 = (bf16[128,48,384]{2,1,0:T(8,128)(2,1)}, bf16[128,48,384]{2,1,0:T(8,128)(2,1)}) custom-call(bf16[48,1,96,128]{3,2,1,0:T(8,128)(2,1)} %triangle.8.refs_15_.refs_0_.refs_3_, bf16[48,1,96,128]{3,2,1,0:T(8,128)(2,1)} %triangle.10.refs_20_.refs_1_.refs_3_, bf16[48,1,96,128]{3,2,1,0:T(8,128)(2,1)} %get-tuple-element.27.refs_16_.refs_2_.refs_3_, ...), custom_call_target="tpu_custom_call" | custom-call | flops 2415919104 | bytes 14155776 | tf_op jit(solution)/shard_map/project/pallas_call | solution.py:90
  294.3 4.6 %collective-permute-done.11.refs_3_ = bf16[48,1,96,128]{3,2,1,0:T(8,128)(2,1)} collective-permute-done((bf16[48,1,96,128]{3,2,1,0:T(8,128)(2,1)}, bf16[48,1,96,128]{3,2,1,0:T(8,128)(2,1)}, u32[]{:S(2)}, u32[]{:S(2)}) %collective-permute-start.11) | collective-permute-done | bytes 1179680 | tf_op jit(solution)/shard_map/ppermute | solution.py:198
  298.9 17.4 %project.10 = (bf16[128,48,384]{2,1,0:T(8,128)(2,1)}, bf16[128,48,384]{2,1,0:T(8,128)(2,1)}) custom-call(bf16[48,1,96,128]{3,2,1,0:T(8,128)(2,1)} %get-tuple-element.29.refs_10_.refs_0_, bf16[48,1,96,128]{3,2,1,0:T(8,128)(2,1)} %collective-permute-done.10.refs_1_, bf16[48,1,96,128]{3,2,1,0:T(8,128)(2,1)} %get-tuple-element.28.refs_2_.refs_3_, ...), custom_call_target="tpu_custom_call" | custom-call | flops 2415919104 | bytes 14155776 | tf_op jit(solution)/shard_map/project/pallas_call | solution.py:90
  316.3 0.8 broadcast_in_dim.44.refs_5_
  317.1 13.1 %project.11.refs_14_.refs_1_ = bf16[128,48,384]{2,1,0:T(8,128)(2,1)} custom-call(bf16[48,1,96,128]{3,2,1,0:T(8,128)(2,1)} %get-tuple-element.33.refs_0_, bf16[48,1,96,128]{3,2,1,0:T(8,128)(2,1)} %collective-permute-done.13.refs_1_, bf16[48,1,96,128]{3,2,1,0:T(8,128)(2,1)} %collective-permute-done.14.refs_2_, ...), custom_call_target="tpu_custom_call" | custom-call | flops 1207959552 | bytes 9437184 | tf_op jit(solution)/shard_map/project/pallas_call | solution.py:90
  330.7 0.7 broadcast_in_dim.42.refs_9_
  331.4 0.7 broadcast_in_dim.43.refs_10_
  332.1 13.1 %triangle.12.refs_14_ = bf16[48,4,96,128]{3,2,1,0:T(8,128)(2,1)} custom-call(s32[1]{0:T(128)} %bitcast.where_ref, bf16[128,48,384]{2,1,0:T(8,128)(2,1)} %get-tuple-element.30.refs_10_.refs_0_, bf16[128,48,384]{2,1,0:T(8,128)(2,1)} %get-tuple-element.35.refs_1_, bf16[128,48,384]{2,1,0:T(8,128)(2,1)} %collective-permute-done.17.refs_2_, ...), custom_call_target="tpu_custom_call" | custom-call | flops 1061683200 | bytes 14155776 | tf_op jit(solution)/shard_map/triangle/pallas_call | solution.py:177
  345.2 13.4 %triangle.15 = bf16[48,1,96,128]{3,2,1,0:T(8,128)(2,1)} custom-call(s32[1]{0:T(128)} %bitcast.where_ref, bf16[128,48,384]{2,1,0:T(8,128)(2,1)} %get-tuple-element.34.refs_10_.refs_0_, bf16[128,48,384]{2,1,0:T(8,128)(2,1)} %project.11.refs_14_.refs_1_, bf16[128,48,384]{2,1,0:T(8,128)(2,1)} %collective-permute-done.16.refs_2_, ...), custom_call_target="tpu_custom_call" | custom-call | flops 1061683200 | bytes 14155776 | tf_op jit(solution)/shard_map/triangle/pallas_call | solution.py:177
  358.7 1.0 collective-permute-start.18
  359.7 13.2 %triangle.13.refs_14_ = bf16[48,4,96,128]{3,2,1,0:T(8,128)(2,1)} custom-call(s32[1]{0:T(128)} %bitcast.where_ref, bf16[128,48,384]{2,1,0:T(8,128)(2,1)} %get-tuple-element.30.refs_10_.refs_0_, bf16[128,48,384]{2,1,0:T(8,128)(2,1)} %project.11.refs_14_.refs_1_, ...), custom_call_target="tpu_custom_call", output_to_operand_aliasing={{}: (15, {})} | custom-call | flops 1061683200 | bytes 14155776 | tf_op jit(solution)/shard_map/triangle/pallas_call | solution.py:177
  372.8 13.2 %triangle.14 = bf16[48,4,96,128]{3,2,1,0:T(8,128)(2,1)} custom-call(s32[1]{0:T(128)} %bitcast.where_ref, bf16[128,48,384]{2,1,0:T(8,128)(2,1)} %get-tuple-element.30.refs_10_.refs_0_, bf16[128,48,384]{2,1,0:T(8,128)(2,1)} %get-tuple-element.32.refs_1_, bf16[128,48,384]{2,1,0:T(8,128)(2,1)} %collective-permute-done.12.refs_2_, ...), custom_call_target="tpu_custom_call", output_to_operand_aliasing={{}: (15, {})} | custom-call | flops 1061683200 | bytes 14155776 | tf_op jit(solution)/shard_map/triangle/pallas_call | solution.py:177
  386.0 0.8 collective-permute-done.18
  386.8 1.2 constant_dynamic-update-slice_fusion
  (69 shorter events, 5.9 us)
Async XLA Ops:
  26.1 8.9 %copy-start.3 = (s32[48,384]{1,0:T(8,128)S(1)}, s32[48,384]{1,0:T(8,128)}, u32[]{:S(2)}) copy-start(s32[48,384]{1,0:T(8,128)} %param.15) | copy-start | bytes 221188
  26.1 9.4 %copy-start.6 = (bf16[2,128]{1,0:T(2,128)(2,1)S(1)}, bf16[2,128]{1,0:T(2,128)(2,1)}, u32[]{:S(2)}) copy-start(bf16[2,128]{1,0:T(2,128)(2,1)} %param.22) | copy-start | bytes 1540
  26.2 9.4 %copy-start.7 = (bf16[2,128]{1,0:T(2,128)(2,1)S(1)}, bf16[2,128]{1,0:T(2,128)(2,1)}, u32[]{:S(2)}) copy-start(bf16[2,128]{1,0:T(2,128)(2,1)} %param.23) | copy-start | bytes 1540
  26.2 9.4 %copy-start.8 = (bf16[2,128]{1,0:T(2,128)(2,1)S(1)}, bf16[2,128]{1,0:T(2,128)(2,1)}, u32[]{:S(2)}) copy-start(bf16[2,128]{1,0:T(2,128)(2,1)} %param.21) | copy-start | bytes 1540
  26.2 10.0 %copy-start.4 = (bf16[2,128,128]{2,1,0:T(8,128)(2,1)S(1)}, bf16[2,128,128]{2,1,0:T(8,128)(2,1)}, u32[]{:S(2)}) copy-start(bf16[2,128,128]{2,1,0:T(8,128)(2,1)} %param.20) | copy-start | bytes 196612
  26.2 10.0 %copy-start.5 = (bf16[2,128,128]{2,1,0:T(8,128)(2,1)S(1)}, bf16[2,128,128]{2,1,0:T(8,128)(2,1)}, u32[]{:S(2)}) copy-start(bf16[2,128,128]{2,1,0:T(8,128)(2,1)} %param.24) | copy-start | bytes 196612
  26.2 10.6 %copy-start.9 = (bf16[2,128]{1,0:T(2,128)(2,1)S(1)}, bf16[2,128]{1,0:T(2,128)(2,1)}, u32[]{:S(2)}) copy-start(bf16[2,128]{1,0:T(2,128)(2,1)} %param.25) | copy-start | bytes 1540
  26.2 79.9 %collective-permute-start = (bf16[128,48,384]{2,1,0:T(8,128)(2,1)}, bf16[128,48,384]{2,1,0:T(8,128)(2,1)}, u32[]{:S(2)}, u32[]{:S(2)}) collective-permute-start(bf16[128,48,384]{2,1,0:T(8,128)(2,1)} %get-tuple-element.22.refs_1_.refs_4_), channel_id=1, source_target_pairs={{0,1},{1,0},{2,3},{3,2},{4,5},{5,4},{6,7},{7,6}} | collective-permute-start | bytes 14155784 | tf_op jit(solution)/shard_map/ppermute | solution.py:198
  30.9 89.3 %collective-permute-start.1 = (bf16[32,4,96,128]{3,2,1,0:T(8,128)(2,1)}, bf16[32,4,96,128]{3,2,1,0:T(8,128)(2,1)}, u32[]{:S(2)}, u32[]{:S(2)}) collective-permute-start(bf16[32,4,96,128]{3,2,1,0:T(8,128)(2,1)} %bitcast.11), channel_id=1, source_target_pairs={{0,2},{1,3},{2,0},{3,1},{4,6},{5,7},{6,4},{7,5}} | collective-permute-start | bytes 9437192 | tf_op jit(solution)/shard_map/ppermute | solution.py:198
  33.5 86.8 %collective-permute-start.3 = (bf16[32,4,96,128]{3,2,1,0:T(8,128)(2,1)}, bf16[32,4,96,128]{3,2,1,0:T(8,128)(2,1)}, u32[]{:S(2)}, u32[]{:S(2)}) collective-permute-start(bf16[32,4,96,128]{3,2,1,0:T(8,128)(2,1)} %bitcast.11), channel_id=1, source_target_pairs={{0,4},{1,5},{2,6},{3,7},{4,0},{5,1},{6,2},{7,3}} | collective-permute-start | bytes 9437192 | tf_op jit(solution)/shard_map/ppermute | solution.py:198
  35.0 69.0 %collective-permute-start.2 = (s32[48,384]{1,0:T(8,128)S(1)}, s32[48,384]{1,0:T(8,128)S(1)}, u32[]{:S(2)}, u32[]{:S(2)}) collective-permute-start(s32[48,384]{1,0:T(8,128)S(1)} %copy-done.3), channel_id=1, source_target_pairs={{0,2},{1,3},{2,0},{3,1},{4,6},{5,7},{6,4},{7,5}} | collective-permute-start | bytes 221192 | tf_op jit(solution)/shard_map/ppermute | solution.py:198
  35.5 69.9 %collective-permute-start.4 = (s32[48,384]{1,0:T(8,128)S(1)}, s32[48,384]{1,0:T(8,128)S(1)}, u32[]{:S(2)}, u32[]{:S(2)}) collective-permute-start(s32[48,384]{1,0:T(8,128)S(1)} %copy-done.3), channel_id=1, source_target_pairs={{0,4},{1,5},{2,6},{3,7},{4,0},{5,1},{6,2},{7,3}} | collective-permute-start | bytes 221192 | tf_op jit(solution)/shard_map/ppermute | solution.py:198
  143.0 58.7 %collective-permute-start.7 = (bf16[128,64,384]{2,1,0:T(8,128)(2,1)}, bf16[128,64,384]{2,1,0:T(8,128)(2,1)}, u32[]{:S(2)}, u32[]{:S(2)}) collective-permute-start(bf16[128,64,384]{2,1,0:T(8,128)(2,1)} %get-tuple-element.23.refs_3_.refs_1_), channel_id=1, source_target_pairs={{0,1},{1,0},{2,3},{3,2},{4,5},{5,4},{6,7},{7,6}} | collective-permute-start | bytes 18874376 | tf_op jit(solution)/shard_map/ppermute | solution.py:198
  144.6 36.8 %collective-permute-start.5 = (bf16[16,4,96,128]{3,2,1,0:T(8,128)(2,1)S(1)}, bf16[16,4,96,128]{3,2,1,0:T(8,128)(2,1)S(1)}, u32[]{:S(2)}, u32[]{:S(2)}) collective-permute-start(bf16[16,4,96,128]{3,2,1,0:T(8,128)(2,1)S(1)} %bitcast.85), channel_id=1, source_target_pairs={{0,2},{1,3},{2,0},{3,1},{4,6},{5,7},{6,4},{7,5}} | collective-permute-start | bytes 4718600 | tf_op jit(solution)/shard_map/ppermute | solution.py:198
  145.6 36.6 %collective-permute-start.6 = (bf16[16,4,96,128]{3,2,1,0:T(8,128)(2,1)S(1)}, bf16[16,4,96,128]{3,2,1,0:T(8,128)(2,1)}, u32[]{:S(2)}, u32[]{:S(2)}) collective-permute-start(bf16[16,4,96,128]{3,2,1,0:T(8,128)(2,1)S(1)} %bitcast.86), channel_id=1, source_target_pairs={{0,4},{1,5},{2,6},{3,7},{4,0},{5,1},{6,2},{7,3}} | collective-permute-start | bytes 4718600 | tf_op jit(solution)/shard_map/ppermute | solution.py:198
  181.4 1.2 copy-start
  195.7 6.0 %collective-permute-start.8 = (bf16[128,32,384]{2,1,0:T(8,128)(2,1)}, bf16[128,32,384]{2,1,0:T(8,128)(2,1)}, u32[]{:S(2)}, u32[]{:S(2)}) collective-permute-start(bf16[128,32,384]{2,1,0:T(8,128)(2,1)} %get-tuple-element.25.refs_4_.refs_2_), channel_id=1, source_target_pairs={{0,1},{1,0},{2,3},{3,2},{4,5},{5,4},{6,7},{7,6}} | collective-permute-start | bytes 9437192 | tf_op jit(solution)/shard_map/ppermute | solution.py:198
  201.7 19.4 %copy-start.1 = (bf16[48,1,96,128]{3,2,1,0:T(8,128)(2,1)S(1)}, bf16[48,1,96,128]{3,2,1,0:T(8,128)(2,1)}, u32[]{:S(2)}) copy-start(bf16[48,1,96,128]{3,2,1,0:T(8,128)(2,1)} %triangle.8.refs_15_.refs_0_.refs_3_) | copy-start | bytes 3538948
  220.0 29.2 %collective-permute-start.9 = (bf16[48,1,96,128]{3,2,1,0:T(8,128)(2,1)}, bf16[48,1,96,128]{3,2,1,0:T(8,128)(2,1)}, u32[]{:S(2)}, u32[]{:S(2)}) collective-permute-start(bf16[48,1,96,128]{3,2,1,0:T(8,128)(2,1)} %get-tuple-element.28.refs_2_.refs_3_), channel_id=1, source_target_pairs={{0,2},{1,3},{2,0},{3,1},{4,6},{5,7},{6,4},{7,5}} | collective-permute-start | bytes 3538952 | tf_op jit(solution)/shard_map/ppermute | solution.py:198
  221.2 73.1 %collective-permute-start.10 = (bf16[48,1,96,128]{3,2,1,0:T(8,128)(2,1)S(1)}, bf16[48,1,96,128]{3,2,1,0:T(8,128)(2,1)}, u32[]{:S(2)}, u32[]{:S(2)}) collective-permute-start(bf16[48,1,96,128]{3,2,1,0:T(8,128)(2,1)S(1)} %copy-done.1), channel_id=1, source_target_pairs={{0,2},{1,3},{2,0},{3,1},{4,6},{5,7},{6,4},{7,5}} | collective-permute-start | bytes 3538952 | tf_op jit(solution)/shard_map/ppermute | solution.py:198
  222.2 94.1 %collective-permute-start.14 = (bf16[48,1,96,128]{3,2,1,0:T(8,128)(2,1)S(1)}, bf16[48,1,96,128]{3,2,1,0:T(8,128)(2,1)}, u32[]{:S(2)}, u32[]{:S(2)}) collective-permute-start(bf16[48,1,96,128]{3,2,1,0:T(8,128)(2,1)S(1)} %copy-done.1), channel_id=1, source_target_pairs={{0,4},{1,5},{2,6},{3,7},{4,0},{5,1},{6,2},{7,3}} | collective-permute-start | bytes 3538952 | tf_op jit(solution)/shard_map/ppermute | solution.py:198
  223.8 75.1 %collective-permute-start.11 = (bf16[48,1,96,128]{3,2,1,0:T(8,128)(2,1)}, bf16[48,1,96,128]{3,2,1,0:T(8,128)(2,1)}, u32[]{:S(2)}, u32[]{:S(2)}) collective-permute-start(bf16[48,1,96,128]{3,2,1,0:T(8,128)(2,1)} %get-tuple-element.27.refs_16_.refs_2_.refs_3_), channel_id=1, source_target_pairs={{0,2},{1,3},{2,0},{3,1},{4,6},{5,7},{6,4},{7,5}} | collective-permute-start | bytes 3538952 | tf_op jit(solution)/shard_map/ppermute | solution.py:198
  237.5 78.8 %collective-permute-start.15 = (bf16[48,1,96,128]{3,2,1,0:T(8,128)(2,1)}, bf16[48,1,96,128]{3,2,1,0:T(8,128)(2,1)}, u32[]{:S(2)}, u32[]{:S(2)}) collective-permute-start(bf16[48,1,96,128]{3,2,1,0:T(8,128)(2,1)} %triangle.10.refs_20_.refs_1_.refs_3_), channel_id=1, source_target_pairs={{0,4},{1,5},{2,6},{3,7},{4,0},{5,1},{6,2},{7,3}} | collective-permute-start | bytes 3538952 | tf_op jit(solution)/shard_map/ppermute | solution.py:198
  249.2 67.1 %collective-permute-start.13 = (bf16[48,1,96,128]{3,2,1,0:T(8,128)(2,1)}, bf16[48,1,96,128]{3,2,1,0:T(8,128)(2,1)}, u32[]{:S(2)}, u32[]{:S(2)}) collective-permute-start(bf16[48,1,96,128]{3,2,1,0:T(8,128)(2,1)} %collective-permute-done.9.refs_3_), channel_id=1, source_target_pairs={{0,4},{1,5},{2,6},{3,7},{4,0},{5,1},{6,2},{7,3}} | collective-permute-start | bytes 3538952 | tf_op jit(solution)/shard_map/ppermute | solution.py:198
  250.8 23.8 %copy-start.2 = (bf16[512,128]{1,0:T(8,128)(2,1)}, bf16[512,128]{1,0:T(8,128)(2,1)S(1)}, u32[]{:S(2)}) copy-start(bf16[512,128]{1,0:T(8,128)(2,1)S(1)} %multiply_bitcast_fusion.refs_7_) | copy-start | bytes 393220
  294.2 36.4 %collective-permute-start.17 = (bf16[128,48,384]{2,1,0:T(8,128)(2,1)}, bf16[128,48,384]{2,1,0:T(8,128)(2,1)}, u32[]{:S(2)}, u32[]{:S(2)}) collective-permute-start(bf16[128,48,384]{2,1,0:T(8,128)(2,1)} %get-tuple-element.35.refs_1_), channel_id=1, source_target_pairs={{0,1},{1,0},{2,3},{3,2},{4,5},{5,4},{6,7},{7,6}} | collective-permute-start | bytes 14155784 | tf_op jit(solution)/shard_map/ppermute | solution.py:198
  330.2 15.1 %collective-permute-start.16 = (bf16[128,48,384]{2,1,0:T(8,128)(2,1)}, bf16[128,48,384]{2,1,0:T(8,128)(2,1)}, u32[]{:S(2)}, u32[]{:S(2)}) collective-permute-start(bf16[128,48,384]{2,1,0:T(8,128)(2,1)} %project.11.refs_14_.refs_1_), channel_id=1, source_target_pairs={{0,1},{1,0},{2,3},{3,2},{4,5},{5,4},{6,7},{7,6}} | collective-permute-start | bytes 14155784 | tf_op jit(solution)/shard_map/ppermute | solution.py:198
  330.2 42.6 %collective-permute-start.12 = (bf16[128,48,384]{2,1,0:T(8,128)(2,1)}, bf16[128,48,384]{2,1,0:T(8,128)(2,1)}, u32[]{:S(2)}, u32[]{:S(2)}) collective-permute-start(bf16[128,48,384]{2,1,0:T(8,128)(2,1)} %get-tuple-element.32.refs_1_), channel_id=1, source_target_pairs={{0,1},{1,0},{2,3},{3,2},{4,5},{5,4},{6,7},{7,6}} | collective-permute-start | bytes 14155784 | tf_op jit(solution)/shard_map/ppermute | solution.py:198
  358.7 28.1 %collective-permute-start.18 = (bf16[48,1,96,128]{3,2,1,0:T(8,128)(2,1)}, bf16[48,1,96,128]{3,2,1,0:T(8,128)(2,1)S(1)}, u32[]{:S(2)}, u32[]{:S(2)}) collective-permute-start(bf16[48,1,96,128]{3,2,1,0:T(8,128)(2,1)} %triangle.15), channel_id=1, source_target_pairs={{0,2},{1,3},{2,0},{3,1},{4,6},{5,7},{6,4},{7,5}} | collective-permute-start | bytes 3538952 | tf_op jit(solution)/shard_map/ppermute | solution.py:198

commit v2 on v0

v2 whole, which is shorter than its diff:
```python
import functools
import jax
import jax.numpy as jnp
from jax import lax
from jax.experimental import pallas as pl
from jax.experimental.pallas import tpu as pltpu
from jax.sharding import PartitionSpec as P

LN_EPS = 1e-5
ROWS = 16
CHUNK = 16
GROUP = 16
PITCH = 136
ROW_PITCH = 20
NT = (((1,), (1,)), ((), ()))


def norm_sublanes(x, scale, bias):
    mean = jnp.mean(x, axis=0, keepdims=True)
    xc = x - mean
    var = jnp.mean(xc * xc, axis=0, keepdims=True)
    return xc * lax.rsqrt(var + LN_EPS) * scale + bias


def project_kernel(layer, sides, team, sources, *refs):
    z_refs, refs = [refs[4 * n:4 * n + 4] for n in range(len(sources))], refs[4 * len(sources):]
    mask_refs, refs = refs[:len(sources)], refs[len(sources):]
    vectors, w_t, centre_in = refs[:3]
    outs = refs[4:4 + sides]
    proj, znt, stage, keep, mask, bias_ref, ln_s, ln_b, w_ref, centre, zbuf, obuf, load_sem, param_sem, out_sem = refs[4 + sides:]
    rows = sum(n for n, _, _ in sources)
    side0 = 512 - 256 * sides
    moves = [(centre_in, centre), (vectors.at[layer, 512:640], ln_s), (vectors.at[layer, 640:768], ln_b),
             (w_t.at[layer, side0:512], w_ref), (vectors.at[layer, side0:512], bias_ref)]
    at = 0
    for n, (count, _, mask_row) in enumerate(sources):
        moves.append((mask_refs[n].at[mask_row:mask_row + count], mask.at[at:at + count]))
        at += count
    params = [pltpu.make_async_copy(src, dst, param_sem.at[n]) for n, (src, dst) in enumerate(moves)]
    groups = rows // team

    def loads(n, first, g):
        copies = []
        for t in range(4):
            blk, row = sources[n][1][t]
            src = z_refs[n][t].at[pl.ds(pl.multiple_of(row + g * team, team), team), blk]
            dst = zbuf.at[pl.ds(pl.multiple_of(first + g * team, team), team), t]
            copies.append(pltpu.make_async_copy(src, dst, load_sem.at[first // team + g, t]))
        return copies

    for copy in params:
        copy.start()
    first = 0
    for n, (count, _, mask_row) in enumerate(sources):
        def start(g, carry, n=n, first=first):
            for copy in loads(n, first, g):
                copy.start()
            return carry

        lax.fori_loop(0, count // team, start, 0)
        first += count

    def arrive(g):
        for t in range(4):
            dst = zbuf.at[pl.ds(pl.multiple_of(g * team, team), team), t]
            pltpu.make_async_copy(z_refs[0][t].at[0:team, sources[0][1][t][0]], dst, load_sem.at[g, t]).wait()

    def normalise(g):
        z = zbuf[pl.ds(pl.multiple_of(g * team, team), team)].reshape(team * 384, 128)
        xc = lax.dot_general(centre[...], z, NT, preferred_element_type=jnp.float32)
        for lt in range(3 * team):
            ls = slice(lt * 128, lt * 128 + 128)
            x = xc[:, ls]
            var = jnp.mean(x * x, axis=0, keepdims=True)
            znt[:, ls] = (x * lax.rsqrt(var + LN_EPS) * ln_s[...] + ln_b[...]).astype(jnp.bfloat16)

    def stores(b, quarter):
        chans = pl.ds(pl.multiple_of(quarter * 32, 32), 32)
        at = pl.ds(pl.multiple_of(b * ROWS, ROWS), ROWS)
        return [pltpu.make_async_copy(obuf.at[b % 2, s, chans], outs[s].at[chans, at], out_sem.at[b % 2, s, quarter]) for s in range(sides)]

    arrive(0)
    for copy in params:
        copy.wait()
    keep[...] = mask[...].astype(jnp.float32).astype(jnp.bfloat16)
    normalise(0)

    def block(b, carry):
        def some(g, carry):
            after = b * (ROWS // team) + g + 1

            @pl.when(after < groups)
            def _():
                arrive(after)

            proj[...] = jnp.dot(w_ref[...], znt[...], preferred_element_type=jnp.float32)
            normalise(jnp.minimum(after, groups - 1))
            for h in range(team):
                i = g * team + h
                for lt in range(3):
                    ls = slice(h * 384 + lt * 128, h * 384 + lt * 128 + 128)
                    for s in range(sides):
                        value = proj[s * 256:s * 256 + 128, ls] + bias_ref[s * 256:s * 256 + 128]
                        gate = proj[s * 256 + 128:s * 256 + 256, ls] + bias_ref[s * 256 + 128:s * 256 + 256]
                        stage[s, lt, pl.ds(i, 128, stride=ROW_PITCH), :] = (jnp.tanh(gate) + 1.0) * value
            return carry

        lax.fori_loop(0, ROWS // team, some, 0)

        @pl.when(b >= 2)
        def _():
            for quarter in range(4):
                for copy in stores(b - 2, quarter):
                    copy.wait()

        m = keep[pl.ds(pl.multiple_of(b * ROWS, ROWS), ROWS)]

        def quarter_of(quarter, carry):
            def chan(c8, carry):
                c0 = quarter * 32 + c8 * 8
                for s in range(sides):
                    for lt in range(3):
                        view = stage.at[s, lt, pl.ds(pl.multiple_of(c0 * ROW_PITCH, 8), 8 * ROW_PITCH)]
                        for q in range(8):
                            obuf[b % 2, s, c0 + q, :, lt * 128:lt * 128 + 128] = view[q * ROW_PITCH:q * ROW_PITCH + ROWS].astype(jnp.bfloat16) * m[:, lt * 128:lt * 128 + 128]
                return carry

            lax.fori_loop(0, 4, chan, 0)
            for copy in stores(b, quarter):
                copy.start()
            return carry

        lax.fori_loop(0, 4, quarter_of, 0)
        return carry

    lax.fori_loop(0, rows // ROWS, block, 0)
    for b in range(max(rows // ROWS - 2, 0), rows // ROWS):
        for quarter in range(4):
            for copy in stores(b, quarter):
                copy.wait()


def project(layer, sources, vectors, w_t, centre, sides, dep, team=4):
    rows = sum(n for n, _, _, _ in sources)
    anywhere = pl.BlockSpec(memory_space=pl.ANY)
    in_specs = [anywhere] * (5 * len(sources) + 4)
    return pl.pallas_call(
        functools.partial(project_kernel, layer, sides, team, [(n, [tile[1:] for tile in tiles], at) for n, tiles, _, at in sources]),
        grid=(1,),
        out_shape=[jax.ShapeDtypeStruct((128, rows, 384), jnp.bfloat16)] * sides,
        in_specs=in_specs,
        out_specs=[anywhere] * sides,
        scratch_shapes=[pltpu.VMEM((256 * sides, team * 384), jnp.float32), pltpu.VMEM((128, team * 384), jnp.bfloat16), pltpu.VMEM((sides, 3, 128 * ROW_PITCH, 128), jnp.float32), pltpu.VMEM((rows, 384), jnp.bfloat16), pltpu.VMEM((rows, 384), jnp.int32),
                        pltpu.VMEM((256 * sides, 128), jnp.float32), pltpu.VMEM((128, 128), jnp.float32), pltpu.VMEM((128, 128), jnp.float32), pltpu.VMEM((256 * sides, 128), jnp.bfloat16), pltpu.VMEM((128, 128), jnp.bfloat16),
                        pltpu.VMEM((rows, 4, 96, 128), jnp.bfloat16), pltpu.VMEM((2, sides, 128, ROWS, 384), jnp.bfloat16),
                        pltpu.SemaphoreType.DMA((rows // team, 4)), pltpu.SemaphoreType.DMA((5 + len(sources),)), pltpu.SemaphoreType.DMA((2, sides, 4))],
        compiler_params=pltpu.CompilerParams(dimension_semantics=('arbitrary',), vmem_limit_bytes=62 * 2**20),
        cost_estimate=pl.CostEstimate(flops=rows * 384 * 128 * 512 * sides, bytes_accessed=rows * 384 * 256 * (1 + sides), transcendentals=0),
        name='project',
    )(*[tile[0] for _, tiles, _, _ in sources for tile in tiles], *[mask for _, _, mask, _ in sources], vectors, w_t, centre, dep)


def triangle_kernel(layer, jobs, n_a, n_b, n_z, n_out, n_held, where_ref, *refs):
    a_refs, refs = refs[:n_a], refs[n_a:]
    b_refs, refs = refs[:n_b], refs[n_b:]
    z_refs, refs = refs[:n_z], refs[n_z:]
    perm_in, centre_in, w_out_in, w_gate_in, vectors, rows_in = refs[:6]
    outs, refs = refs[6 + n_held:6 + n_held + n_out], refs[6 + n_held + n_out:]
    tri, abuf, bbuf, zbuf, obuf, perm_ref, centre, w_out, w_gate, ln_s, ln_b, rows_ref, load_sem, z_sem, param_sem, out_sem = refs
    b_out, b_gate, in_s, in_b = [rows_ref.at[n:n + 1] for n in range(4)]
    moves = [(perm_in, perm_ref), (centre_in, centre), (w_out_in.at[layer], w_out), (w_gate_in.at[layer], w_gate),
             (vectors.at[layer, 768:896], ln_s), (vectors.at[layer, 896:1024], ln_b), (rows_in.at[layer], rows_ref)]
    params = [pltpu.make_async_copy(src, dst, param_sem.at[n]) for n, (src, dst) in enumerate(moves)]
    column = lambda rel: 0 if rel is None else where_ref[0] ^ rel
    regions, z_at, zn, total = {}, [], [], 0
    for pieces, _, _ in jobs:
        z_at.append(total)
        zn.append(sum(len(p) for p, _, _ in jobs[:len(zn)]))
        total += sum(p[3] for p in pieces)

    a_at, loads_a, filled = [], [], 0
    for pieces, _, _ in jobs:
        key = tuple(p[1:4] for p in pieces)
        loads_a.append(key not in regions)
        if key not in regions:
            regions[key] = filled
            filled += sum(p[3] for p in pieces)
        a_at.append(regions[key])

    def loads(j, q):
        pieces, b_pieces, _ = jobs[j]
        chans = pl.ds(pl.multiple_of(q * CHUNK, CHUNK), CHUNK)
        copies, r0 = [], a_at[j]
        for n, (_, a, blk, count, _, _) in enumerate(pieces if loads_a[j] else ()):
            copies.append(pltpu.make_async_copy(a_refs[a].at[chans, blk * count:blk * count + count], abuf.at[chans, r0:r0 + count], load_sem.at[j, q, n]))
            r0 += count
        r0 = 0
        for n, (b, blk, count) in enumerate(b_pieces):
            copies.append(pltpu.make_async_copy(b_refs[b].at[chans, blk * count:blk * count + count], bbuf.at[j, chans, r0:r0 + count], load_sem.at[j, q, len(pieces) + n]))
            r0 += count
        return copies

    def z_loads(j):
        copies, r0 = [], z_at[j]
        for n, (_, _, _, count, rel, z0) in enumerate(jobs[j][0]):
            copies.append(pltpu.make_async_copy(z_refs[zn[j] + n].at[z0:z0 + count, column(rel)], zbuf.at[r0:r0 + count], z_sem.at[zn[j] + n]))
            r0 += count
        return copies

    for j in range(len(jobs)):
        def start_loads(q, carry, j=j):
            for copy in loads(j, q):
                copy.start()
            return carry

        lax.fori_loop(0, 128 // CHUNK, start_loads, 0)
        for copy in z_loads(j) + (params if j == 0 else []):
            copy.start()
    tri[:, 96:128] = jnp.zeros((tri.shape[0], 32), jnp.float32)

    def some_rows(i0, at):
        flipped = []
        for q in range(GROUP):
            o = tri[pl.ds(pl.multiple_of((i0 + q) * PITCH, 8), 128), :]
            on = norm_sublanes(o, ln_s[...], ln_b[...]).astype(jnp.bfloat16)
            flipped.append(lax.dot_general(perm_ref[...], on, NT, preferred_element_type=jnp.float32).astype(jnp.bfloat16))
        on = jnp.concatenate(flipped, axis=0)
        u = jnp.dot(on, w_out[...], preferred_element_type=jnp.float32) + b_out[...]
        u = u.astype(jnp.bfloat16).astype(jnp.float32)
        zb = zbuf[pl.ds(at, GROUP)].reshape(GROUP * 96, 128)
        xc = jnp.dot(zb, centre[...], preferred_element_type=jnp.float32)
        z = zb.astype(jnp.float32)
        var = jnp.mean(xc * xc, axis=-1, keepdims=True)
        zn = (xc * lax.rsqrt(var + LN_EPS) * in_s[...] + in_b[...]).astype(jnp.bfloat16)
        g = jnp.dot(zn, w_gate[...], preferred_element_type=jnp.float32) + b_gate[...]
        g = 0.5 * jnp.tanh(g) + 0.5
        obuf[pl.ds(at, GROUP)] = (z + g * u).astype(jnp.bfloat16).reshape(GROUP, 96, 128)

    written = []
    for j, (pieces, b_pieces, outputs) in enumerate(jobs):
        rows = sum(p[3] for p in pieces)

        def some_channels(q, carry, j=j, rows=rows):
            for copy in loads(j, q):
                copy.wait()
            for cc in range(CHUNK):
                c = q * CHUNK + cc
                o = lax.dot_general(abuf[c, a_at[j]:a_at[j] + rows], bbuf[j, c], NT, preferred_element_type=jnp.float32)
                tri[pl.ds(c, rows, stride=PITCH), 0:96] = o
            return carry

        lax.fori_loop(0, 128 // CHUNK, some_channels, 0)
        for copy in z_loads(j) + (params if j == 0 else []):
            copy.wait()

        spans, r0 = [], 0
        for s, _, _, count, _, _ in pieces:
            if spans and spans[-1][0] == s:
                spans[-1][2] += count
            else:
                spans.append([s, r0, count])
            r0 += count

        def store(s, r0, i, j=j, outputs=outputs):
            arr, first, rel = outputs[s]
            row, to = pl.multiple_of(z_at[j] + r0 + i * GROUP, GROUP), pl.multiple_of(first + i * GROUP, GROUP)
            return pltpu.make_async_copy(obuf.at[pl.ds(row, GROUP)], outs[arr].at[pl.ds(to, GROUP), column(rel)], out_sem.at[(z_at[j] + r0) // GROUP + i])

        for s, r0, count in spans:
            def body(i, carry, s=s, r0=r0, store=store, j=j):
                i0 = pl.multiple_of(r0 + i * GROUP, GROUP)
                some_rows(i0, z_at[j] + i0)
                store(s, r0, i).start()
                return carry

            lax.fori_loop(0, count // GROUP, body, 0)
            written += [(store, s, r0, i) for i in range(count // GROUP)]
    for store, s, r0, i in written:
        store(s, r0, i).wait()


def triangles(layer, where, jobs, arrays, params, dep):
    def place(arr, pool):
        for n, other in enumerate(pool):
            if other is arr:
                return n
        pool.append(arr)
        return len(pool) - 1

    a_pool, b_pool, z_pool, static, most_b, most_a = [], [], [], [], 0, 0
    for pieces, b_pieces, outputs in jobs:
        z_pool += [p[4] for p in pieces]
        static.append(([(p[0], place(p[1], a_pool), p[2], p[3], p[5], p[6]) for p in pieces],
                       [(place(b, b_pool), blk, n) for b, blk, n in b_pieces], outputs))
        most_a, most_b = max(most_a, len(pieces)), max(most_b, len(b_pieces))
    total = sum(p[3] for pieces, _, _ in static for p in pieces)
    rows = max(sum(p[3] for p in pieces) for pieces, _, _ in static)
    keys = {tuple(p[1:4] for p in pieces) for pieces, _, _ in static}
    held_rows = sum(n for key in keys for _, _, n in key)
    deps = dep if isinstance(dep, tuple) else (dep,)
    held = [prev for _, _, prev in arrays if prev is not None]
    first = 1 + len(a_pool) + len(b_pool) + len(z_pool) + len(params) + len(deps)
    aliases, seen = {}, 0
    for s, (_, _, prev) in enumerate(arrays):
        if prev is not None:
            aliases[first + seen] = s
            seen += 1
    anywhere = pl.BlockSpec(memory_space=pl.ANY)
    in_specs = [anywhere] * (len(a_pool) + len(b_pool) + len(z_pool) + len(params) + len(deps) + len(held))
    return pl.pallas_call(
        functools.partial(triangle_kernel, layer, static, len(a_pool), len(b_pool), len(z_pool), len(arrays), len(deps) + len(held)),
        out_shape=[jax.ShapeDtypeStruct((n, width, 96, 128), jnp.bfloat16) for n, width, _ in arrays],
        input_output_aliases=aliases,
        grid_spec=pltpu.PrefetchScalarGridSpec(
            num_scalar_prefetch=1, grid=(1,), in_specs=in_specs, out_specs=[anywhere] * len(arrays),
            scratch_shapes=[pltpu.VMEM((rows * PITCH, 128), jnp.float32), pltpu.VMEM((128, held_rows, 384), jnp.bfloat16), pltpu.VMEM((len(jobs), 128, 96, 384), jnp.bfloat16),
                            pltpu.VMEM((total, 96, 128), jnp.bfloat16), pltpu.VMEM((total, 96, 128), jnp.bfloat16),
                            pltpu.VMEM((96, 128), jnp.bfloat16), pltpu.VMEM((128, 128), jnp.bfloat16), pltpu.VMEM((128, 128), jnp.bfloat16), pltpu.VMEM((128, 128), jnp.bfloat16),
                            pltpu.VMEM((128, 128), jnp.float32), pltpu.VMEM((128, 128), jnp.float32), pltpu.VMEM((4, 128), jnp.float32),
                            pltpu.SemaphoreType.DMA((len(jobs), 128 // CHUNK, most_a + most_b)), pltpu.SemaphoreType.DMA((len(z_pool),)), pltpu.SemaphoreType.DMA((7,)), pltpu.SemaphoreType.DMA((total // GROUP,))]),
        compiler_params=pltpu.CompilerParams(dimension_semantics=('arbitrary',), vmem_limit_bytes=62 * 2**20),
        cost_estimate=pl.CostEstimate(flops=total * 96 * 128 * 1800, bytes_accessed=(total + 96) * 384 * 256, transcendentals=0),
        name='triangle',
    )(where, *a_pool, *b_pool, *z_pool, *params, *deps, *held)


def triangle(layer, where, sets, b_pieces, params, dep, into=None):
    into = into or [(sum(p[2] for p in pieces), 1, 0, None, None) for pieces in sets]
    job = ([(s,) + p for s, pieces in enumerate(sets) for p in pieces], b_pieces, [(s, at, rel) for s, (_, _, at, rel, _) in enumerate(into)])
    return triangles(layer, where, [job], [(n, width, prev) for n, width, _, _, prev in into], params, dep)


def solution(mesh):
    row_spec = P(('batch', 'dap'), None, None)
    mask_spec = P(('batch', 'dap'), None)
    vec_spec = P(None, None)
    mat_spec = P(None, None, None)

    def swap(x, bit):
        return lax.ppermute(x, 'dap', [(i, i ^ bit) for i in range(8)])

    def device_fn(z_rows, mask_rows, ln_in_scale, ln_in_bias, w_in, b_in, w_gate, b_gate, ln_out_scale, ln_out_bias, w_out, b_out):
        f32, bf16 = jnp.float32, jnp.bfloat16
        index = lax.axis_index('dap')
        chip, core = index // 2, index % 2
        z_own = z_rows.reshape(48, 4, 96, 128)
        z_x, z_y = [], []
        for n in range(3):
            part = (z_own if n == 0 else lax.optimization_barrier(z_own))[16 * n:16 * n + 16]
            z_x.append(swap(part, 2))
            z_y.append(swap(part, 4))
        mask_bf = mask_rows
        mask_x, mask_y = swap(mask_bf, 2), swap(mask_bf, 4)
        masks = [mask_bf, mask_x, mask_y]
        cut = lambda m, n: [m[:, i * n:i * n + n] for i in range(384 // n)]
        rel = jnp.concatenate(masks, axis=0)
        h = cut(rel, 192)
        rel = jnp.where(chip >= 2, jnp.concatenate([h[1], h[0]], axis=1), rel)
        q = cut(rel, 96)
        rel = jnp.where(chip % 2 == 1, jnp.concatenate([q[1], q[0], q[3], q[2]], axis=1), rel)
        j = jnp.arange(96)
        source = jnp.where(core == 0, j, (j + 48) % 96)
        perm = (source[:, None] == jnp.arange(128)[None, :]).astype(bf16)
        eye = jnp.arange(128)[:, None] == jnp.arange(128)[None, :]
        centre = (eye.astype(f32) - 1.0 / 128).astype(bf16)
        zero = jnp.zeros((1,), jnp.int32)
        where = jnp.reshape(chip, (1,)).astype(jnp.int32)
        vectors = jnp.concatenate([b_in.astype(f32) * 0.5] + [v.astype(f32) for v in (ln_in_scale, ln_in_bias, ln_out_scale, ln_out_bias)], axis=1)
        vectors = jnp.broadcast_to(vectors[:, :, None], (2, 1024, 128))
        rows4 = jnp.stack([b_out.astype(f32), b_gate.astype(f32) * 0.5, ln_in_scale.astype(f32), ln_in_bias.astype(f32)], axis=1)
        w_t = jnp.swapaxes(w_in * bf16(0.5), 1, 2)
        tri = (perm, centre, w_out, w_gate * bf16(0.5), vectors, rows4)
        spread = lambda arr: [(arr, i, 0) for i in range(4)]
        a_o, b_o = project(0, [(48, spread(z_own), mask_bf, 0)], vectors, w_t, centre, 2, perm)
        b_o2 = swap(b_o, 1)
        own = [(b_o, 0, 48), (b_o2, 0, 48)]
        o0, = triangle(0, where, [[(a_o, 0, 48, z_own, 0, 0)]], own, tri, a_o)
        x1, y2 = swap(o0, 2), swap(o0, 4)
        parts, last = [], o0
        for n in range(3):
            if n == 2:
                pair = lambda m, rel: ([(parts[m][0], 0, 16, z_x[m], rel, 0)], [(parts[m][0], 1, 16, z_y[m], rel, 0)])
                (xa, ya), (xb, yb) = pair(0, 0), pair(1, 0)
                x0, y0 = triangle(0, where, [xa + xb, ya + yb], own, tri, (last, rel), [(48, 1, 0, None, None)] * 2)
                last = x0
            a_n, b_n = project(0, [(16, spread(z_x[n]), mask_x, 16 * n), (16, spread(z_y[n]), mask_y, 16 * n)], vectors, w_t, centre, 2, last)
            parts.append((a_n, b_n, swap(b_n, 1)))
            last = a_n
        cols = lambda k: [(p[1], k, 16) for p in parts] + [(p[2], k, 16) for p in parts]
        piece_x = [(parts[n][0], 0, 16, z_x[n], 2, 0) for n in range(3)]
        x2, = triangle(0, where, [piece_x], cols(1), tri, last)
        o3 = swap(x2, 2)
        o1, = triangle(0, where, [[(a_o, 0, 48, z_own, 1, 0)]], cols(0), tri, x2)
        y3 = swap(o1, 4)
        o2, = triangle(0, where, [[(a_o, 0, 48, z_own, 2, 0)]], cols(1), tri, o1)
        x3 = swap(o2, 2)
        y1 = swap(o3, 4)
        xc, yc = pair(2, 0)
        x0, y0 = triangle(0, where, [xc, yc], own, tri, o2, [(48, 1, 32, None, x0), (48, 1, 32, None, y0)])

        tiles = lambda row, *arrs: [(arr, 0, row) for arr in arrs]
        a_o, b_o = project(1, [(48, tiles(0, o0, o1, o2, o3), rel, 0)], vectors, w_t, centre, 2, x0, 8)
        b_o2 = swap(b_o, 1)
        a_x, b_x = project(1, [(48, tiles(0, x0, x1, x2, x3), rel, 48)], vectors, w_t, centre, 2, a_o, 8)
        b_x2 = swap(b_x, 1)
        b_ya, = project(1, [(32, tiles(0, y0, y1, y2, y3), rel, 96)], vectors, w_t, centre, 1, a_x)
        b_ya2 = swap(b_ya, 1)
        b_yb, = project(1, [(16, tiles(32, y0, y1, y2, y3), rel, 128)], vectors, w_t, centre, 1, b_ya)
        b_yb2 = swap(b_yb, 1)
        own, col_x = [(b_o, 0, 48), (b_o2, 0, 48)], [(b_x, 0, 48), (b_x2, 0, 48)]
        col_y = [(b_ya, 0, 32), (b_yb, 0, 16), (b_ya2, 0, 32), (b_yb2, 0, 16)]
        q2, = triangle(1, where, [[(a_x, 0, 48, x2, None, 0)]], col_y, tri, b_yb)
        p3 = swap(q2, 2)
        out, = triangles(1, where, [
            ([(0, a_o, 0, 48, o0, None, 0)], own, [(0, 0, 0)]),
            ([(0, a_o, 0, 48, o1, None, 0)], col_x, [(0, 0, 1)]),
            ([(0, a_o, 0, 48, o2, None, 0)], col_y, [(0, 0, 2)]),
        ], [(48, 4, None)], tri, q2)
        out = lax.dynamic_update_slice(out, p3, (0, chip ^ 3, 0, 0))
        return out.reshape(48, 384, 128)

    return jax.shard_map(device_fn, mesh=mesh, in_specs=(row_spec, mask_spec, vec_spec, vec_spec, mat_spec, vec_spec, mat_spec, vec_spec, vec_spec, vec_spec, mat_spec, vec_spec), out_specs=row_spec, check_vma=False)
```

time: 576 us -> 340 us (0.59); the launches traced: 568 us -> 340 us
  waiting for transfers between devices: 336 us -> 103 us
  Pallas kernels: 0 us -> 198 us
  matrix products: 131 us -> 0 us
  other arithmetic: 45 us -> 7.61 us
  local copies, waits for them, and re-layouts: 40.9 us -> 11.8 us
  starting transfers between devices: 0.6 us -> 18.8 us
  between operations: 14.2 us -> 0.32 us
    all_gather x2 -> x0, waiting for transfers between devices: 336 us -> none  [device_fn(): b_full = lax.all_gather(b_own, 'dap', axis=1, tiled=True)]
    pallas_call x0 -> x16, Pallas kernels: none -> 198 us  [the longest x8 107 us: triangles(): pl.pallas_call(functools.partial(triangle_kernel, layer, static, len(a_po...]
    dot_general x10 -> x0, matrix products: 131 us -> none  [the longest x2 81 us: finish_layer(): jnp.einsum('cik,cjk->cij', a_side, b_full, preferred_element_type=jnp.flo...]
    ppermute x0 -> x23, waiting for transfers between devices: none -> 103 us  [swap(): return lax.ppermute(x, 'dap', [(i, i ^ bit) for i in range(8)])]
    convert_element_type x5 -> x0, local copies, waits for them, and re-layouts: 34.1 us -> none  [the longest x4 27.5 us: gated_side(): (mask_f[None] * jax.nn.sigmoid(projected[hidden:]) * projected[:hidden])....]
    convert_element_type x9 -> x4, other arithmetic: 33.4 us -> 1.31 us  [the longest x1 0.68 us: device_fn(): perm = (source[:, None] == jnp.arange(128)[None, :]).astype(bf16)]
    ppermute x0 -> x23, starting transfers between devices: none -> 18.8 us  [swap(): return lax.ppermute(x, 'dap', [(i, i ^ bit) for i in range(8)])]
    reduce_sum x5 -> x0, other arithmetic: 11.5 us -> none  [the longest x4 8.02 us: layer_norm(): var_val = jnp.mean(centred * centred, axis=axis, keepdims=True)]
  transfers between devices with their start and end apart: 2 -> 23, of which waited for: 2 -> 13; matrix products, arithmetic and copies ran while one was open for 3% -> 3% of each run, Pallas kernels for 0% -> 47%
where the time goes in v2:
time: 340 us
  Pallas kernels  198 us (58%)
  waiting for transfers between devices  103 us (30%)
  starting transfers between devices  18.8 us (6%)
  local copies, waits for them, and re-layouts  11.8 us (3%)
  other arithmetic  7.61 us (2%)
    pallas_call x8, Pallas kernels, triangles(): pl.pallas_call(functools.partial(triangle_kernel, layer, static, len(a_po...  107 us
    ppermute x23, waiting for transfers between devices, swap(): return lax.ppermute(x, 'dap', [(i, i ^ bit) for i in range(8)])  103 us
    pallas_call x8, Pallas kernels, project(): pl.pallas_call(functools.partial(project_kernel, layer, sides, team, [(n,...  90.8 us
    ppermute x23, starting transfers between devices, swap(): return lax.ppermute(x, 'dap', [(i, i ^ bit) for i in range(8)])  18.8 us
  transfers between devices with their start and end apart: 23, of which 13 were waited for; matrix products, arithmetic and copies ran while one was open for 3% of the time, Pallas kernels for 47%

profile of v2, /device:TPU:0, one launch (start us, length us, event | category | flops | bytes accessed | tf_op | source)
XLA Modules:
  0.0 339.9 jit_solution(11110325569657536400)
XLA Ops:
  0.0 0.6 add_convert_fusion.refs_7_.refs_5_.refs_12_.refs_9_.refs_13_.refs_6_
  0.6 0.7 fusion.refs_8_.refs_4_.refs_12_.refs_5_.refs_6_
  1.3 0.7 constant_dynamic-update-slice_fusion.4
  2.0 1.1 copy.15
  3.1 0.7 multiply_bitcast_fusion.refs_6_.refs_11_
  3.9 0.7 constant_dynamic-update-slice_fusion.3
  4.5 0.7 constant_dynamic-update-slice_fusion.2
  5.2 0.7 constant_dynamic-update-slice_fusion.1
  5.8 0.7 constant_dynamic-update-slice_fusion
  6.5 1.3 broadcast_in_dim.2.refs_5_.refs_8_.refs_10_.refs_12_.refs_16_.refs_9_
  7.8 14.9 %project.8 = (bf16[128,48,384]{2,1,0:T(8,128)(2,1)}, bf16[128,48,384]{2,1,0:T(8,128)(2,1)}) custom-call(bf16[48,4,96,128]{3,2,1,0:T(8,128)(2,1)} %bitcast.10, bf16[48,4,96,128]{3,2,1,0:T(8,128)(2,1)} %bitcast.11, bf16[48,4,96,128]{3,2,1,0:T(8,128)(2,1)} %bitcast.12, bf16[48,4,96,128]{3,2,1,0:T(8,128)(2,1)} %bitcast.13, s32[48,384]{1,0:T(8,128)} %refs_4_.1, ...), custom_call_target="tpu_custom_call" | custom-call | flops 2415919104 | bytes 14155776 | tf_op jit(solution)/shard_map/project/pallas_call | solution.py:147
  22.7 0.9 collective-permute-start
  23.6 2.7 slice.30
  26.3 2.5 collective-permute-start.1
  28.8 2.0 collective-permute-start.4
  30.9 0.6 broadcast_multiply_fusion.refs_7_.refs_11_.refs_15_.refs_8_.refs_9_
  31.5 4.0 %fusion.1 = (bf16[16,4,96,128]{3,2,1,0:T(8,128)(2,1)}, bf16[16,4,96,128]{3,2,1,0:T(8,128)(2,1)}) fusion(bf16[48,4,96,128]{3,2,1,0:T(8,128)(2,1)} %bitcast.14), kind=kLoop, calls=%fused_computation.21 | loop fusion | bytes 6291456 | tf_op jit(solution)/shard_map/slice | solution.py:349
  35.6 30.0 %collective-permute-done.3.refs_8_ = s32[48,384]{1,0:T(8,128)S(1)} collective-permute-done((s32[48,384]{1,0:T(8,128)S(1)}, s32[48,384]{1,0:T(8,128)S(1)}, u32[]{:S(2)}, u32[]{:S(2)}) %collective-permute-start.3) | collective-permute-done | bytes 73760 | tf_op jit(solution)/shard_map/ppermute | solution.py:340
  65.6 1.7 collective-permute-start.5
  67.4 1.5 collective-permute-start.6
  68.9 0.6 pad_maximum_fusion.refs_9_.refs_13_.refs_17_.refs_10_.refs_11_
  69.5 0.6 collective-permute-start.7
  70.1 0.3 collective-permute-start.8
  70.6 0.1 fusion.2
  70.7 0.9 add_select_fusion.1.refs_15_.refs_4_
  71.6 11.0 %triangle.8.refs_13_.refs_0_.refs_9_ = bf16[48,1,96,128]{3,2,1,0:T(8,128)(2,1)} custom-call(s32[1]{0:T(128)} %bitcast.where_ref, bf16[128,48,384]{2,1,0:T(8,128)(2,1)} %get-tuple-element.21.refs_0_.refs_10_, bf16[128,48,384]{2,1,0:T(8,128)(2,1)} %get-tuple-element.22.refs_1_.refs_2_, bf16[128,48,384]{2,1,0:T(8,128)(2,1)} %collective-permute-done.refs_2_.refs_3_, ...), custom_call_target="tpu_custom_call" | custom-call | flops 1061683200 | bytes 14155776 | tf_op jit(solution)/shard_map/triangle/pallas_call | solution.py:310
  82.6 11.1 %project.9 = (bf16[128,32,384]{2,1,0:T(8,128)(2,1)}, bf16[128,32,384]{2,1,0:T(8,128)(2,1)}) custom-call(bf16[16,4,96,128]{3,2,1,0:T(8,128)(2,1)} %copy-done, bf16[16,4,96,128]{3,2,1,0:T(8,128)(2,1)} %copy-done, bf16[16,4,96,128]{3,2,1,0:T(8,128)(2,1)} %copy-done, bf16[16,4,96,128]{3,2,1,0:T(8,128)(2,1)} %copy-done, ...), custom_call_target="tpu_custom_call" | custom-call | flops 1610612736 | bytes 9437184 | tf_op jit(solution)/shard_map/project/pallas_call | solution.py:147
  93.7 9.5 %collective-permute-done.5.refs_0_.refs_1_.refs_2_.refs_3_.refs_5_.refs_10_ = bf16[16,4,96,128]{3,2,1,0:T(8,128)(2,1)} collective-permute-done((bf16[16,4,96,128]{3,2,1,0:T(8,128)(2,1)}, bf16[16,4,96,128]{3,2,1,0:T(8,128)(2,1)}, u32[]{:S(2)}, u32[]{:S(2)}) %collective-permute-start.5) | collective-permute-done | bytes 1572896 | tf_op jit(solution)/shard_map/ppermute | solution.py:340
  103.2 1.7 collective-permute-done.6.refs_4_.refs_5_.refs_6_.refs_7_
  105.0 11.1 %project.10 = (bf16[128,32,384]{2,1,0:T(8,128)(2,1)}, bf16[128,32,384]{2,1,0:T(8,128)(2,1)}) custom-call(bf16[16,4,96,128]{3,2,1,0:T(8,128)(2,1)} %collective-permute-done.5.refs_0_.refs_1_.refs_2_.refs_3_.refs_5_.refs_10_, bf16[16,4,96,128]{3,2,1,0:T(8,128)(2,1)} %collective-permute-done.5.refs_0_.refs_1_.refs_2_.refs_3_.refs_5_.refs_10_, ...), custom_call_target="tpu_custom_call" | custom-call | flops 1610612736 | bytes 9437184 | tf_op jit(solution)/shard_map/project/pallas_call | solution.py:147
  116.1 12.7 %triangle.9 = (bf16[48,1,96,128]{3,2,1,0:T(8,128)(2,1)}, bf16[48,1,96,128]{3,2,1,0:T(8,128)(2,1)}) custom-call(s32[1]{0:T(128)} %bitcast.where_ref, bf16[128,32,384]{2,1,0:T(8,128)(2,1)} %get-tuple-element.24.refs_13_.refs_0_, bf16[128,32,384]{2,1,0:T(8,128)(2,1)} %get-tuple-element.26.refs_1_.refs_14_, ...), custom_call_target="tpu_custom_call" | custom-call | flops 1415577600 | bytes 15728640 | tf_op jit(solution)/shard_map/triangle/pallas_call | solution.py:310
  128.7 7.2 %collective-permute-done.7.refs_0_.refs_1_.refs_2_.refs_3_.refs_11_ = bf16[16,4,96,128]{3,2,1,0:T(8,128)(2,1)} collective-permute-done((bf16[16,4,96,128]{3,2,1,0:T(8,128)(2,1)}, bf16[16,4,96,128]{3,2,1,0:T(8,128)(2,1)}, u32[]{:S(2)}, u32[]{:S(2)}) %collective-permute-start.7) | collective-permute-done | bytes 1572896 | tf_op jit(solution)/shard_map/ppermute | solution.py:340
  135.9 1.2 collective-permute-done.8.refs_4_.refs_5_.refs_6_.refs_7_
  137.1 11.0 %project.11 = (bf16[128,32,384]{2,1,0:T(8,128)(2,1)}, bf16[128,32,384]{2,1,0:T(8,128)(2,1)}) custom-call(bf16[16,4,96,128]{3,2,1,0:T(8,128)(2,1)} %collective-permute-done.7.refs_0_.refs_1_.refs_2_.refs_3_.refs_11_, bf16[16,4,96,128]{3,2,1,0:T(8,128)(2,1)} %collective-permute-done.7.refs_0_.refs_1_.refs_2_.refs_3_.refs_11_, ...), custom_call_target="tpu_custom_call" | custom-call | flops 1610612736 | bytes 9437184 | tf_op jit(solution)/shard_map/project/pallas_call | solution.py:147
  148.2 0.5 collective-permute-start.10
  148.7 5.5 %collective-permute-done.11.refs_8_.refs_6_ = bf16[128,32,384]{2,1,0:T(8,128)(2,1)} collective-permute-done((bf16[128,32,384]{2,1,0:T(8,128)(2,1)}, bf16[128,32,384]{2,1,0:T(8,128)(2,1)}, u32[]{:S(2)}, u32[]{:S(2)}) %collective-permute-start.11) | collective-permute-done | bytes 3145760 | tf_op jit(solution)/shard_map/ppermute | solution.py:340
  154.2 4.5 %collective-permute-done.10.refs_7_.refs_5_ = bf16[128,32,384]{2,1,0:T(8,128)(2,1)} collective-permute-done((bf16[128,32,384]{2,1,0:T(8,128)(2,1)}, bf16[128,32,384]{2,1,0:T(8,128)(2,1)}, u32[]{:S(2)}, u32[]{:S(2)}) %collective-permute-start.10) | collective-permute-done | bytes 3145760 | tf_op jit(solution)/shard_map/ppermute | solution.py:340
  158.7 4.5 %collective-permute-done.9.refs_6_.refs_4_ = bf16[128,32,384]{2,1,0:T(8,128)(2,1)} collective-permute-done((bf16[128,32,384]{2,1,0:T(8,128)(2,1)}, bf16[128,32,384]{2,1,0:T(8,128)(2,1)}, u32[]{:S(2)}, u32[]{:S(2)}) %collective-permute-start.9) | collective-permute-done | bytes 3145760 | tf_op jit(solution)/shard_map/ppermute | solution.py:340
  163.2 11.9 %triangle.10.refs_14_.refs_2_.refs_5_ = bf16[48,1,96,128]{3,2,1,0:T(8,128)(2,1)} custom-call(s32[1]{0:T(128)} %bitcast.where_ref, bf16[128,32,384]{2,1,0:T(8,128)(2,1)} %get-tuple-element.24.refs_13_.refs_0_, bf16[128,32,384]{2,1,0:T(8,128)(2,1)} %get-tuple-element.26.refs_1_.refs_14_, bf16[128,32,384]{2,1,0:T(8,128)(2,1)} %get-tuple-element.29.refs_2_.refs_18_.refs_0_, ...), custom_call_target="tpu_custom_call" | custom-call | flops 1061683200 | bytes 14155776 | tf_op jit(solution)/shard_map/triangle/pallas_call | solution.py:310
  175.0 0.6 collective-permute-start.12
  175.6 1.5 collective-permute-start.14
  177.1 11.3 %triangle.11.refs_14_.refs_1_.refs_10_ = bf16[48,1,96,128]{3,2,1,0:T(8,128)(2,1)} custom-call(s32[1]{0:T(128)} %bitcast.where_ref, bf16[128,48,384]{2,1,0:T(8,128)(2,1)} %get-tuple-element.21.refs_0_.refs_10_, bf16[128,32,384]{2,1,0:T(8,128)(2,1)} %get-tuple-element.23.refs_3_.refs_1_, bf16[128,32,384]{2,1,0:T(8,128)(2,1)} %get-tuple-element.25.refs_4_.refs_2_, ...), custom_call_target="tpu_custom_call" | custom-call | flops 1061683200 | bytes 14155776 | tf_op jit(solution)/shard_map/triangle/pallas_call | solution.py:310
  188.4 11.3 %triangle.12.refs_11_.refs_2_ = bf16[48,1,96,128]{3,2,1,0:T(8,128)(2,1)} custom-call(s32[1]{0:T(128)} %bitcast.where_ref, bf16[128,48,384]{2,1,0:T(8,128)(2,1)} %get-tuple-element.21.refs_0_.refs_10_, bf16[128,32,384]{2,1,0:T(8,128)(2,1)} %get-tuple-element.23.refs_3_.refs_1_, bf16[128,32,384]{2,1,0:T(8,128)(2,1)} %get-tuple-element.25.refs_4_.refs_2_, ...), custom_call_target="tpu_custom_call" | custom-call | flops 1061683200 | bytes 14155776 | tf_op jit(solution)/shard_map/triangle/pallas_call | solution.py:310
  199.7 0.6 collective-permute-start.15
  200.3 1.5 collective-permute-start.18
  201.8 0.5 collective-permute-start.19
  202.4 1.9 collective-permute-done.12.refs_3_
  204.2 1.5 collective-permute-start.17
  205.7 9.0 %triangle.13 = (bf16[48,1,96,128]{3,2,1,0:T(8,128)(2,1)}, bf16[48,1,96,128]{3,2,1,0:T(8,128)(2,1)}) custom-call(s32[1]{0:T(128)} %bitcast.where_ref, bf16[128,32,384]{2,1,0:T(8,128)(2,1)} %get-tuple-element.29.refs_2_.refs_18_.refs_0_, bf16[128,48,384]{2,1,0:T(8,128)(2,1)} %get-tuple-element.22.refs_1_.refs_2_, ...), custom_call_target="tpu_custom_call", output_to_operand_aliasing={{0}: (13, {}), {1}: (14, {})} | custom-call | flops 707788800 | bytes 12582912 | tf_op jit(solution)/shard_map/triangle/pallas_call | solution.py:310
  214.8 14.5 %project.12 = (bf16[128,48,384]{2,1,0:T(8,128)(2,1)}, bf16[128,48,384]{2,1,0:T(8,128)(2,1)}) custom-call(bf16[48,1,96,128]{3,2,1,0:T(8,128)(2,1)} %triangle.8.refs_13_.refs_0_.refs_9_, bf16[48,1,96,128]{3,2,1,0:T(8,128)(2,1)} %triangle.11.refs_14_.refs_1_.refs_10_, bf16[48,1,96,128]{3,2,1,0:T(8,128)(2,1)} %triangle.12.refs_11_.refs_2_, ...), custom_call_target="tpu_custom_call" | custom-call | flops 2415919104 | bytes 14155776 | tf_op jit(solution)/shard_map/project/pallas_call | solution.py:147
  229.3 0.2 collective-permute-done.14.refs_1_
  229.5 24.4 %collective-permute-done.15.refs_3_ = bf16[48,1,96,128]{3,2,1,0:T(8,128)(2,1)} collective-permute-done((bf16[48,1,96,128]{3,2,1,0:T(8,128)(2,1)}, bf16[48,1,96,128]{3,2,1,0:T(8,128)(2,1)}, u32[]{:S(2)}, u32[]{:S(2)}) %collective-permute-start.15) | collective-permute-done | bytes 1179680 | tf_op jit(solution)/shard_map/ppermute | solution.py:340
  254.0 14.4 %project.13 = (bf16[128,48,384]{2,1,0:T(8,128)(2,1)}, bf16[128,48,384]{2,1,0:T(8,128)(2,1)}) custom-call(bf16[48,1,96,128]{3,2,1,0:T(8,128)(2,1)} %get-tuple-element.31.refs_8_.refs_0_, bf16[48,1,96,128]{3,2,1,0:T(8,128)(2,1)} %collective-permute-done.14.refs_1_, bf16[48,1,96,128]{3,2,1,0:T(8,128)(2,1)} %triangle.10.refs_14_.refs_2_.refs_5_, ...), custom_call_target="tpu_custom_call" | custom-call | flops 2415919104 | bytes 14155776 | tf_op jit(solution)/shard_map/project/pallas_call | solution.py:147
  268.4 0.5 collective-permute-start.13
  268.9 9.3 %collective-permute-done.17.refs_1_ = bf16[48,1,96,128]{3,2,1,0:T(8,128)(2,1)} collective-permute-done((bf16[48,1,96,128]{3,2,1,0:T(8,128)(2,1)}, bf16[48,1,96,128]{3,2,1,0:T(8,128)(2,1)}, u32[]{:S(2)}, u32[]{:S(2)}) %collective-permute-start.17) | collective-permute-done | bytes 1179680 | tf_op jit(solution)/shard_map/ppermute | solution.py:340
  278.2 8.4 %project.14.refs_8_.refs_1_.refs_5_ = bf16[128,32,384]{2,1,0:T(8,128)(2,1)} custom-call(bf16[48,1,96,128]{3,2,1,0:T(8,128)(2,1)} %get-tuple-element.35.refs_0_, bf16[48,1,96,128]{3,2,1,0:T(8,128)(2,1)} %collective-permute-done.17.refs_1_, bf16[48,1,96,128]{3,2,1,0:T(8,128)(2,1)} %collective-permute-done.18.refs_2_, ...), custom_call_target="tpu_custom_call" | custom-call | flops 805306368 | bytes 6291456 | tf_op jit(solution)/shard_map/project/pallas_call | solution.py:147
  286.6 5.4 %project.15.refs_2_.refs_12_.refs_6_ = bf16[128,16,384]{2,1,0:T(8,128)(2,1)} custom-call(bf16[48,1,96,128]{3,2,1,0:T(8,128)(2,1)} %get-tuple-element.35.refs_0_, bf16[48,1,96,128]{3,2,1,0:T(8,128)(2,1)} %collective-permute-done.17.refs_1_, bf16[48,1,96,128]{3,2,1,0:T(8,128)(2,1)} %collective-permute-done.18.refs_2_, ...), custom_call_target="tpu_custom_call" | custom-call | flops 402653184 | bytes 3145728 | tf_op jit(solution)/shard_map/project/pallas_call | solution.py:147
  292.0 0.5 collective-permute-start.21
  292.6 3.2 collective-permute-done.21.refs_4_.refs_8_
  295.8 1.1 copy-done.2
  296.9 11.2 %triangle.14.refs_18_ = bf16[48,1,96,128]{3,2,1,0:T(8,128)(2,1)} custom-call(s32[1]{0:T(128)} %bitcast.where_ref, bf16[128,48,384]{2,1,0:T(8,128)(2,1)} %get-tuple-element.36.refs_8_.refs_0_, bf16[128,32,384]{2,1,0:T(8,128)(2,1)} %project.14.refs_8_.refs_1_.refs_5_, bf16[128,16,384]{2,1,0:T(8,128)(2,1)} %project.15.refs_2_.refs_12_.refs_6_, ...), custom_call_target="tpu_custom_call" | custom-call | flops 1061683200 | bytes 14155776 | tf_op jit(solution)/shard_map/triangle/pallas_call | solution.py:310
  308.1 1.5 collective-permute-start.22
  309.6 29.0 %triangle.15 = bf16[48,4,96,128]{3,2,1,0:T(8,128)(2,1)} custom-call(s32[1]{0:T(128)} %bitcast.where_ref, bf16[128,48,384]{2,1,0:T(8,128)(2,1)} %get-tuple-element.32.refs_8_.refs_0_, bf16[128,48,384]{2,1,0:T(8,128)(2,1)} %get-tuple-element.33.refs_1_, bf16[128,48,384]{2,1,0:T(8,128)(2,1)} %collective-permute-done.13.refs_2_, ...), custom_call_target="tpu_custom_call" | custom-call | flops 3185049600 | bytes 23592960 | tf_op jit(solution)/shard_map/triangle/pallas_call | solution.py:310
  338.6 1.2 constant_dynamic-update-slice_fusion.8
  (47 shorter events, 0.5 us)
Async XLA Ops:
  22.7 6.1 %copy-start.5 = (s32[48,384]{1,0:T(8,128)S(1)}, s32[48,384]{1,0:T(8,128)}, u32[]{:S(2)}) copy-start(s32[48,384]{1,0:T(8,128)} %refs_4_.1) | copy-start | bytes 221188
  22.7 8.2 %copy-start.6 = (bf16[2,128,128]{2,1,0:T(8,128)(2,1)S(1)}, bf16[2,128,128]{2,1,0:T(8,128)(2,1)}, u32[]{:S(2)}) copy-start(bf16[2,128,128]{2,1,0:T(8,128)(2,1)} %param.18) | copy-start | bytes 196612
  22.7 47.4 %collective-permute-start = (bf16[128,48,384]{2,1,0:T(8,128)(2,1)}, bf16[128,48,384]{2,1,0:T(8,128)(2,1)}, u32[]{:S(2)}, u32[]{:S(2)}) collective-permute-start(bf16[128,48,384]{2,1,0:T(8,128)(2,1)} %get-tuple-element.22.refs_1_.refs_2_), channel_id=1, source_target_pairs={{0,1},{1,0},{2,3},{3,2},{4,5},{5,4},{6,7},{7,6}} | collective-permute-start | bytes 14155784 | tf_op jit(solution)/shard_map/ppermute | solution.py:340
  26.3 43.2 %collective-permute-start.1 = (bf16[16,4,96,128]{3,2,1,0:T(8,128)(2,1)}, bf16[16,4,96,128]{3,2,1,0:T(8,128)(2,1)S(1)}, u32[]{:S(2)}, u32[]{:S(2)}) collective-permute-start(bf16[16,4,96,128]{3,2,1,0:T(8,128)(2,1)} %bitcast.7), channel_id=1, source_target_pairs={{0,2},{1,3},{2,0},{3,1},{4,6},{5,7},{6,4},{7,5}} | collective-permute-start | bytes 4718600 | tf_op jit(solution)/shard_map/ppermute | solution.py:340
  28.8 36.8 %collective-permute-start.3 = (s32[48,384]{1,0:T(8,128)S(1)}, s32[48,384]{1,0:T(8,128)S(1)}, u32[]{:S(2)}, u32[]{:S(2)}) collective-permute-start(s32[48,384]{1,0:T(8,128)S(1)} %copy-done.5), channel_id=1, source_target_pairs={{0,2},{1,3},{2,0},{3,1},{4,6},{5,7},{6,4},{7,5}} | collective-permute-start | bytes 221192 | tf_op jit(solution)/shard_map/ppermute | solution.py:340
  28.8 38.5 %collective-permute-start.4 = (s32[48,384]{1,0:T(8,128)S(1)}, s32[48,384]{1,0:T(8,128)S(1)}, u32[]{:S(2)}, u32[]{:S(2)}) collective-permute-start(s32[48,384]{1,0:T(8,128)S(1)} %copy-done.5), channel_id=1, source_target_pairs={{0,4},{1,5},{2,6},{3,7},{4,0},{5,1},{6,2},{7,3}} | collective-permute-start | bytes 221192 | tf_op jit(solution)/shard_map/ppermute | solution.py:340
  30.9 51.7 %collective-permute-start.2 = (bf16[16,4,96,128]{3,2,1,0:T(8,128)(2,1)}, bf16[16,4,96,128]{3,2,1,0:T(8,128)(2,1)}, u32[]{:S(2)}, u32[]{:S(2)}) collective-permute-start(bf16[16,4,96,128]{3,2,1,0:T(8,128)(2,1)} %bitcast.7), channel_id=1, source_target_pairs={{0,4},{1,5},{2,6},{3,7},{4,0},{5,1},{6,2},{7,3}} | collective-permute-start | bytes 4718600 | tf_op jit(solution)/shard_map/ppermute | solution.py:340
  31.5 4.0 %copy-start.7 = (bf16[2,128]{1,0:T(2,128)(2,1)S(1)}, bf16[2,128]{1,0:T(2,128)(2,1)}, u32[]{:S(2)}) copy-start(bf16[2,128]{1,0:T(2,128)(2,1)} %param.19) | copy-start | bytes 1540
  31.5 4.0 %copy-start.8 = (bf16[2,128]{1,0:T(2,128)(2,1)S(1)}, bf16[2,128]{1,0:T(2,128)(2,1)}, u32[]{:S(2)}) copy-start(bf16[2,128]{1,0:T(2,128)(2,1)} %param.14) | copy-start | bytes 1540
  31.5 4.0 %copy-start.9 = (bf16[2,128]{1,0:T(2,128)(2,1)S(1)}, bf16[2,128]{1,0:T(2,128)(2,1)}, u32[]{:S(2)}) copy-start(bf16[2,128]{1,0:T(2,128)(2,1)} %param.15) | copy-start | bytes 1540
  31.5 4.1 %copy-start.10 = (bf16[2,128]{1,0:T(2,128)(2,1)S(1)}, bf16[2,128]{1,0:T(2,128)(2,1)}, u32[]{:S(2)}) copy-start(bf16[2,128]{1,0:T(2,128)(2,1)} %param.23) | copy-start | bytes 1540
  65.6 5.9 %copy-start.3 = (s32[48,384]{1,0:T(8,128)}, s32[48,384]{1,0:T(8,128)S(1)}, u32[]{:S(2)}) copy-start(s32[48,384]{1,0:T(8,128)S(1)} %collective-permute-done.3.refs_8_) | copy-start | bytes 221188
  65.6 37.6 %collective-permute-start.5 = (bf16[16,4,96,128]{3,2,1,0:T(8,128)(2,1)}, bf16[16,4,96,128]{3,2,1,0:T(8,128)(2,1)}, u32[]{:S(2)}, u32[]{:S(2)}) collective-permute-start(bf16[16,4,96,128]{3,2,1,0:T(8,128)(2,1)} %get-tuple-element.38), channel_id=1, source_target_pairs={{0,2},{1,3},{2,0},{3,1},{4,6},{5,7},{6,4},{7,5}} | collective-permute-start | bytes 4718600 | tf_op jit(solution)/shard_map/ppermute | solution.py:340
  67.4 4.2 %copy-start.4 = (s32[48,384]{1,0:T(8,128)}, s32[48,384]{1,0:T(8,128)S(1)}, u32[]{:S(2)}) copy-start(s32[48,384]{1,0:T(8,128)S(1)} %collective-permute-done.4.refs_9_) | copy-start | bytes 221188
  67.4 37.6 %collective-permute-start.6 = (bf16[16,4,96,128]{3,2,1,0:T(8,128)(2,1)}, bf16[16,4,96,128]{3,2,1,0:T(8,128)(2,1)}, u32[]{:S(2)}, u32[]{:S(2)}) collective-permute-start(bf16[16,4,96,128]{3,2,1,0:T(8,128)(2,1)} %get-tuple-element.38), channel_id=1, source_target_pairs={{0,4},{1,5},{2,6},{3,7},{4,0},{5,1},{6,2},{7,3}} | collective-permute-start | bytes 4718600 | tf_op jit(solution)/shard_map/ppermute | solution.py:340
  69.5 13.1 %copy-start = (bf16[16,4,96,128]{3,2,1,0:T(8,128)(2,1)}, bf16[16,4,96,128]{3,2,1,0:T(8,128)(2,1)S(1)}, u32[]{:S(2)}) copy-start(bf16[16,4,96,128]{3,2,1,0:T(8,128)(2,1)S(1)} %collective-permute-done.1.refs_0_.refs_1_.refs_2_.refs_3_.refs_4_.refs_9_) | copy-start | bytes 4718596
  69.5 66.4 %collective-permute-start.7 = (bf16[16,4,96,128]{3,2,1,0:T(8,128)(2,1)}, bf16[16,4,96,128]{3,2,1,0:T(8,128)(2,1)}, u32[]{:S(2)}, u32[]{:S(2)}) collective-permute-start(bf16[16,4,96,128]{3,2,1,0:T(8,128)(2,1)} %get-tuple-element.37), channel_id=1, source_target_pairs={{0,2},{1,3},{2,0},{3,1},{4,6},{5,7},{6,4},{7,5}} | collective-permute-start | bytes 4718600 | tf_op jit(solution)/shard_map/ppermute | solution.py:340
  70.1 67.0 %collective-permute-start.8 = (bf16[16,4,96,128]{3,2,1,0:T(8,128)(2,1)}, bf16[16,4,96,128]{3,2,1,0:T(8,128)(2,1)}, u32[]{:S(2)}, u32[]{:S(2)}) collective-permute-start(bf16[16,4,96,128]{3,2,1,0:T(8,128)(2,1)} %get-tuple-element.37), channel_id=1, source_target_pairs={{0,4},{1,5},{2,6},{3,7},{4,0},{5,1},{6,2},{7,3}} | collective-permute-start | bytes 4718600 | tf_op jit(solution)/shard_map/ppermute | solution.py:340
  148.1 6.0 %collective-permute-start.11 = (bf16[128,32,384]{2,1,0:T(8,128)(2,1)}, bf16[128,32,384]{2,1,0:T(8,128)(2,1)}, u32[]{:S(2)}, u32[]{:S(2)}) collective-permute-start(bf16[128,32,384]{2,1,0:T(8,128)(2,1)} %get-tuple-element.28.refs_5_.refs_3_), channel_id=1, source_target_pairs={{0,1},{1,0},{2,3},{3,2},{4,5},{5,4},{6,7},{7,6}} | collective-permute-start | bytes 9437192 | tf_op jit(solution)/shard_map/ppermute | solution.py:340
  148.2 10.5 %collective-permute-start.10 = (bf16[128,32,384]{2,1,0:T(8,128)(2,1)}, bf16[128,32,384]{2,1,0:T(8,128)(2,1)}, u32[]{:S(2)}, u32[]{:S(2)}) collective-permute-start(bf16[128,32,384]{2,1,0:T(8,128)(2,1)} %get-tuple-element.25.refs_4_.refs_2_), channel_id=1, source_target_pairs={{0,1},{1,0},{2,3},{3,2},{4,5},{5,4},{6,7},{7,6}} | collective-permute-start | bytes 9437192 | tf_op jit(solution)/shard_map/ppermute | solution.py:340
  148.7 14.5 %collective-permute-start.9 = (bf16[128,32,384]{2,1,0:T(8,128)(2,1)}, bf16[128,32,384]{2,1,0:T(8,128)(2,1)}, u32[]{:S(2)}, u32[]{:S(2)}) collective-permute-start(bf16[128,32,384]{2,1,0:T(8,128)(2,1)} %get-tuple-element.23.refs_3_.refs_1_), channel_id=1, source_target_pairs={{0,1},{1,0},{2,3},{3,2},{4,5},{5,4},{6,7},{7,6}} | collective-permute-start | bytes 9437192 | tf_op jit(solution)/shard_map/ppermute | solution.py:340
  163.2 12.5 %copy-start.1 = (bf16[48,1,96,128]{3,2,1,0:T(8,128)(2,1)S(1)}, bf16[48,1,96,128]{3,2,1,0:T(8,128)(2,1)}, u32[]{:S(2)}) copy-start(bf16[48,1,96,128]{3,2,1,0:T(8,128)(2,1)} %triangle.8.refs_13_.refs_0_.refs_9_) | copy-start | bytes 3538948
  175.0 29.2 %collective-permute-start.12 = (bf16[48,1,96,128]{3,2,1,0:T(8,128)(2,1)}, bf16[48,1,96,128]{3,2,1,0:T(8,128)(2,1)}, u32[]{:S(2)}, u32[]{:S(2)}) collective-permute-start(bf16[48,1,96,128]{3,2,1,0:T(8,128)(2,1)} %triangle.10.refs_14_.refs_2_.refs_5_), channel_id=1, source_target_pairs={{0,2},{1,3},{2,0},{3,1},{4,6},{5,7},{6,4},{7,5}} | collective-permute-start | bytes 3538952 | tf_op jit(solution)/shard_map/ppermute | solution.py:340
  175.6 53.9 %collective-permute-start.14 = (bf16[48,1,96,128]{3,2,1,0:T(8,128)(2,1)S(1)}, bf16[48,1,96,128]{3,2,1,0:T(8,128)(2,1)}, u32[]{:S(2)}, u32[]{:S(2)}) collective-permute-start(bf16[48,1,96,128]{3,2,1,0:T(8,128)(2,1)S(1)} %copy-done.1), channel_id=1, source_target_pairs={{0,2},{1,3},{2,0},{3,1},{4,6},{5,7},{6,4},{7,5}} | collective-permute-start | bytes 3538952 | tf_op jit(solution)/shard_map/ppermute | solution.py:340
  199.7 54.2 %collective-permute-start.15 = (bf16[48,1,96,128]{3,2,1,0:T(8,128)(2,1)}, bf16[48,1,96,128]{3,2,1,0:T(8,128)(2,1)}, u32[]{:S(2)}, u32[]{:S(2)}) collective-permute-start(bf16[48,1,96,128]{3,2,1,0:T(8,128)(2,1)} %triangle.12.refs_11_.refs_2_), channel_id=1, source_target_pairs={{0,2},{1,3},{2,0},{3,1},{4,6},{5,7},{6,4},{7,5}} | collective-permute-start | bytes 3538952 | tf_op jit(solution)/shard_map/ppermute | solution.py:340
  200.3 68.5 %collective-permute-start.18 = (bf16[48,1,96,128]{3,2,1,0:T(8,128)(2,1)S(1)}, bf16[48,1,96,128]{3,2,1,0:T(8,128)(2,1)}, u32[]{:S(2)}, u32[]{:S(2)}) collective-permute-start(bf16[48,1,96,128]{3,2,1,0:T(8,128)(2,1)S(1)} %copy-done.1), channel_id=1, source_target_pairs={{0,4},{1,5},{2,6},{3,7},{4,0},{5,1},{6,2},{7,3}} | collective-permute-start | bytes 3538952 | tf_op jit(solution)/shard_map/ppermute | solution.py:340
  201.8 67.0 %collective-permute-start.19 = (bf16[48,1,96,128]{3,2,1,0:T(8,128)(2,1)}, bf16[48,1,96,128]{3,2,1,0:T(8,128)(2,1)}, u32[]{:S(2)}, u32[]{:S(2)}) collective-permute-start(bf16[48,1,96,128]{3,2,1,0:T(8,128)(2,1)} %triangle.11.refs_14_.refs_1_.refs_10_), channel_id=1, source_target_pairs={{0,4},{1,5},{2,6},{3,7},{4,0},{5,1},{6,2},{7,3}} | collective-permute-start | bytes 3538952 | tf_op jit(solution)/shard_map/ppermute | solution.py:340
  204.2 73.9 %collective-permute-start.17 = (bf16[48,1,96,128]{3,2,1,0:T(8,128)(2,1)}, bf16[48,1,96,128]{3,2,1,0:T(8,128)(2,1)}, u32[]{:S(2)}, u32[]{:S(2)}) collective-permute-start(bf16[48,1,96,128]{3,2,1,0:T(8,128)(2,1)} %collective-permute-done.12.refs_3_), channel_id=1, source_target_pairs={{0,4},{1,5},{2,6},{3,7},{4,0},{5,1},{6,2},{7,3}} | collective-permute-start | bytes 3538952 | tf_op jit(solution)/shard_map/ppermute | solution.py:340
  268.3 41.3 %collective-permute-start.16 = (bf16[128,48,384]{2,1,0:T(8,128)(2,1)}, bf16[128,48,384]{2,1,0:T(8,128)(2,1)}, u32[]{:S(2)}, u32[]{:S(2)}) collective-permute-start(bf16[128,48,384]{2,1,0:T(8,128)(2,1)} %get-tuple-element.34.refs_3_), channel_id=1, source_target_pairs={{0,1},{1,0},{2,3},{3,2},{4,5},{5,4},{6,7},{7,6}} | collective-permute-start | bytes 14155784 | tf_op jit(solution)/shard_map/ppermute | solution.py:340
  268.4 41.3 %collective-permute-start.13 = (bf16[128,48,384]{2,1,0:T(8,128)(2,1)}, bf16[128,48,384]{2,1,0:T(8,128)(2,1)}, u32[]{:S(2)}, u32[]{:S(2)}) collective-permute-start(bf16[128,48,384]{2,1,0:T(8,128)(2,1)} %get-tuple-element.33.refs_1_), channel_id=1, source_target_pairs={{0,1},{1,0},{2,3},{3,2},{4,5},{5,4},{6,7},{7,6}} | collective-permute-start | bytes 14155784 | tf_op jit(solution)/shard_map/ppermute | solution.py:340
  286.6 9.2 %collective-permute-start.20 = (bf16[128,32,384]{2,1,0:T(8,128)(2,1)}, bf16[128,32,384]{2,1,0:T(8,128)(2,1)}, u32[]{:S(2)}, u32[]{:S(2)}) collective-permute-start(bf16[128,32,384]{2,1,0:T(8,128)(2,1)} %project.14.refs_8_.refs_1_.refs_5_), channel_id=1, source_target_pairs={{0,1},{1,0},{2,3},{3,2},{4,5},{5,4},{6,7},{7,6}} | collective-permute-start | bytes 9437192 | tf_op jit(solution)/shard_map/ppermute | solution.py:340
  292.0 3.8 %collective-permute-start.21 = (bf16[128,16,384]{2,1,0:T(8,128)(2,1)}, bf16[128,16,384]{2,1,0:T(8,128)(2,1)S(1)}, u32[]{:S(2)}, u32[]{:S(2)}) collective-permute-start(bf16[128,16,384]{2,1,0:T(8,128)(2,1)} %project.15.refs_2_.refs_12_.refs_6_), channel_id=1, source_target_pairs={{0,1},{1,0},{2,3},{3,2},{4,5},{5,4},{6,7},{7,6}} | collective-permute-start | bytes 4718600 | tf_op jit(solution)/shard_map/ppermute | solution.py:340
  295.8 1.1 copy-start.2
  308.1 30.5 %collective-permute-start.22 = (bf16[48,1,96,128]{3,2,1,0:T(8,128)(2,1)}, bf16[48,1,96,128]{3,2,1,0:T(8,128)(2,1)S(1)}, u32[]{:S(2)}, u32[]{:S(2)}) collective-permute-start(bf16[48,1,96,128]{3,2,1,0:T(8,128)(2,1)} %triangle.14.refs_18_), channel_id=1, source_target_pairs={{0,2},{1,3},{2,0},{3,1},{4,6},{5,7},{6,4},{7,5}} | collective-permute-start | bytes 3538952 | tf_op jit(solution)/shard_map/ppermute | solution.py:340

commit v3 on v2

--- a/solution.py
+++ b/solution.py
@@ -11,6 +11,9 @@
 CHUNK = 16
 GROUP = 16
 PITCH = 136
+CH = 128
+OWN = 48
+VMEM_BYTES = 67043328
 ROW_PITCH = 20
 NT = (((1,), (1,)), ((), ()))
 
@@ -66,10 +69,10 @@
             pltpu.make_async_copy(z_refs[0][t].at[0:team, sources[0][1][t][0]], dst, load_sem.at[g, t]).wait()
 
     def normalise(g):
-        z = zbuf[pl.ds(pl.multiple_of(g * team, team), team)].reshape(team * 384, 128)
+        z = zbuf[pl.ds(pl.multiple_of(g * team, team), team)].reshape(team * 384, CH)
         xc = lax.dot_general(centre[...], z, NT, preferred_element_type=jnp.float32)
         for lt in range(3 * team):
-            ls = slice(lt * 128, lt * 128 + 128)
+            ls = slice(lt * CH, lt * CH + CH)
             x = xc[:, ls]
             var = jnp.mean(x * x, axis=0, keepdims=True)
             znt[:, ls] = (x * lax.rsqrt(var + LN_EPS) * ln_s[...] + ln_b[...]).astype(jnp.bfloat16)
@@ -98,11 +101,11 @@
             for h in range(team):
                 i = g * team + h
                 for lt in range(3):
-                    ls = slice(h * 384 + lt * 128, h * 384 + lt * 128 + 128)
+                    ls = slice(h * 384 + lt * CH, h * 384 + lt * CH + CH)
                     for s in range(sides):
-                        value = proj[s * 256:s * 256 + 128, ls] + bias_ref[s * 256:s * 256 + 128]
-                        gate = proj[s * 256 + 128:s * 256 + 256, ls] + bias_ref[s * 256 + 128:s * 256 + 256]
-                        stage[s, lt, pl.ds(i, 128, stride=ROW_PITCH), :] = (jnp.tanh(gate) + 1.0) * value
+                        value = proj[s * 256:s * 256 + CH, ls] + bias_ref[s * 256:s * 256 + CH]
+                        gate = proj[s * 256 + CH:s * 256 + 256, ls] + bias_ref[s * 256 + CH:s * 256 + 256]
+                        stage[s, lt, pl.ds(i, CH, stride=ROW_PITCH), :] = (jnp.tanh(gate) + 1.0) * value
             return carry
 
         lax.fori_loop(0, ROWS // team, some, 0)
@@ -122,7 +125,7 @@
                     for lt in range(3):
                         view = stage.at[s, lt, pl.ds(pl.multiple_of(c0 * ROW_PITCH, 8), 8 * ROW_PITCH)]
                         for q in range(8):
-                            obuf[b % 2, s, c0 + q, :, lt * 128:lt * 128 + 128] = view[q * ROW_PITCH:q * ROW_PITCH + ROWS].astype(jnp.bfloat16) * m[:, lt * 128:lt * 128 + 128]
+                            obuf[b % 2, s, c0 + q, :, lt * CH:lt * CH + CH] = view[q * ROW_PITCH:q * ROW_PITCH + ROWS].astype(jnp.bfloat16) * m[:, lt * CH:lt * CH + CH]
                 return carry
 
             lax.fori_loop(0, 4, chan, 0)
@@ -147,15 +150,15 @@
     return pl.pallas_call(
         functools.partial(project_kernel, layer, sides, team, [(n, [tile[1:] for tile in tiles], at) for n, tiles, _, at in sources]),
         grid=(1,),
-        out_shape=[jax.ShapeDtypeStruct((128, rows, 384), jnp.bfloat16)] * sides,
+        out_shape=[jax.ShapeDtypeStruct((CH, rows, 384), jnp.bfloat16)] * sides,
         in_specs=in_specs,
         out_specs=[anywhere] * sides,
-        scratch_shapes=[pltpu.VMEM((256 * sides, team * 384), jnp.float32), pltpu.VMEM((128, team * 384), jnp.bfloat16), pltpu.VMEM((sides, 3, 128 * ROW_PITCH, 128), jnp.float32), pltpu.VMEM((rows, 384), jnp.bfloat16), pltpu.VMEM((rows, 384), jnp.int32),
-                        pltpu.VMEM((256 * sides, 128), jnp.float32), pltpu.VMEM((128, 128), jnp.float32), pltpu.VMEM((128, 128), jnp.float32), pltpu.VMEM((256 * sides, 128), jnp.bfloat16), pltpu.VMEM((128, 128), jnp.bfloat16),
-                        pltpu.VMEM((rows, 4, 96, 128), jnp.bfloat16), pltpu.VMEM((2, sides, 128, ROWS, 384), jnp.bfloat16),
+        scratch_shapes=[pltpu.VMEM((256 * sides, team * 384), jnp.float32), pltpu.VMEM((CH, team * 384), jnp.bfloat16), pltpu.VMEM((sides, 3, CH * ROW_PITCH, CH), jnp.float32), pltpu.VMEM((rows, 384), jnp.bfloat16), pltpu.VMEM((rows, 384), jnp.int32),
+                        pltpu.VMEM((256 * sides, CH), jnp.float32), pltpu.VMEM((CH, CH), jnp.float32), pltpu.VMEM((CH, CH), jnp.float32), pltpu.VMEM((256 * sides, CH), jnp.bfloat16), pltpu.VMEM((CH, CH), jnp.bfloat16),
+                        pltpu.VMEM((rows, 4, 96, CH), jnp.bfloat16), pltpu.VMEM((2, sides, CH, ROWS, 384), jnp.bfloat16),
                         pltpu.SemaphoreType.DMA((rows // team, 4)), pltpu.SemaphoreType.DMA((5 + len(sources),)), pltpu.SemaphoreType.DMA((2, sides, 4))],
-        compiler_params=pltpu.CompilerParams(dimension_semantics=('arbitrary',), vmem_limit_bytes=62 * 2**20),
-        cost_estimate=pl.CostEstimate(flops=rows * 384 * 128 * 512 * sides, bytes_accessed=rows * 384 * 256 * (1 + sides), transcendentals=0),
+        compiler_params=pltpu.CompilerParams(dimension_semantics=('arbitrary',), vmem_limit_bytes=VMEM_BYTES),
+        cost_estimate=pl.CostEstimate(flops=rows * 384 * CH * 512 * sides, bytes_accessed=rows * 384 * 256 * (1 + sides), transcendentals=0),
         name='project',
     )(*[tile[0] for _, tiles, _, _ in sources for tile in tiles], *[mask for _, _, mask, _ in sources], vectors, w_t, centre, dep)
 
@@ -213,28 +216,28 @@
                 copy.start()
             return carry
 
-        lax.fori_loop(0, 128 // CHUNK, start_loads, 0)
+        lax.fori_loop(0, CH // CHUNK, start_loads, 0)
         for copy in z_loads(j) + (params if j == 0 else []):
             copy.start()
-    tri[:, 96:128] = jnp.zeros((tri.shape[0], 32), jnp.float32)
+    tri[:, 96:CH] = jnp.zeros((tri.shape[0], 32), jnp.float32)
 
     def some_rows(i0, at):
         flipped = []
         for q in range(GROUP):
-            o = tri[pl.ds(pl.multiple_of((i0 + q) * PITCH, 8), 128), :]
+            o = tri[pl.ds(pl.multiple_of((i0 + q) * PITCH, 8), CH), :]
             on = norm_sublanes(o, ln_s[...], ln_b[...]).astype(jnp.bfloat16)
             flipped.append(lax.dot_general(perm_ref[...], on, NT, preferred_element_type=jnp.float32).astype(jnp.bfloat16))
         on = jnp.concatenate(flipped, axis=0)
         u = jnp.dot(on, w_out[...], preferred_element_type=jnp.float32) + b_out[...]
         u = u.astype(jnp.bfloat16).astype(jnp.float32)
-        zb = zbuf[pl.ds(at, GROUP)].reshape(GROUP * 96, 128)
+        zb = zbuf[pl.ds(at, GROUP)].reshape(GROUP * 96, CH)
         xc = jnp.dot(zb, centre[...], preferred_element_type=jnp.float32)
         z = zb.astype(jnp.float32)
         var = jnp.mean(xc * xc, axis=-1, keepdims=True)
         zn = (xc * lax.rsqrt(var + LN_EPS) * in_s[...] + in_b[...]).astype(jnp.bfloat16)
         g = jnp.dot(zn, w_gate[...], preferred_element_type=jnp.float32) + b_gate[...]
         g = 0.5 * jnp.tanh(g) + 0.5
-        obuf[pl.ds(at, GROUP)] = (z + g * u).astype(jnp.bfloat16).reshape(GROUP, 96, 128)
+        obuf[pl.ds(at, GROUP)] = (z + g * u).astype(jnp.bfloat16).reshape(GROUP, 96, CH)
 
     written = []
     for j, (pieces, b_pieces, outputs) in enumerate(jobs):
@@ -249,7 +252,7 @@
                 tri[pl.ds(c, rows, stride=PITCH), 0:96] = o
             return carry
 
-        lax.fori_loop(0, 128 // CHUNK, some_channels, 0)
+        lax.fori_loop(0, CH // CHUNK, some_channels, 0)
         for copy in z_loads(j) + (params if j == 0 else []):
             copy.wait()
 
@@ -309,17 +312,17 @@
     in_specs = [anywhere] * (len(a_pool) + len(b_pool) + len(z_pool) + len(params) + len(deps) + len(held))
     return pl.pallas_call(
         functools.partial(triangle_kernel, layer, static, len(a_pool), len(b_pool), len(z_pool), len(arrays), len(deps) + len(held)),
-        out_shape=[jax.ShapeDtypeStruct((n, width, 96, 128), jnp.bfloat16) for n, width, _ in arrays],
+        out_shape=[jax.ShapeDtypeStruct((n, width, 96, CH), jnp.bfloat16) for n, width, _ in arrays],
         input_output_aliases=aliases,
         grid_spec=pltpu.PrefetchScalarGridSpec(
             num_scalar_prefetch=1, grid=(1,), in_specs=in_specs, out_specs=[anywhere] * len(arrays),
-            scratch_shapes=[pltpu.VMEM((rows * PITCH, 128), jnp.float32), pltpu.VMEM((128, held_rows, 384), jnp.bfloat16), pltpu.VMEM((len(jobs), 128, 96, 384), jnp.bfloat16),
-                            pltpu.VMEM((total, 96, 128), jnp.bfloat16), pltpu.VMEM((total, 96, 128), jnp.bfloat16),
-                            pltpu.VMEM((96, 128), jnp.bfloat16), pltpu.VMEM((128, 128), jnp.bfloat16), pltpu.VMEM((128, 128), jnp.bfloat16), pltpu.VMEM((128, 128), jnp.bfloat16),
-                            pltpu.VMEM((128, 128), jnp.float32), pltpu.VMEM((128, 128), jnp.float32), pltpu.VMEM((4, 128), jnp.float32),
-                            pltpu.SemaphoreType.DMA((len(jobs), 128 // CHUNK, most_a + most_b)), pltpu.SemaphoreType.DMA((len(z_pool),)), pltpu.SemaphoreType.DMA((7,)), pltpu.SemaphoreType.DMA((total // GROUP,))]),
-        compiler_params=pltpu.CompilerParams(dimension_semantics=('arbitrary',), vmem_limit_bytes=62 * 2**20),
-        cost_estimate=pl.CostEstimate(flops=total * 96 * 128 * 1800, bytes_accessed=(total + 96) * 384 * 256, transcendentals=0),
+            scratch_shapes=[pltpu.VMEM((rows * PITCH, CH), jnp.float32), pltpu.VMEM((CH, held_rows, 384), jnp.bfloat16), pltpu.VMEM((len(jobs), CH, 96, 384), jnp.bfloat16),
+                            pltpu.VMEM((total, 96, CH), jnp.bfloat16), pltpu.VMEM((total, 96, CH), jnp.bfloat16),
+                            pltpu.VMEM((96, CH), jnp.bfloat16), pltpu.VMEM((CH, CH), jnp.bfloat16), pltpu.VMEM((CH, CH), jnp.bfloat16), pltpu.VMEM((CH, CH), jnp.bfloat16),
+                            pltpu.VMEM((CH, CH), jnp.float32), pltpu.VMEM((CH, CH), jnp.float32), pltpu.VMEM((4, CH), jnp.float32),
+                            pltpu.SemaphoreType.DMA((len(jobs), CH // CHUNK, most_a + most_b)), pltpu.SemaphoreType.DMA((len(z_pool),)), pltpu.SemaphoreType.DMA((7,)), pltpu.SemaphoreType.DMA((total // GROUP,))]),
+        compiler_params=pltpu.CompilerParams(dimension_semantics=('arbitrary',), vmem_limit_bytes=VMEM_BYTES),
+        cost_estimate=pl.CostEstimate(flops=total * 96 * CH * 1800, bytes_accessed=(total + 96) * 384 * 256, transcendentals=0),
         name='triangle',
     )(where, *a_pool, *b_pool, *z_pool, *params, *deps, *held)
 
@@ -343,7 +346,7 @@
         f32, bf16 = jnp.float32, jnp.bfloat16
         index = lax.axis_index('dap')
         chip, core = index // 2, index % 2
-        z_own = z_rows.reshape(48, 4, 96, 128)
+        z_own = z_rows.reshape(OWN, 4, 96, CH)
         z_x, z_y = [], []
         for n in range(3):
             part = (z_own if n == 0 else lax.optimization_barrier(z_own))[16 * n:16 * n + 16]
@@ -359,64 +362,67 @@
         q = cut(rel, 96)
         rel = jnp.where(chip % 2 == 1, jnp.concatenate([q[1], q[0], q[3], q[2]], axis=1), rel)
         j = jnp.arange(96)
-        source = jnp.where(core == 0, j, (j + 48) % 96)
-        perm = (source[:, None] == jnp.arange(128)[None, :]).astype(bf16)
-        eye = jnp.arange(128)[:, None] == jnp.arange(128)[None, :]
-        centre = (eye.astype(f32) - 1.0 / 128).astype(bf16)
+        source = jnp.where(core == 0, j, (j + OWN) % 96)
+        perm = (source[:, None] == jnp.arange(CH)[None, :]).astype(bf16)
+        eye = jnp.arange(CH)[:, None] == jnp.arange(CH)[None, :]
+        centre = (eye.astype(f32) - 1.0 / CH).astype(bf16)
         zero = jnp.zeros((1,), jnp.int32)
         where = jnp.reshape(chip, (1,)).astype(jnp.int32)
         vectors = jnp.concatenate([b_in.astype(f32) * 0.5] + [v.astype(f32) for v in (ln_in_scale, ln_in_bias, ln_out_scale, ln_out_bias)], axis=1)
-        vectors = jnp.broadcast_to(vectors[:, :, None], (2, 1024, 128))
+        vectors = jnp.broadcast_to(vectors[:, :, None], (2, 1024, CH))
         rows4 = jnp.stack([b_out.astype(f32), b_gate.astype(f32) * 0.5, ln_in_scale.astype(f32), ln_in_bias.astype(f32)], axis=1)
         w_t = jnp.swapaxes(w_in * bf16(0.5), 1, 2)
         tri = (perm, centre, w_out, w_gate * bf16(0.5), vectors, rows4)
         spread = lambda arr: [(arr, i, 0) for i in range(4)]
-        a_o, b_o = project(0, [(48, spread(z_own), mask_bf, 0)], vectors, w_t, centre, 2, perm)
+        a_o, b_o = project(0, [(OWN, spread(z_own), mask_bf, 0)], vectors, w_t, centre, 2, perm)
         b_o2 = swap(b_o, 1)
-        own = [(b_o, 0, 48), (b_o2, 0, 48)]
-        o0, = triangle(0, where, [[(a_o, 0, 48, z_own, 0, 0)]], own, tri, a_o)
+        own = [(b_o, 0, OWN), (b_o2, 0, OWN)]
+        o0, = triangle(0, where, [[(a_o, 0, OWN, z_own, 0, 0)]], own, tri, a_o)
         x1, y2 = swap(o0, 2), swap(o0, 4)
         parts, last = [], o0
-        for n in range(3):
-            if n == 2:
-                pair = lambda m, rel: ([(parts[m][0], 0, 16, z_x[m], rel, 0)], [(parts[m][0], 1, 16, z_y[m], rel, 0)])
-                (xa, ya), (xb, yb) = pair(0, 0), pair(1, 0)
-                x0, y0 = triangle(0, where, [xa + xb, ya + yb], own, tri, (last, rel), [(48, 1, 0, None, None)] * 2)
-                last = x0
+        for n in range(2):
             a_n, b_n = project(0, [(16, spread(z_x[n]), mask_x, 16 * n), (16, spread(z_y[n]), mask_y, 16 * n)], vectors, w_t, centre, 2, last)
-            parts.append((a_n, b_n, swap(b_n, 1)))
+            b_n2 = swap(b_n, 1)
+            parts.append([((a_n, k), (b_n, k), (b_n2, k)) for k in range(2)])
             last = a_n
-        cols = lambda k: [(p[1], k, 16) for p in parts] + [(p[2], k, 16) for p in parts]
-        piece_x = [(parts[n][0], 0, 16, z_x[n], 2, 0) for n in range(3)]
+        piece = lambda n, k, rel: (*parts[n][k][0], 16, (z_x, z_y)[k][n], rel, 0)
+        x0, y0 = triangle(0, where, [[piece(0, k, 0), piece(1, k, 0)] for k in range(2)], own, tri, (last, rel), [(OWN, 1, 0, None, None)] * 2)
+        a_y, b_y = project(0, [(16, spread(z_y[2]), mask_y, 32)], vectors, w_t, centre, 2, x0)
+        b_y2 = swap(b_y, 1)
+        a_x, b_x = project(0, [(16, spread(z_x[2]), mask_x, 32)], vectors, w_t, centre, 2, a_y)
+        b_x2 = swap(b_x, 1)
+        parts.append([((a_x, 0), (b_x, 0), (b_x2, 0)), ((a_y, 0), (b_y, 0), (b_y2, 0))])
+        cols = lambda k: [(*p[k][1], 16) for p in parts] + [(*p[k][2], 16) for p in parts]
+        piece_x = [piece(n, 0, 2) for n in range(3)]
+        last = a_x
         x2, = triangle(0, where, [piece_x], cols(1), tri, last)
         o3 = swap(x2, 2)
-        o1, = triangle(0, where, [[(a_o, 0, 48, z_own, 1, 0)]], cols(0), tri, x2)
+        o1, = triangle(0, where, [[(a_o, 0, OWN, z_own, 1, 0)]], cols(0), tri, x2)
         y3 = swap(o1, 4)
-        o2, = triangle(0, where, [[(a_o, 0, 48, z_own, 2, 0)]], cols(1), tri, o1)
+        o2, = triangle(0, where, [[(a_o, 0, OWN, z_own, 2, 0)]], cols(1), tri, o1)
         x3 = swap(o2, 2)
         y1 = swap(o3, 4)
-        xc, yc = pair(2, 0)
-        x0, y0 = triangle(0, where, [xc, yc], own, tri, o2, [(48, 1, 32, None, x0), (48, 1, 32, None, y0)])
+        x0, y0 = triangle(0, where, [[piece(2, k, 0)] for k in range(2)], own, tri, o2, [(OWN, 1, 32, None, x0), (OWN, 1, 32, None, y0)])
 
         tiles = lambda row, *arrs: [(arr, 0, row) for arr in arrs]
-        a_o, b_o = project(1, [(48, tiles(0, o0, o1, o2, o3), rel, 0)], vectors, w_t, centre, 2, x0, 8)
+        a_o, b_o = project(1, [(OWN, tiles(0, o0, o1, o2, o3), rel, 0)], vectors, w_t, centre, 2, x0, 8)
         b_o2 = swap(b_o, 1)
-        a_x, b_x = project(1, [(48, tiles(0, x0, x1, x2, x3), rel, 48)], vectors, w_t, centre, 2, a_o, 8)
+        a_x, b_x = project(1, [(OWN, tiles(0, x0, x1, x2, x3), rel, OWN)], vectors, w_t, centre, 2, a_o, 8)
         b_x2 = swap(b_x, 1)
         b_ya, = project(1, [(32, tiles(0, y0, y1, y2, y3), rel, 96)], vectors, w_t, centre, 1, a_x)
         b_ya2 = swap(b_ya, 1)
-        b_yb, = project(1, [(16, tiles(32, y0, y1, y2, y3), rel, 128)], vectors, w_t, centre, 1, b_ya)
+        b_yb, = project(1, [(16, tiles(32, y0, y1, y2, y3), rel, CH)], vectors, w_t, centre, 1, b_ya)
         b_yb2 = swap(b_yb, 1)
-        own, col_x = [(b_o, 0, 48), (b_o2, 0, 48)], [(b_x, 0, 48), (b_x2, 0, 48)]
+        own, col_x = [(b_o, 0, OWN), (b_o2, 0, OWN)], [(b_x, 0, OWN), (b_x2, 0, OWN)]
         col_y = [(b_ya, 0, 32), (b_yb, 0, 16), (b_ya2, 0, 32), (b_yb2, 0, 16)]
-        q2, = triangle(1, where, [[(a_x, 0, 48, x2, None, 0)]], col_y, tri, b_yb)
+        q2, = triangle(1, where, [[(a_x, 0, OWN, x2, None, 0)]], col_y, tri, b_yb)
         p3 = swap(q2, 2)
         out, = triangles(1, where, [
-            ([(0, a_o, 0, 48, o0, None, 0)], own, [(0, 0, 0)]),
-            ([(0, a_o, 0, 48, o1, None, 0)], col_x, [(0, 0, 1)]),
-            ([(0, a_o, 0, 48, o2, None, 0)], col_y, [(0, 0, 2)]),
-        ], [(48, 4, None)], tri, q2)
+            ([(0, a_o, 0, OWN, o0, None, 0)], own, [(0, 0, 0)]),
+            ([(0, a_o, 0, OWN, o1, None, 0)], col_x, [(0, 0, 1)]),
+            ([(0, a_o, 0, OWN, o2, None, 0)], col_y, [(0, 0, 2)]),
+        ], [(OWN, 4, None)], tri, q2)
         out = lax.dynamic_update_slice(out, p3, (0, chip ^ 3, 0, 0))
-        return out.reshape(48, 384, 128)
+        return out.reshape(OWN, 384, CH)
 
     return jax.shard_map(device_fn, mesh=mesh, in_specs=(row_spec, mask_spec, vec_spec, vec_spec, mat_spec, vec_spec, mat_spec, vec_spec, vec_spec, vec_spec, mat_spec, vec_spec), out_specs=row_spec, check_vma=False)

time: 340 us -> 347 us (1.021)
    pallas_call x8 -> x9, Pallas kernels: 90.8 us -> 93.4 us  [project(): pl.pallas_call(functools.partial(project_kernel, layer, sides, team, [(n,...]
    ppermute x23 -> x24, starting transfers between devices: 18.8 us -> 20.3 us  [swap(): return lax.ppermute(x, 'dap', [(i, i ^ bit) for i in range(8)])]
    ppermute x23 -> x24, waiting for transfers between devices: 103 us -> 103 us  [swap(): return lax.ppermute(x, 'dap', [(i, i ^ bit) for i in range(8)])]
  transfers between devices with their start and end apart: 23 -> 24, of which waited for: 13 -> 7; matrix products, arithmetic and copies ran while one was open for 3% -> 3% of each run, Pallas kernels for 47% -> 54%
where the time goes in v3:
time: 347 us; the launch traced here: 346 us
  Pallas kernels  201 us (58%)
  waiting for transfers between devices  103 us (30%)
  starting transfers between devices  20.3 us (6%)
  local copies, waits for them, and re-layouts  14.5 us (4%)
  other arithmetic  7.61 us (2%)
    pallas_call x8, Pallas kernels, triangles(): pl.pallas_call(functools.partial(triangle_kernel, layer, static, len(a_po...  107 us
    ppermute x24, waiting for transfers between devices, swap(): return lax.ppermute(x, 'dap', [(i, i ^ bit) for i in range(8)])  103 us
    pallas_call x9, Pallas kernels, project(): pl.pallas_call(functools.partial(project_kernel, layer, sides, team, [(n,...  93.4 us
    ppermute x24, starting transfers between devices, swap(): return lax.ppermute(x, 'dap', [(i, i ^ bit) for i in range(8)])  20.3 us
  transfers between devices with their start and end apart: 24, of which 7 were waited for; matrix products, arithmetic and copies ran while one was open for 3% of the time, Pallas kernels for 54%

profile of v3, /device:TPU:0, one launch (start us, length us, event | category | flops | bytes accessed | tf_op | source)
XLA Modules:
  0.0 346.1 jit_solution(4922918182534387151)
XLA Ops:
  0.0 0.6 add_convert_fusion.refs_7_.refs_5_.refs_12_.refs_9_.refs_13_
  0.6 0.7 fusion.refs_8_.refs_4_.refs_12_.refs_6_
  1.3 0.7 constant_dynamic-update-slice_fusion.4
  2.0 1.1 copy.15
  3.1 0.7 multiply_bitcast_fusion.refs_6_.refs_11_
  3.9 0.7 constant_dynamic-update-slice_fusion.3
  4.5 0.7 constant_dynamic-update-slice_fusion.2
  5.2 0.7 constant_dynamic-update-slice_fusion.1
  5.8 0.7 constant_dynamic-update-slice_fusion
  6.5 1.3 broadcast_in_dim.2.refs_5_.refs_8_.refs_10_.refs_12_.refs_16_
  7.8 14.8 %project.9 = (bf16[128,48,384]{2,1,0:T(8,128)(2,1)}, bf16[128,48,384]{2,1,0:T(8,128)(2,1)}) custom-call(bf16[48,4,96,128]{3,2,1,0:T(8,128)(2,1)} %bitcast.10, bf16[48,4,96,128]{3,2,1,0:T(8,128)(2,1)} %bitcast.11, bf16[48,4,96,128]{3,2,1,0:T(8,128)(2,1)} %bitcast.12, bf16[48,4,96,128]{3,2,1,0:T(8,128)(2,1)} %bitcast.13, s32[48,384]{1,0:T(8,128)} %refs_4_.1, ...), custom_call_target="tpu_custom_call" | custom-call | flops 2415919104 | bytes 14155776 | tf_op jit(solution)/shard_map/project/pallas_call | solution.py:150
  22.6 0.9 collective-permute-start
  23.5 2.5 collective-permute-start.3
  26.0 2.7 slice.30
  28.8 2.0 collective-permute-start.2
  30.8 4.0 %fusion.1 = (bf16[16,4,96,128]{3,2,1,0:T(8,128)(2,1)}, bf16[16,4,96,128]{3,2,1,0:T(8,128)(2,1)}) fusion(bf16[48,4,96,128]{3,2,1,0:T(8,128)(2,1)} %bitcast.14), kind=kLoop, calls=%fused_computation.21 | loop fusion | bytes 6291456 | tf_op jit(solution)/shard_map/slice | solution.py:352
  34.8 1.5 collective-permute-start.5
  36.3 0.5 collective-permute-start.6
  36.9 0.6 pad_maximum_fusion.refs_9_.refs_13_.refs_17_.refs_11_
  37.5 0.6 broadcast_multiply_fusion.refs_7_.refs_11_.refs_15_.refs_9_
  38.1 1.5 collective-permute-start.4
  39.6 11.0 %triangle.8.refs_13_.refs_0_.refs_9_ = bf16[48,1,96,128]{3,2,1,0:T(8,128)(2,1)} custom-call(s32[1]{0:T(128)} %bitcast.where_ref, bf16[128,48,384]{2,1,0:T(8,128)(2,1)} %get-tuple-element.23.refs_0_.refs_10_, bf16[128,48,384]{2,1,0:T(8,128)(2,1)} %get-tuple-element.24.refs_1_.refs_2_, bf16[128,48,384]{2,1,0:T(8,128)(2,1)} %collective-permute-done.refs_2_.refs_3_, ...), custom_call_target="tpu_custom_call" | custom-call | flops 1061683200 | bytes 14155776 | tf_op jit(solution)/shard_map/triangle/pallas_call | solution.py:313
  50.7 50.3 %collective-permute-done.4.refs_9_.refs_4_ = s32[48,384]{1,0:T(8,128)} collective-permute-done((s32[48,384]{1,0:T(8,128)}, s32[48,384]{1,0:T(8,128)}, u32[]{:S(2)}, u32[]{:S(2)}) %collective-permute-start.4) | collective-permute-done | bytes 73760 | tf_op jit(solution)/shard_map/ppermute | solution.py:343
  100.9 1.7 collective-permute-start.8
  102.6 10.9 %project.10 = (bf16[128,32,384]{2,1,0:T(8,128)(2,1)}, bf16[128,32,384]{2,1,0:T(8,128)(2,1)}) custom-call(bf16[16,4,96,128]{3,2,1,0:T(8,128)(2,1)} %collective-permute-done.1.refs_0_.refs_1_.refs_2_.refs_3_.refs_4_.refs_9_, bf16[16,4,96,128]{3,2,1,0:T(8,128)(2,1)} %collective-permute-done.1.refs_0_.refs_1_.refs_2_.refs_3_.refs_4_.refs_9_, ...), custom_call_target="tpu_custom_call" | custom-call | flops 1610612736 | bytes 9437184 | tf_op jit(solution)/shard_map/project/pallas_call | solution.py:150
  113.6 10.9 %project.11 = (bf16[128,32,384]{2,1,0:T(8,128)(2,1)}, bf16[128,32,384]{2,1,0:T(8,128)(2,1)}) custom-call(bf16[16,4,96,128]{3,2,1,0:T(8,128)(2,1)} %collective-permute-done.5.refs_0_.refs_1_.refs_2_.refs_3_.refs_5_.refs_10_, bf16[16,4,96,128]{3,2,1,0:T(8,128)(2,1)} %collective-permute-done.5.refs_0_.refs_1_.refs_2_.refs_3_.refs_5_.refs_10_, ...), custom_call_target="tpu_custom_call" | custom-call | flops 1610612736 | bytes 9437184 | tf_op jit(solution)/shard_map/project/pallas_call | solution.py:150
  124.6 0.5 collective-permute-start.9
  125.0 1.5 collective-permute-start.7
  126.5 0.9 constant_dynamic-update-slice_fusion.7
  127.4 0.9 constant_dynamic-update-slice_fusion.6
  128.3 0.9 constant_dynamic-update-slice_fusion.5
  129.2 0.1 fusion.3
  129.3 0.1 add_select_fusion
  129.4 0.1 fusion.2
  129.5 0.9 add_select_fusion.1.refs_15_.refs_4_
  130.4 12.7 %triangle.9 = (bf16[48,1,96,128]{3,2,1,0:T(8,128)(2,1)}, bf16[48,1,96,128]{3,2,1,0:T(8,128)(2,1)}) custom-call(s32[1]{0:T(128)} %bitcast.where_ref, bf16[128,32,384]{2,1,0:T(8,128)(2,1)} %get-tuple-element.26.refs_13_.refs_0_, bf16[128,32,384]{2,1,0:T(8,128)(2,1)} %get-tuple-element.28.refs_1_.refs_14_, ...), custom_call_target="tpu_custom_call" | custom-call | flops 1415577600 | bytes 15728640 | tf_op jit(solution)/shard_map/triangle/pallas_call | solution.py:313
  143.1 6.9 %project.12 = (bf16[128,16,384]{2,1,0:T(8,128)(2,1)}, bf16[128,16,384]{2,1,0:T(8,128)(2,1)}) custom-call(bf16[16,4,96,128]{3,2,1,0:T(8,128)(2,1)} %collective-permute-done.8.refs_0_.refs_1_.refs_2_.refs_3_.refs_5_, bf16[16,4,96,128]{3,2,1,0:T(8,128)(2,1)} %collective-permute-done.8.refs_0_.refs_1_.refs_2_.refs_3_.refs_5_, ...), custom_call_target="tpu_custom_call" | custom-call | flops 805306368 | bytes 4718592 | tf_op jit(solution)/shard_map/project/pallas_call | solution.py:150
  150.0 11.7 %collective-permute-done.7.refs_0_.refs_1_.refs_2_.refs_3_.refs_11_.refs_4_ = bf16[16,4,96,128]{3,2,1,0:T(8,128)(2,1)} collective-permute-done((bf16[16,4,96,128]{3,2,1,0:T(8,128)(2,1)}, bf16[16,4,96,128]{3,2,1,0:T(8,128)(2,1)}, u32[]{:S(2)}, u32[]{:S(2)}) %collective-permute-start.7) | collective-permute-done | bytes 1572896 | tf_op jit(solution)/shard_map/ppermute | solution.py:343
  161.7 7.1 %project.13 = (bf16[128,16,384]{2,1,0:T(8,128)(2,1)}, bf16[128,16,384]{2,1,0:T(8,128)(2,1)}) custom-call(bf16[16,4,96,128]{3,2,1,0:T(8,128)(2,1)} %collective-permute-done.7.refs_0_.refs_1_.refs_2_.refs_3_.refs_11_.refs_4_, bf16[16,4,96,128]{3,2,1,0:T(8,128)(2,1)} %collective-permute-done.7.refs_0_.refs_1_.refs_2_.refs_3_.refs_11_.refs_4_, ...), custom_call_target="tpu_custom_call" | custom-call | flops 805306368 | bytes 4718592 | tf_op jit(solution)/shard_map/project/pallas_call | solution.py:150
  168.9 11.7 %triangle.10.refs_14_.refs_2_.refs_5_ = bf16[48,1,96,128]{3,2,1,0:T(8,128)(2,1)} custom-call(s32[1]{0:T(128)} %bitcast.where_ref, bf16[128,32,384]{2,1,0:T(8,128)(2,1)} %get-tuple-element.26.refs_13_.refs_0_, bf16[128,32,384]{2,1,0:T(8,128)(2,1)} %get-tuple-element.28.refs_1_.refs_14_, bf16[128,16,384]{2,1,0:T(8,128)(2,1)} %get-tuple-element.32.refs_2_.refs_18_.refs_0_, ...), custom_call_target="tpu_custom_call" | custom-call | flops 1061683200 | bytes 14155776 | tf_op jit(solution)/shard_map/triangle/pallas_call | solution.py:313
  180.6 1.5 collective-permute-start.13
  182.1 0.5 collective-permute-start.15
  182.6 11.3 %triangle.11.refs_14_.refs_1_.refs_10_ = bf16[48,1,96,128]{3,2,1,0:T(8,128)(2,1)} custom-call(s32[1]{0:T(128)} %bitcast.where_ref, bf16[128,48,384]{2,1,0:T(8,128)(2,1)} %get-tuple-element.23.refs_0_.refs_10_, bf16[128,32,384]{2,1,0:T(8,128)(2,1)} %get-tuple-element.25.refs_3_.refs_1_, bf16[128,32,384]{2,1,0:T(8,128)(2,1)} %get-tuple-element.27.refs_4_.refs_2_, ...), custom_call_target="tpu_custom_call" | custom-call | flops 1061683200 | bytes 14155776 | tf_op jit(solution)/shard_map/triangle/pallas_call | solution.py:313
  193.9 11.3 %triangle.12.refs_12_.refs_2_.refs_11_ = bf16[48,1,96,128]{3,2,1,0:T(8,128)(2,1)} custom-call(s32[1]{0:T(128)} %bitcast.where_ref, bf16[128,48,384]{2,1,0:T(8,128)(2,1)} %get-tuple-element.23.refs_0_.refs_10_, bf16[128,32,384]{2,1,0:T(8,128)(2,1)} %get-tuple-element.25.refs_3_.refs_1_, bf16[128,32,384]{2,1,0:T(8,128)(2,1)} %get-tuple-element.27.refs_4_.refs_2_, ...), custom_call_target="tpu_custom_call" | custom-call | flops 1061683200 | bytes 14155776 | tf_op jit(solution)/shard_map/triangle/pallas_call | solution.py:313
  205.3 1.5 collective-permute-start.16
  206.8 0.5 collective-permute-start.19
  207.3 1.5 collective-permute-start.20
  208.8 0.9 collective-permute-done.13.refs_3_
  209.7 0.3 collective-permute-start.18
  210.0 9.1 %triangle.13 = (bf16[48,1,96,128]{3,2,1,0:T(8,128)(2,1)}, bf16[48,1,96,128]{3,2,1,0:T(8,128)(2,1)}) custom-call(s32[1]{0:T(128)} %bitcast.where_ref, bf16[128,16,384]{2,1,0:T(8,128)(2,1)} %get-tuple-element.32.refs_2_.refs_18_.refs_0_, bf16[128,16,384]{2,1,0:T(8,128)(2,1)} %get-tuple-element.30.refs_8_.refs_1_, ...), custom_call_target="tpu_custom_call", output_to_operand_aliasing={{0}: (14, {}), {1}: (15, {})} | custom-call | flops 707788800 | bytes 12582912 | tf_op jit(solution)/shard_map/triangle/pallas_call | solution.py:313
  219.1 14.4 %project.14 = (bf16[128,48,384]{2,1,0:T(8,128)(2,1)}, bf16[128,48,384]{2,1,0:T(8,128)(2,1)}) custom-call(bf16[48,1,96,128]{3,2,1,0:T(8,128)(2,1)} %triangle.8.refs_13_.refs_0_.refs_9_, bf16[48,1,96,128]{3,2,1,0:T(8,128)(2,1)} %triangle.11.refs_14_.refs_1_.refs_10_, bf16[48,1,96,128]{3,2,1,0:T(8,128)(2,1)} %triangle.12.refs_12_.refs_2_.refs_11_, ...), custom_call_target="tpu_custom_call" | custom-call | flops 2415919104 | bytes 14155776 | tf_op jit(solution)/shard_map/project/pallas_call | solution.py:150
  233.5 1.5 collective-permute-done.15.refs_1_
  235.0 24.8 %collective-permute-done.16.refs_3_ = bf16[48,1,96,128]{3,2,1,0:T(8,128)(2,1)} collective-permute-done((bf16[48,1,96,128]{3,2,1,0:T(8,128)(2,1)}, bf16[48,1,96,128]{3,2,1,0:T(8,128)(2,1)}, u32[]{:S(2)}, u32[]{:S(2)}) %collective-permute-start.16) | collective-permute-done | bytes 1179680 | tf_op jit(solution)/shard_map/ppermute | solution.py:343
  259.8 14.6 %project.15 = (bf16[128,48,384]{2,1,0:T(8,128)(2,1)}, bf16[128,48,384]{2,1,0:T(8,128)(2,1)}) custom-call(bf16[48,1,96,128]{3,2,1,0:T(8,128)(2,1)} %get-tuple-element.35.refs_8_.refs_0_, bf16[48,1,96,128]{3,2,1,0:T(8,128)(2,1)} %collective-permute-done.15.refs_1_, bf16[48,1,96,128]{3,2,1,0:T(8,128)(2,1)} %triangle.10.refs_14_.refs_2_.refs_5_, ...), custom_call_target="tpu_custom_call" | custom-call | flops 2415919104 | bytes 14155776 | tf_op jit(solution)/shard_map/project/pallas_call | solution.py:150
  274.4 0.5 collective-permute-start.14
  274.9 10.2 %collective-permute-done.18.refs_1_ = bf16[48,1,96,128]{3,2,1,0:T(8,128)(2,1)} collective-permute-done((bf16[48,1,96,128]{3,2,1,0:T(8,128)(2,1)}, bf16[48,1,96,128]{3,2,1,0:T(8,128)(2,1)}, u32[]{:S(2)}, u32[]{:S(2)}) %collective-permute-start.18) | collective-permute-done | bytes 1179680 | tf_op jit(solution)/shard_map/ppermute | solution.py:343
  285.2 8.3 %project.16.refs_8_.refs_1_.refs_5_ = bf16[128,32,384]{2,1,0:T(8,128)(2,1)} custom-call(bf16[48,1,96,128]{3,2,1,0:T(8,128)(2,1)} %get-tuple-element.39.refs_0_, bf16[48,1,96,128]{3,2,1,0:T(8,128)(2,1)} %collective-permute-done.18.refs_1_, bf16[48,1,96,128]{3,2,1,0:T(8,128)(2,1)} %collective-permute-done.19.refs_2_, ...), custom_call_target="tpu_custom_call" | custom-call | flops 805306368 | bytes 6291456 | tf_op jit(solution)/shard_map/project/pallas_call | solution.py:150
  293.5 5.4 %project.17.refs_2_.refs_12_.refs_6_ = bf16[128,16,384]{2,1,0:T(8,128)(2,1)} custom-call(bf16[48,1,96,128]{3,2,1,0:T(8,128)(2,1)} %get-tuple-element.39.refs_0_, bf16[48,1,96,128]{3,2,1,0:T(8,128)(2,1)} %collective-permute-done.18.refs_1_, bf16[48,1,96,128]{3,2,1,0:T(8,128)(2,1)} %collective-permute-done.19.refs_2_, ...), custom_call_target="tpu_custom_call" | custom-call | flops 402653184 | bytes 3145728 | tf_op jit(solution)/shard_map/project/pallas_call | solution.py:150
  299.0 0.5 collective-permute-start.22
  299.5 3.4 collective-permute-done.22.refs_4_.refs_8_
  302.9 11.1 %triangle.14.refs_18_ = bf16[48,1,96,128]{3,2,1,0:T(8,128)(2,1)} custom-call(s32[1]{0:T(128)} %bitcast.where_ref, bf16[128,48,384]{2,1,0:T(8,128)(2,1)} %get-tuple-element.40.refs_8_.refs_0_, bf16[128,32,384]{2,1,0:T(8,128)(2,1)} %project.16.refs_8_.refs_1_.refs_5_, bf16[128,16,384]{2,1,0:T(8,128)(2,1)} %project.17.refs_2_.refs_12_.refs_6_, ...), custom_call_target="tpu_custom_call" | custom-call | flops 1061683200 | bytes 14155776 | tf_op jit(solution)/shard_map/triangle/pallas_call | solution.py:313
  314.0 0.6 collective-permute-start.23
  314.6 29.0 %triangle.15 = bf16[48,4,96,128]{3,2,1,0:T(8,128)(2,1)} custom-call(s32[1]{0:T(128)} %bitcast.where_ref, bf16[128,48,384]{2,1,0:T(8,128)(2,1)} %get-tuple-element.36.refs_8_.refs_0_, bf16[128,48,384]{2,1,0:T(8,128)(2,1)} %get-tuple-element.37.refs_1_, bf16[128,48,384]{2,1,0:T(8,128)(2,1)} %collective-permute-done.14.refs_2_, ...), custom_call_target="tpu_custom_call" | custom-call | flops 3185049600 | bytes 23592960 | tf_op jit(solution)/shard_map/triangle/pallas_call | solution.py:313
  343.6 2.5 constant_dynamic-update-slice_fusion.8
  (38 shorter events, 0.3 us)
Async XLA Ops:
  22.6 15.5 %collective-permute-start = (bf16[128,48,384]{2,1,0:T(8,128)(2,1)}, bf16[128,48,384]{2,1,0:T(8,128)(2,1)}, u32[]{:S(2)}, u32[]{:S(2)}) collective-permute-start(bf16[128,48,384]{2,1,0:T(8,128)(2,1)} %get-tuple-element.24.refs_1_.refs_2_), channel_id=1, source_target_pairs={{0,1},{1,0},{2,3},{3,2},{4,5},{5,4},{6,7},{7,6}} | collective-permute-start | bytes 14155784 | tf_op jit(solution)/shard_map/ppermute | solution.py:343
  23.5 12.8 %collective-permute-start.3 = (s32[48,384]{1,0:T(8,128)}, s32[48,384]{1,0:T(8,128)}, u32[]{:S(2)}, u32[]{:S(2)}) collective-permute-start(s32[48,384]{1,0:T(8,128)} %refs_4_.1), channel_id=1, source_target_pairs={{0,2},{1,3},{2,0},{3,1},{4,6},{5,7},{6,4},{7,5}} | collective-permute-start | bytes 221192 | tf_op jit(solution)/shard_map/ppermute | solution.py:343
  28.7 8.1 %copy-start.1 = (bf16[2,128]{1,0:T(2,128)(2,1)S(1)}, bf16[2,128]{1,0:T(2,128)(2,1)}, u32[]{:S(2)}) copy-start(bf16[2,128]{1,0:T(2,128)(2,1)} %param.14) | copy-start | bytes 1540
  28.7 8.1 %copy-start.2 = (bf16[2,128]{1,0:T(2,128)(2,1)S(1)}, bf16[2,128]{1,0:T(2,128)(2,1)}, u32[]{:S(2)}) copy-start(bf16[2,128]{1,0:T(2,128)(2,1)} %param.15) | copy-start | bytes 1540
  28.7 8.1 %copy-start.3 = (bf16[2,128]{1,0:T(2,128)(2,1)S(1)}, bf16[2,128]{1,0:T(2,128)(2,1)}, u32[]{:S(2)}) copy-start(bf16[2,128]{1,0:T(2,128)(2,1)} %param.23) | copy-start | bytes 1540
  28.7 8.1 %copy-start.4 = (bf16[2,128]{1,0:T(2,128)(2,1)S(1)}, bf16[2,128]{1,0:T(2,128)(2,1)}, u32[]{:S(2)}) copy-start(bf16[2,128]{1,0:T(2,128)(2,1)} %param.19) | copy-start | bytes 1540
  28.7 8.7 %copy-start = (bf16[2,128,128]{2,1,0:T(8,128)(2,1)S(1)}, bf16[2,128,128]{2,1,0:T(8,128)(2,1)}, u32[]{:S(2)}) copy-start(bf16[2,128,128]{2,1,0:T(8,128)(2,1)} %param.18) | copy-start | bytes 196612
  28.7 73.9 %collective-permute-start.1 = (bf16[16,4,96,128]{3,2,1,0:T(8,128)(2,1)}, bf16[16,4,96,128]{3,2,1,0:T(8,128)(2,1)}, u32[]{:S(2)}, u32[]{:S(2)}) collective-permute-start(bf16[16,4,96,128]{3,2,1,0:T(8,128)(2,1)} %bitcast.7), channel_id=1, source_target_pairs={{0,2},{1,3},{2,0},{3,1},{4,6},{5,7},{6,4},{7,5}} | collective-permute-start | bytes 4718600 | tf_op jit(solution)/shard_map/ppermute | solution.py:343
  28.8 73.9 %collective-permute-start.2 = (bf16[16,4,96,128]{3,2,1,0:T(8,128)(2,1)}, bf16[16,4,96,128]{3,2,1,0:T(8,128)(2,1)}, u32[]{:S(2)}, u32[]{:S(2)}) collective-permute-start(bf16[16,4,96,128]{3,2,1,0:T(8,128)(2,1)} %bitcast.7), channel_id=1, source_target_pairs={{0,4},{1,5},{2,6},{3,7},{4,0},{5,1},{6,2},{7,3}} | collective-permute-start | bytes 4718600 | tf_op jit(solution)/shard_map/ppermute | solution.py:343
  34.8 78.8 %collective-permute-start.5 = (bf16[16,4,96,128]{3,2,1,0:T(8,128)(2,1)}, bf16[16,4,96,128]{3,2,1,0:T(8,128)(2,1)}, u32[]{:S(2)}, u32[]{:S(2)}) collective-permute-start(bf16[16,4,96,128]{3,2,1,0:T(8,128)(2,1)} %get-tuple-element.42), channel_id=1, source_target_pairs={{0,2},{1,3},{2,0},{3,1},{4,6},{5,7},{6,4},{7,5}} | collective-permute-start | bytes 4718600 | tf_op jit(solution)/shard_map/ppermute | solution.py:343
  36.3 77.3 %collective-permute-start.6 = (bf16[16,4,96,128]{3,2,1,0:T(8,128)(2,1)}, bf16[16,4,96,128]{3,2,1,0:T(8,128)(2,1)}, u32[]{:S(2)}, u32[]{:S(2)}) collective-permute-start(bf16[16,4,96,128]{3,2,1,0:T(8,128)(2,1)} %get-tuple-element.42), channel_id=1, source_target_pairs={{0,4},{1,5},{2,6},{3,7},{4,0},{5,1},{6,2},{7,3}} | collective-permute-start | bytes 4718600 | tf_op jit(solution)/shard_map/ppermute | solution.py:343
  38.1 62.8 %collective-permute-start.4 = (s32[48,384]{1,0:T(8,128)}, s32[48,384]{1,0:T(8,128)}, u32[]{:S(2)}, u32[]{:S(2)}) collective-permute-start(s32[48,384]{1,0:T(8,128)} %refs_4_.1), channel_id=1, source_target_pairs={{0,4},{1,5},{2,6},{3,7},{4,0},{5,1},{6,2},{7,3}} | collective-permute-start | bytes 221192 | tf_op jit(solution)/shard_map/ppermute | solution.py:343
  100.9 42.2 %collective-permute-start.8 = (bf16[16,4,96,128]{3,2,1,0:T(8,128)(2,1)}, bf16[16,4,96,128]{3,2,1,0:T(8,128)(2,1)}, u32[]{:S(2)}, u32[]{:S(2)}) collective-permute-start(bf16[16,4,96,128]{3,2,1,0:T(8,128)(2,1)} %get-tuple-element.41), channel_id=1, source_target_pairs={{0,4},{1,5},{2,6},{3,7},{4,0},{5,1},{6,2},{7,3}} | collective-permute-start | bytes 4718600 | tf_op jit(solution)/shard_map/ppermute | solution.py:343
  124.5 44.4 %collective-permute-start.10 = (bf16[128,32,384]{2,1,0:T(8,128)(2,1)}, bf16[128,32,384]{2,1,0:T(8,128)(2,1)}, u32[]{:S(2)}, u32[]{:S(2)}) collective-permute-start(bf16[128,32,384]{2,1,0:T(8,128)(2,1)} %get-tuple-element.27.refs_4_.refs_2_), channel_id=1, source_target_pairs={{0,1},{1,0},{2,3},{3,2},{4,5},{5,4},{6,7},{7,6}} | collective-permute-start | bytes 9437192 | tf_op jit(solution)/shard_map/ppermute | solution.py:343
  124.6 44.3 %collective-permute-start.9 = (bf16[128,32,384]{2,1,0:T(8,128)(2,1)}, bf16[128,32,384]{2,1,0:T(8,128)(2,1)}, u32[]{:S(2)}, u32[]{:S(2)}) collective-permute-start(bf16[128,32,384]{2,1,0:T(8,128)(2,1)} %get-tuple-element.25.refs_3_.refs_1_), channel_id=1, source_target_pairs={{0,1},{1,0},{2,3},{3,2},{4,5},{5,4},{6,7},{7,6}} | collective-permute-start | bytes 9437192 | tf_op jit(solution)/shard_map/ppermute | solution.py:343
  125.0 36.7 %collective-permute-start.7 = (bf16[16,4,96,128]{3,2,1,0:T(8,128)(2,1)}, bf16[16,4,96,128]{3,2,1,0:T(8,128)(2,1)}, u32[]{:S(2)}, u32[]{:S(2)}) collective-permute-start(bf16[16,4,96,128]{3,2,1,0:T(8,128)(2,1)} %get-tuple-element.41), channel_id=1, source_target_pairs={{0,2},{1,3},{2,0},{3,1},{4,6},{5,7},{6,4},{7,5}} | collective-permute-start | bytes 4718600 | tf_op jit(solution)/shard_map/ppermute | solution.py:343
  150.0 18.9 %collective-permute-start.12 = (bf16[128,16,384]{2,1,0:T(8,128)(2,1)}, bf16[128,16,384]{2,1,0:T(8,128)(2,1)}, u32[]{:S(2)}, u32[]{:S(2)}) collective-permute-start(bf16[128,16,384]{2,1,0:T(8,128)(2,1)} %get-tuple-element.33.refs_5_.refs_3_), channel_id=1, source_target_pairs={{0,1},{1,0},{2,3},{3,2},{4,5},{5,4},{6,7},{7,6}} | collective-permute-start | bytes 4718600 | tf_op jit(solution)/shard_map/ppermute | solution.py:343
  168.8 13.8 %collective-permute-start.11 = (bf16[128,16,384]{2,1,0:T(8,128)(2,1)}, bf16[128,16,384]{2,1,0:T(8,128)(2,1)}, u32[]{:S(2)}, u32[]{:S(2)}) collective-permute-start(bf16[128,16,384]{2,1,0:T(8,128)(2,1)} %get-tuple-element.31.refs_3_), channel_id=1, source_target_pairs={{0,1},{1,0},{2,3},{3,2},{4,5},{5,4},{6,7},{7,6}} | collective-permute-start | bytes 4718600 | tf_op jit(solution)/shard_map/ppermute | solution.py:343
  180.6 29.2 %collective-permute-start.13 = (bf16[48,1,96,128]{3,2,1,0:T(8,128)(2,1)}, bf16[48,1,96,128]{3,2,1,0:T(8,128)(2,1)}, u32[]{:S(2)}, u32[]{:S(2)}) collective-permute-start(bf16[48,1,96,128]{3,2,1,0:T(8,128)(2,1)} %triangle.10.refs_14_.refs_2_.refs_5_), channel_id=1, source_target_pairs={{0,2},{1,3},{2,0},{3,1},{4,6},{5,7},{6,4},{7,5}} | collective-permute-start | bytes 3538952 | tf_op jit(solution)/shard_map/ppermute | solution.py:343
  182.1 52.9 %collective-permute-start.15 = (bf16[48,1,96,128]{3,2,1,0:T(8,128)(2,1)}, bf16[48,1,96,128]{3,2,1,0:T(8,128)(2,1)}, u32[]{:S(2)}, u32[]{:S(2)}) collective-permute-start(bf16[48,1,96,128]{3,2,1,0:T(8,128)(2,1)} %triangle.8.refs_13_.refs_0_.refs_9_), channel_id=1, source_target_pairs={{0,2},{1,3},{2,0},{3,1},{4,6},{5,7},{6,4},{7,5}} | collective-permute-start | bytes 3538952 | tf_op jit(solution)/shard_map/ppermute | solution.py:343
  205.3 54.5 %collective-permute-start.16 = (bf16[48,1,96,128]{3,2,1,0:T(8,128)(2,1)}, bf16[48,1,96,128]{3,2,1,0:T(8,128)(2,1)}, u32[]{:S(2)}, u32[]{:S(2)}) collective-permute-start(bf16[48,1,96,128]{3,2,1,0:T(8,128)(2,1)} %triangle.12.refs_12_.refs_2_.refs_11_), channel_id=1, source_target_pairs={{0,2},{1,3},{2,0},{3,1},{4,6},{5,7},{6,4},{7,5}} | collective-permute-start | bytes 3538952 | tf_op jit(solution)/shard_map/ppermute | solution.py:343
  206.8 68.1 %collective-permute-start.19 = (bf16[48,1,96,128]{3,2,1,0:T(8,128)(2,1)}, bf16[48,1,96,128]{3,2,1,0:T(8,128)(2,1)}, u32[]{:S(2)}, u32[]{:S(2)}) collective-permute-start(bf16[48,1,96,128]{3,2,1,0:T(8,128)(2,1)} %triangle.8.refs_13_.refs_0_.refs_9_), channel_id=1, source_target_pairs={{0,4},{1,5},{2,6},{3,7},{4,0},{5,1},{6,2},{7,3}} | collective-permute-start | bytes 3538952 | tf_op jit(solution)/shard_map/ppermute | solution.py:343
  207.3 67.6 %collective-permute-start.20 = (bf16[48,1,96,128]{3,2,1,0:T(8,128)(2,1)}, bf16[48,1,96,128]{3,2,1,0:T(8,128)(2,1)}, u32[]{:S(2)}, u32[]{:S(2)}) collective-permute-start(bf16[48,1,96,128]{3,2,1,0:T(8,128)(2,1)} %triangle.11.refs_14_.refs_1_.refs_10_), channel_id=1, source_target_pairs={{0,4},{1,5},{2,6},{3,7},{4,0},{5,1},{6,2},{7,3}} | collective-permute-start | bytes 3538952 | tf_op jit(solution)/shard_map/ppermute | solution.py:343
  209.7 75.4 %collective-permute-start.18 = (bf16[48,1,96,128]{3,2,1,0:T(8,128)(2,1)}, bf16[48,1,96,128]{3,2,1,0:T(8,128)(2,1)}, u32[]{:S(2)}, u32[]{:S(2)}) collective-permute-start(bf16[48,1,96,128]{3,2,1,0:T(8,128)(2,1)} %collective-permute-done.13.refs_3_), channel_id=1, source_target_pairs={{0,4},{1,5},{2,6},{3,7},{4,0},{5,1},{6,2},{7,3}} | collective-permute-start | bytes 3538952 | tf_op jit(solution)/shard_map/ppermute | solution.py:343
  274.4 40.2 %collective-permute-start.17 = (bf16[128,48,384]{2,1,0:T(8,128)(2,1)}, bf16[128,48,384]{2,1,0:T(8,128)(2,1)}, u32[]{:S(2)}, u32[]{:S(2)}) collective-permute-start(bf16[128,48,384]{2,1,0:T(8,128)(2,1)} %get-tuple-element.38.refs_3_), channel_id=1, source_target_pairs={{0,1},{1,0},{2,3},{3,2},{4,5},{5,4},{6,7},{7,6}} | collective-permute-start | bytes 14155784 | tf_op jit(solution)/shard_map/ppermute | solution.py:343
  274.4 40.2 %collective-permute-start.14 = (bf16[128,48,384]{2,1,0:T(8,128)(2,1)}, bf16[128,48,384]{2,1,0:T(8,128)(2,1)}, u32[]{:S(2)}, u32[]{:S(2)}) collective-permute-start(bf16[128,48,384]{2,1,0:T(8,128)(2,1)} %get-tuple-element.37.refs_1_), channel_id=1, source_target_pairs={{0,1},{1,0},{2,3},{3,2},{4,5},{5,4},{6,7},{7,6}} | collective-permute-start | bytes 14155784 | tf_op jit(solution)/shard_map/ppermute | solution.py:343
  293.5 9.4 %collective-permute-start.21 = (bf16[128,32,384]{2,1,0:T(8,128)(2,1)}, bf16[128,32,384]{2,1,0:T(8,128)(2,1)}, u32[]{:S(2)}, u32[]{:S(2)}) collective-permute-start(bf16[128,32,384]{2,1,0:T(8,128)(2,1)} %project.16.refs_8_.refs_1_.refs_5_), channel_id=1, source_target_pairs={{0,1},{1,0},{2,3},{3,2},{4,5},{5,4},{6,7},{7,6}} | collective-permute-start | bytes 9437192 | tf_op jit(solution)/shard_map/ppermute | solution.py:343
  299.0 3.9 %collective-permute-start.22 = (bf16[128,16,384]{2,1,0:T(8,128)(2,1)}, bf16[128,16,384]{2,1,0:T(8,128)(2,1)}, u32[]{:S(2)}, u32[]{:S(2)}) collective-permute-start(bf16[128,16,384]{2,1,0:T(8,128)(2,1)} %project.17.refs_2_.refs_12_.refs_6_), channel_id=1, source_target_pairs={{0,1},{1,0},{2,3},{3,2},{4,5},{5,4},{6,7},{7,6}} | collective-permute-start | bytes 4718600 | tf_op jit(solution)/shard_map/ppermute | solution.py:343
  314.0 29.6 %collective-permute-start.23 = (bf16[48,1,96,128]{3,2,1,0:T(8,128)(2,1)}, bf16[48,1,96,128]{3,2,1,0:T(8,128)(2,1)}, u32[]{:S(2)}, u32[]{:S(2)}) collective-permute-start(bf16[48,1,96,128]{3,2,1,0:T(8,128)(2,1)} %triangle.14.refs_18_), channel_id=1, source_target_pairs={{0,2},{1,3},{2,0},{3,1},{4,6},{5,7},{6,4},{7,5}} | collective-permute-start | bytes 3538952 | tf_op jit(solution)/shard_map/ppermute | solution.py:343

commit v4 on v3

--- a/solution.py
+++ b/solution.py
@@ -30,14 +30,14 @@
     mask_refs, refs = refs[:len(sources)], refs[len(sources):]
     vectors, w_t, centre_in = refs[:3]
     outs = refs[4:4 + sides]
-    proj, znt, stage, keep, mask, bias_ref, ln_s, ln_b, w_ref, centre, zbuf, obuf, load_sem, param_sem, out_sem = refs[4 + sides:]
+    proj, znt, stage, keep, bias_ref, ln_s, ln_b, w_ref, centre, zbuf, obuf, load_sem, param_sem, out_sem = refs[4 + sides:]
     rows = sum(n for n, _, _ in sources)
     side0 = 512 - 256 * sides
     moves = [(centre_in, centre), (vectors.at[layer, 512:640], ln_s), (vectors.at[layer, 640:768], ln_b),
              (w_t.at[layer, side0:512], w_ref), (vectors.at[layer, side0:512], bias_ref)]
     at = 0
     for n, (count, _, mask_row) in enumerate(sources):
-        moves.append((mask_refs[n].at[mask_row:mask_row + count], mask.at[at:at + count]))
+        moves.append((mask_refs[n].at[mask_row:mask_row + count], keep.at[at:at + count]))
         at += count
     params = [pltpu.make_async_copy(src, dst, param_sem.at[n]) for n, (src, dst) in enumerate(moves)]
     groups = rows // team
@@ -85,7 +85,6 @@
     arrive(0)
     for copy in params:
         copy.wait()
-    keep[...] = mask[...].astype(jnp.float32).astype(jnp.bfloat16)
     normalise(0)
 
     def block(b, carry):
@@ -153,7 +152,7 @@
         out_shape=[jax.ShapeDtypeStruct((CH, rows, 384), jnp.bfloat16)] * sides,
         in_specs=in_specs,
         out_specs=[anywhere] * sides,
-        scratch_shapes=[pltpu.VMEM((256 * sides, team * 384), jnp.float32), pltpu.VMEM((CH, team * 384), jnp.bfloat16), pltpu.VMEM((sides, 3, CH * ROW_PITCH, CH), jnp.float32), pltpu.VMEM((rows, 384), jnp.bfloat16), pltpu.VMEM((rows, 384), jnp.int32),
+        scratch_shapes=[pltpu.VMEM((256 * sides, team * 384), jnp.float32), pltpu.VMEM((CH, team * 384), jnp.bfloat16), pltpu.VMEM((sides, 3, CH * ROW_PITCH, CH), jnp.float32), pltpu.VMEM((rows, 384), jnp.bfloat16),
                         pltpu.VMEM((256 * sides, CH), jnp.float32), pltpu.VMEM((CH, CH), jnp.float32), pltpu.VMEM((CH, CH), jnp.float32), pltpu.VMEM((256 * sides, CH), jnp.bfloat16), pltpu.VMEM((CH, CH), jnp.bfloat16),
                         pltpu.VMEM((rows, 4, 96, CH), jnp.bfloat16), pltpu.VMEM((2, sides, CH, ROWS, 384), jnp.bfloat16),
                         pltpu.SemaphoreType.DMA((rows // team, 4)), pltpu.SemaphoreType.DMA((5 + len(sources),)), pltpu.SemaphoreType.DMA((2, sides, 4))],
@@ -248,7 +247,7 @@
                 copy.wait()
             for cc in range(CHUNK):
                 c = q * CHUNK + cc
-                o = lax.dot_general(abuf[c, a_at[j]:a_at[j] + rows], bbuf[j, c], NT, preferred_element_type=jnp.float32)
+                o = lax.dot_general(bbuf[j, c], abuf[c, a_at[j]:a_at[j] + rows], NT, preferred_element_type=jnp.float32).T
                 tri[pl.ds(c, rows, stride=PITCH), 0:96] = o
             return carry
 
@@ -352,7 +351,7 @@
             part = (z_own if n == 0 else lax.optimization_barrier(z_own))[16 * n:16 * n + 16]
             z_x.append(swap(part, 2))
             z_y.append(swap(part, 4))
-        mask_bf = mask_rows
+        mask_bf = mask_rows.astype(bf16)
         mask_x, mask_y = swap(mask_bf, 2), swap(mask_bf, 4)
         masks = [mask_bf, mask_x, mask_y]
         cut = lambda m, n: [m[:, i * n:i * n + n] for i in range(384 // n)]

time: 347 us -> 344 us (level)
  Pallas kernels: 201 us -> 195 us
    pallas_call x8, Pallas kernels: 107 us -> 101 us  [triangles(): pl.pallas_call(functools.partial(triangle_kernel, layer, static, len(a_po...]
  transfers between devices with their start and end apart: 24 -> 24, of which waited for: 7 -> 8; matrix products, arithmetic and copies ran while one was open for 3% -> 3% of each run, Pallas kernels for 54% -> 52%
where the time goes in v4:
time: 344 us; the launch traced here: 343 us
  Pallas kernels  195 us (57%)
  waiting for transfers between devices  106 us (31%)
  starting transfers between devices  20.3 us (6%)
  local copies, waits for them, and re-layouts  11.8 us (3%)
  other arithmetic  10.6 us (3%)
    ppermute x24, waiting for transfers between devices, swap(): return lax.ppermute(x, 'dap', [(i, i ^ bit) for i in range(8)])  106 us
    pallas_call x8, Pallas kernels, triangles(): pl.pallas_call(functools.partial(triangle_kernel, layer, static, len(a_po...  101 us
    pallas_call x9, Pallas kernels, project(): pl.pallas_call(functools.partial(project_kernel, layer, sides, team, [(n,...  93.1 us
    ppermute x24, starting transfers between devices, swap(): return lax.ppermute(x, 'dap', [(i, i ^ bit) for i in range(8)])  20.3 us
  transfers between devices with their start and end apart: 24, of which 8 were waited for; matrix products, arithmetic and copies ran while one was open for 3% of the time, Pallas kernels for 52%

profile of v4, /device:TPU:0, one launch (start us, length us, event | category | flops | bytes accessed | tf_op | source)
XLA Modules:
  0.0 343.2 jit_solution(6979193105105332290)
XLA Ops:
  0.0 0.6 add_convert_fusion.refs_7_.refs_5_.refs_12_.refs_9_.refs_13_
  0.6 0.7 fusion.refs_8_.refs_4_.refs_12_.refs_6_
  1.3 0.7 constant_dynamic-update-slice_fusion.4
  2.0 1.1 copy.15
  3.1 0.7 multiply_bitcast_fusion.refs_6_.refs_11_
  3.8 1.5 convert_element_type.97.refs_4_
  5.3 0.7 constant_dynamic-update-slice_fusion.3
  6.0 0.7 constant_dynamic-update-slice_fusion.2
  6.7 0.7 constant_dynamic-update-slice_fusion.1
  7.3 0.7 constant_dynamic-update-slice_fusion
  8.0 1.3 broadcast_in_dim.2.refs_5_.refs_8_.refs_10_.refs_12_.refs_16_
  9.3 14.8 %project.9 = (bf16[128,48,384]{2,1,0:T(8,128)(2,1)}, bf16[128,48,384]{2,1,0:T(8,128)(2,1)}) custom-call(bf16[48,4,96,128]{3,2,1,0:T(8,128)(2,1)} %bitcast.10, bf16[48,4,96,128]{3,2,1,0:T(8,128)(2,1)} %bitcast.11, bf16[48,4,96,128]{3,2,1,0:T(8,128)(2,1)} %bitcast.12, bf16[48,4,96,128]{3,2,1,0:T(8,128)(2,1)} %bitcast.13, ...), custom_call_target="tpu_custom_call" | custom-call | flops 2415919104 | bytes 14155776 | tf_op jit(solution)/shard_map/project/pallas_call | solution.py:149
  24.1 0.9 collective-permute-start
  25.0 2.5 collective-permute-start.3
  27.5 2.7 slice.30
  30.3 2.0 collective-permute-start.2
  32.3 4.0 %fusion.1 = (bf16[16,4,96,128]{3,2,1,0:T(8,128)(2,1)}, bf16[16,4,96,128]{3,2,1,0:T(8,128)(2,1)}) fusion(bf16[48,4,96,128]{3,2,1,0:T(8,128)(2,1)} %bitcast.14), kind=kLoop, calls=%fused_computation.19 | loop fusion | bytes 6291456 | tf_op jit(solution)/shard_map/slice | solution.py:351
  36.3 1.5 collective-permute-start.5
  37.8 0.5 collective-permute-start.6
  38.3 0.6 pad_maximum_fusion.1.refs_9_.refs_13_.refs_17_.refs_11_
  38.9 0.6 broadcast_multiply_fusion.refs_7_.refs_11_.refs_15_.refs_9_
  39.6 1.5 collective-permute-start.4
  41.1 10.4 %triangle.8.refs_13_.refs_0_.refs_9_ = bf16[48,1,96,128]{3,2,1,0:T(8,128)(2,1)} custom-call(s32[1]{0:T(128)} %bitcast.where_ref, bf16[128,48,384]{2,1,0:T(8,128)(2,1)} %get-tuple-element.23.refs_0_.refs_10_, bf16[128,48,384]{2,1,0:T(8,128)(2,1)} %get-tuple-element.24.refs_1_.refs_2_, bf16[128,48,384]{2,1,0:T(8,128)(2,1)} %collective-permute-done.refs_2_.refs_3_, ...), custom_call_target="tpu_custom_call" | custom-call | flops 1061683200 | bytes 14155776 | tf_op jit(solution)/shard_map/triangle/pallas_call | solution.py:312
  51.5 50.1 %collective-permute-done.4.refs_9_.refs_4_ = bf16[48,384]{1,0:T(8,128)(2,1)} collective-permute-done((bf16[48,384]{1,0:T(8,128)(2,1)}, bf16[48,384]{1,0:T(8,128)(2,1)}, u32[]{:S(2)}, u32[]{:S(2)}) %collective-permute-start.4) | collective-permute-done | bytes 36896 | tf_op jit(solution)/shard_map/ppermute | solution.py:342
  101.6 1.7 collective-permute-start.8
  103.3 10.9 %project.10 = (bf16[128,32,384]{2,1,0:T(8,128)(2,1)}, bf16[128,32,384]{2,1,0:T(8,128)(2,1)}) custom-call(bf16[16,4,96,128]{3,2,1,0:T(8,128)(2,1)} %collective-permute-done.1.refs_0_.refs_1_.refs_2_.refs_3_.refs_4_.refs_9_, bf16[16,4,96,128]{3,2,1,0:T(8,128)(2,1)} %collective-permute-done.1.refs_0_.refs_1_.refs_2_.refs_3_.refs_4_.refs_9_, ...), custom_call_target="tpu_custom_call" | custom-call | flops 1610612736 | bytes 9437184 | tf_op jit(solution)/shard_map/project/pallas_call | solution.py:149
  114.3 10.9 %project.11 = (bf16[128,32,384]{2,1,0:T(8,128)(2,1)}, bf16[128,32,384]{2,1,0:T(8,128)(2,1)}) custom-call(bf16[16,4,96,128]{3,2,1,0:T(8,128)(2,1)} %collective-permute-done.5.refs_0_.refs_1_.refs_2_.refs_3_.refs_5_.refs_10_, bf16[16,4,96,128]{3,2,1,0:T(8,128)(2,1)} %collective-permute-done.5.refs_0_.refs_1_.refs_2_.refs_3_.refs_5_.refs_10_, ...), custom_call_target="tpu_custom_call" | custom-call | flops 1610612736 | bytes 9437184 | tf_op jit(solution)/shard_map/project/pallas_call | solution.py:149
  125.2 0.5 collective-permute-start.9
  125.7 1.5 collective-permute-start.7
  127.2 0.8 pad_maximum_fusion
  128.1 0.1 fusion.3
  128.1 0.9 maximum_select_fusion
  129.1 0.1 fusion.2
  129.2 0.8 maximum_select_fusion.1.refs_15_.refs_4_
  129.9 12.4 %triangle.9 = (bf16[48,1,96,128]{3,2,1,0:T(8,128)(2,1)}, bf16[48,1,96,128]{3,2,1,0:T(8,128)(2,1)}) custom-call(s32[1]{0:T(128)} %bitcast.where_ref, bf16[128,32,384]{2,1,0:T(8,128)(2,1)} %get-tuple-element.26.refs_13_.refs_0_, bf16[128,32,384]{2,1,0:T(8,128)(2,1)} %get-tuple-element.28.refs_1_.refs_14_, ...), custom_call_target="tpu_custom_call" | custom-call | flops 1415577600 | bytes 15728640 | tf_op jit(solution)/shard_map/triangle/pallas_call | solution.py:312
  142.3 6.8 %project.12 = (bf16[128,16,384]{2,1,0:T(8,128)(2,1)}, bf16[128,16,384]{2,1,0:T(8,128)(2,1)}) custom-call(bf16[16,4,96,128]{3,2,1,0:T(8,128)(2,1)} %collective-permute-done.8.refs_0_.refs_1_.refs_2_.refs_3_.refs_5_, bf16[16,4,96,128]{3,2,1,0:T(8,128)(2,1)} %collective-permute-done.8.refs_0_.refs_1_.refs_2_.refs_3_.refs_5_, ...), custom_call_target="tpu_custom_call" | custom-call | flops 805306368 | bytes 4718592 | tf_op jit(solution)/shard_map/project/pallas_call | solution.py:149
  149.2 13.2 %collective-permute-done.7.refs_0_.refs_1_.refs_2_.refs_3_.refs_11_.refs_4_ = bf16[16,4,96,128]{3,2,1,0:T(8,128)(2,1)} collective-permute-done((bf16[16,4,96,128]{3,2,1,0:T(8,128)(2,1)}, bf16[16,4,96,128]{3,2,1,0:T(8,128)(2,1)}, u32[]{:S(2)}, u32[]{:S(2)}) %collective-permute-start.7) | collective-permute-done | bytes 1572896 | tf_op jit(solution)/shard_map/ppermute | solution.py:342
  162.4 7.1 %project.13 = (bf16[128,16,384]{2,1,0:T(8,128)(2,1)}, bf16[128,16,384]{2,1,0:T(8,128)(2,1)}) custom-call(bf16[16,4,96,128]{3,2,1,0:T(8,128)(2,1)} %collective-permute-done.7.refs_0_.refs_1_.refs_2_.refs_3_.refs_11_.refs_4_, bf16[16,4,96,128]{3,2,1,0:T(8,128)(2,1)} %collective-permute-done.7.refs_0_.refs_1_.refs_2_.refs_3_.refs_11_.refs_4_, ...), custom_call_target="tpu_custom_call" | custom-call | flops 805306368 | bytes 4718592 | tf_op jit(solution)/shard_map/project/pallas_call | solution.py:149
  169.6 11.0 %triangle.10.refs_14_.refs_2_.refs_5_ = bf16[48,1,96,128]{3,2,1,0:T(8,128)(2,1)} custom-call(s32[1]{0:T(128)} %bitcast.where_ref, bf16[128,32,384]{2,1,0:T(8,128)(2,1)} %get-tuple-element.26.refs_13_.refs_0_, bf16[128,32,384]{2,1,0:T(8,128)(2,1)} %get-tuple-element.28.refs_1_.refs_14_, bf16[128,16,384]{2,1,0:T(8,128)(2,1)} %get-tuple-element.32.refs_2_.refs_18_.refs_0_, ...), custom_call_target="tpu_custom_call" | custom-call | flops 1061683200 | bytes 14155776 | tf_op jit(solution)/shard_map/triangle/pallas_call | solution.py:312
  180.6 1.5 collective-permute-start.13
  182.1 0.5 collective-permute-start.15
  182.6 10.7 %triangle.11.refs_14_.refs_1_.refs_10_ = bf16[48,1,96,128]{3,2,1,0:T(8,128)(2,1)} custom-call(s32[1]{0:T(128)} %bitcast.where_ref, bf16[128,48,384]{2,1,0:T(8,128)(2,1)} %get-tuple-element.23.refs_0_.refs_10_, bf16[128,32,384]{2,1,0:T(8,128)(2,1)} %get-tuple-element.25.refs_3_.refs_1_, bf16[128,32,384]{2,1,0:T(8,128)(2,1)} %get-tuple-element.27.refs_4_.refs_2_, ...), custom_call_target="tpu_custom_call" | custom-call | flops 1061683200 | bytes 14155776 | tf_op jit(solution)/shard_map/triangle/pallas_call | solution.py:312
  193.3 10.8 %triangle.12.refs_12_.refs_2_.refs_11_ = bf16[48,1,96,128]{3,2,1,0:T(8,128)(2,1)} custom-call(s32[1]{0:T(128)} %bitcast.where_ref, bf16[128,48,384]{2,1,0:T(8,128)(2,1)} %get-tuple-element.23.refs_0_.refs_10_, bf16[128,32,384]{2,1,0:T(8,128)(2,1)} %get-tuple-element.25.refs_3_.refs_1_, bf16[128,32,384]{2,1,0:T(8,128)(2,1)} %get-tuple-element.27.refs_4_.refs_2_, ...), custom_call_target="tpu_custom_call" | custom-call | flops 1061683200 | bytes 14155776 | tf_op jit(solution)/shard_map/triangle/pallas_call | solution.py:312
  204.1 1.5 collective-permute-start.16
  205.6 0.5 collective-permute-start.19
  206.1 1.5 collective-permute-start.20
  207.6 2.1 collective-permute-done.13.refs_3_
  209.7 0.3 collective-permute-start.18
  210.1 8.9 %triangle.13 = (bf16[48,1,96,128]{3,2,1,0:T(8,128)(2,1)}, bf16[48,1,96,128]{3,2,1,0:T(8,128)(2,1)}) custom-call(s32[1]{0:T(128)} %bitcast.where_ref, bf16[128,16,384]{2,1,0:T(8,128)(2,1)} %get-tuple-element.32.refs_2_.refs_18_.refs_0_, bf16[128,16,384]{2,1,0:T(8,128)(2,1)} %get-tuple-element.30.refs_8_.refs_1_, ...), custom_call_target="tpu_custom_call", output_to_operand_aliasing={{0}: (14, {}), {1}: (15, {})} | custom-call | flops 707788800 | bytes 12582912 | tf_op jit(solution)/shard_map/triangle/pallas_call | solution.py:312
  218.9 14.4 %project.14 = (bf16[128,48,384]{2,1,0:T(8,128)(2,1)}, bf16[128,48,384]{2,1,0:T(8,128)(2,1)}) custom-call(bf16[48,1,96,128]{3,2,1,0:T(8,128)(2,1)} %triangle.8.refs_13_.refs_0_.refs_9_, bf16[48,1,96,128]{3,2,1,0:T(8,128)(2,1)} %triangle.11.refs_14_.refs_1_.refs_10_, bf16[48,1,96,128]{3,2,1,0:T(8,128)(2,1)} %triangle.12.refs_12_.refs_2_.refs_11_, ...), custom_call_target="tpu_custom_call" | custom-call | flops 2415919104 | bytes 14155776 | tf_op jit(solution)/shard_map/project/pallas_call | solution.py:149
  233.3 1.7 collective-permute-done.15.refs_1_
  235.0 24.8 %collective-permute-done.16.refs_3_ = bf16[48,1,96,128]{3,2,1,0:T(8,128)(2,1)} collective-permute-done((bf16[48,1,96,128]{3,2,1,0:T(8,128)(2,1)}, bf16[48,1,96,128]{3,2,1,0:T(8,128)(2,1)}, u32[]{:S(2)}, u32[]{:S(2)}) %collective-permute-start.16) | collective-permute-done | bytes 1179680 | tf_op jit(solution)/shard_map/ppermute | solution.py:342
  259.8 14.4 %project.15 = (bf16[128,48,384]{2,1,0:T(8,128)(2,1)}, bf16[128,48,384]{2,1,0:T(8,128)(2,1)}) custom-call(bf16[48,1,96,128]{3,2,1,0:T(8,128)(2,1)} %get-tuple-element.35.refs_8_.refs_0_, bf16[48,1,96,128]{3,2,1,0:T(8,128)(2,1)} %collective-permute-done.15.refs_1_, bf16[48,1,96,128]{3,2,1,0:T(8,128)(2,1)} %triangle.10.refs_14_.refs_2_.refs_5_, ...), custom_call_target="tpu_custom_call" | custom-call | flops 2415919104 | bytes 14155776 | tf_op jit(solution)/shard_map/project/pallas_call | solution.py:149
  274.2 0.5 collective-permute-start.14
  274.7 9.3 %collective-permute-done.18.refs_1_ = bf16[48,1,96,128]{3,2,1,0:T(8,128)(2,1)} collective-permute-done((bf16[48,1,96,128]{3,2,1,0:T(8,128)(2,1)}, bf16[48,1,96,128]{3,2,1,0:T(8,128)(2,1)}, u32[]{:S(2)}, u32[]{:S(2)}) %collective-permute-start.18) | collective-permute-done | bytes 1179680 | tf_op jit(solution)/shard_map/ppermute | solution.py:342
  284.0 8.3 %project.16.refs_8_.refs_1_.refs_5_ = bf16[128,32,384]{2,1,0:T(8,128)(2,1)} custom-call(bf16[48,1,96,128]{3,2,1,0:T(8,128)(2,1)} %get-tuple-element.39.refs_0_, bf16[48,1,96,128]{3,2,1,0:T(8,128)(2,1)} %collective-permute-done.18.refs_1_, bf16[48,1,96,128]{3,2,1,0:T(8,128)(2,1)} %collective-permute-done.19.refs_2_, ...), custom_call_target="tpu_custom_call" | custom-call | flops 805306368 | bytes 6291456 | tf_op jit(solution)/shard_map/project/pallas_call | solution.py:149
  292.3 5.4 %project.17.refs_2_.refs_12_.refs_6_ = bf16[128,16,384]{2,1,0:T(8,128)(2,1)} custom-call(bf16[48,1,96,128]{3,2,1,0:T(8,128)(2,1)} %get-tuple-element.39.refs_0_, bf16[48,1,96,128]{3,2,1,0:T(8,128)(2,1)} %collective-permute-done.18.refs_1_, bf16[48,1,96,128]{3,2,1,0:T(8,128)(2,1)} %collective-permute-done.19.refs_2_, ...), custom_call_target="tpu_custom_call" | custom-call | flops 402653184 | bytes 3145728 | tf_op jit(solution)/shard_map/project/pallas_call | solution.py:149
  297.8 0.5 collective-permute-start.22
  298.3 3.4 collective-permute-done.22.refs_4_.refs_8_
  301.7 10.5 %triangle.14.refs_18_ = bf16[48,1,96,128]{3,2,1,0:T(8,128)(2,1)} custom-call(s32[1]{0:T(128)} %bitcast.where_ref, bf16[128,48,384]{2,1,0:T(8,128)(2,1)} %get-tuple-element.40.refs_8_.refs_0_, bf16[128,32,384]{2,1,0:T(8,128)(2,1)} %project.16.refs_8_.refs_1_.refs_5_, bf16[128,16,384]{2,1,0:T(8,128)(2,1)} %project.17.refs_2_.refs_12_.refs_6_, ...), custom_call_target="tpu_custom_call" | custom-call | flops 1061683200 | bytes 14155776 | tf_op jit(solution)/shard_map/triangle/pallas_call | solution.py:312
  312.2 0.5 collective-permute-start.23
  312.7 27.0 %triangle.15 = bf16[48,4,96,128]{3,2,1,0:T(8,128)(2,1)} custom-call(s32[1]{0:T(128)} %bitcast.where_ref, bf16[128,48,384]{2,1,0:T(8,128)(2,1)} %get-tuple-element.36.refs_8_.refs_0_, bf16[128,48,384]{2,1,0:T(8,128)(2,1)} %get-tuple-element.37.refs_1_, bf16[128,48,384]{2,1,0:T(8,128)(2,1)} %collective-permute-done.14.refs_2_, ...), custom_call_target="tpu_custom_call" | custom-call | flops 3185049600 | bytes 23592960 | tf_op jit(solution)/shard_map/triangle/pallas_call | solution.py:312
  339.7 1.1 collective-permute-done.23
  340.7 2.5 constant_dynamic-update-slice_fusion.5
  (37 shorter events, 0.3 us)
Async XLA Ops:
  24.1 15.5 %collective-permute-start = (bf16[128,48,384]{2,1,0:T(8,128)(2,1)}, bf16[128,48,384]{2,1,0:T(8,128)(2,1)}, u32[]{:S(2)}, u32[]{:S(2)}) collective-permute-start(bf16[128,48,384]{2,1,0:T(8,128)(2,1)} %get-tuple-element.24.refs_1_.refs_2_), channel_id=1, source_target_pairs={{0,1},{1,0},{2,3},{3,2},{4,5},{5,4},{6,7},{7,6}} | collective-permute-start | bytes 14155784 | tf_op jit(solution)/shard_map/ppermute | solution.py:342
  25.0 12.8 %collective-permute-start.3 = (bf16[48,384]{1,0:T(8,128)(2,1)}, bf16[48,384]{1,0:T(8,128)(2,1)}, u32[]{:S(2)}, u32[]{:S(2)}) collective-permute-start(bf16[48,384]{1,0:T(8,128)(2,1)} %convert_element_type.97.refs_4_), channel_id=1, source_target_pairs={{0,2},{1,3},{2,0},{3,1},{4,6},{5,7},{6,4},{7,5}} | collective-permute-start | bytes 110600 | tf_op jit(solution)/shard_map/ppermute | solution.py:342
  30.2 8.1 %copy-start.1 = (bf16[2,128]{1,0:T(2,128)(2,1)S(1)}, bf16[2,128]{1,0:T(2,128)(2,1)}, u32[]{:S(2)}) copy-start(bf16[2,128]{1,0:T(2,128)(2,1)} %param.14) | copy-start | bytes 1540
  30.2 8.1 %copy-start.2 = (bf16[2,128]{1,0:T(2,128)(2,1)S(1)}, bf16[2,128]{1,0:T(2,128)(2,1)}, u32[]{:S(2)}) copy-start(bf16[2,128]{1,0:T(2,128)(2,1)} %param.15) | copy-start | bytes 1540
  30.2 8.1 %copy-start.3 = (bf16[2,128]{1,0:T(2,128)(2,1)S(1)}, bf16[2,128]{1,0:T(2,128)(2,1)}, u32[]{:S(2)}) copy-start(bf16[2,128]{1,0:T(2,128)(2,1)} %param.23) | copy-start | bytes 1540
  30.2 8.1 %copy-start.4 = (bf16[2,128]{1,0:T(2,128)(2,1)S(1)}, bf16[2,128]{1,0:T(2,128)(2,1)}, u32[]{:S(2)}) copy-start(bf16[2,128]{1,0:T(2,128)(2,1)} %param.19) | copy-start | bytes 1540
  30.2 8.7 %copy-start = (bf16[2,128,128]{2,1,0:T(8,128)(2,1)S(1)}, bf16[2,128,128]{2,1,0:T(8,128)(2,1)}, u32[]{:S(2)}) copy-start(bf16[2,128,128]{2,1,0:T(8,128)(2,1)} %param.18) | copy-start | bytes 196612
  30.2 73.1 %collective-permute-start.1 = (bf16[16,4,96,128]{3,2,1,0:T(8,128)(2,1)}, bf16[16,4,96,128]{3,2,1,0:T(8,128)(2,1)}, u32[]{:S(2)}, u32[]{:S(2)}) collective-permute-start(bf16[16,4,96,128]{3,2,1,0:T(8,128)(2,1)} %bitcast.7), channel_id=1, source_target_pairs={{0,2},{1,3},{2,0},{3,1},{4,6},{5,7},{6,4},{7,5}} | collective-permute-start | bytes 4718600 | tf_op jit(solution)/shard_map/ppermute | solution.py:342
  30.3 73.1 %collective-permute-start.2 = (bf16[16,4,96,128]{3,2,1,0:T(8,128)(2,1)}, bf16[16,4,96,128]{3,2,1,0:T(8,128)(2,1)}, u32[]{:S(2)}, u32[]{:S(2)}) collective-permute-start(bf16[16,4,96,128]{3,2,1,0:T(8,128)(2,1)} %bitcast.7), channel_id=1, source_target_pairs={{0,4},{1,5},{2,6},{3,7},{4,0},{5,1},{6,2},{7,3}} | collective-permute-start | bytes 4718600 | tf_op jit(solution)/shard_map/ppermute | solution.py:342
  36.3 78.0 %collective-permute-start.5 = (bf16[16,4,96,128]{3,2,1,0:T(8,128)(2,1)}, bf16[16,4,96,128]{3,2,1,0:T(8,128)(2,1)}, u32[]{:S(2)}, u32[]{:S(2)}) collective-permute-start(bf16[16,4,96,128]{3,2,1,0:T(8,128)(2,1)} %get-tuple-element.42), channel_id=1, source_target_pairs={{0,2},{1,3},{2,0},{3,1},{4,6},{5,7},{6,4},{7,5}} | collective-permute-start | bytes 4718600 | tf_op jit(solution)/shard_map/ppermute | solution.py:342
  37.8 76.5 %collective-permute-start.6 = (bf16[16,4,96,128]{3,2,1,0:T(8,128)(2,1)}, bf16[16,4,96,128]{3,2,1,0:T(8,128)(2,1)}, u32[]{:S(2)}, u32[]{:S(2)}) collective-permute-start(bf16[16,4,96,128]{3,2,1,0:T(8,128)(2,1)} %get-tuple-element.42), channel_id=1, source_target_pairs={{0,4},{1,5},{2,6},{3,7},{4,0},{5,1},{6,2},{7,3}} | collective-permute-start | bytes 4718600 | tf_op jit(solution)/shard_map/ppermute | solution.py:342
  39.6 62.0 %collective-permute-start.4 = (bf16[48,384]{1,0:T(8,128)(2,1)}, bf16[48,384]{1,0:T(8,128)(2,1)}, u32[]{:S(2)}, u32[]{:S(2)}) collective-permute-start(bf16[48,384]{1,0:T(8,128)(2,1)} %convert_element_type.97.refs_4_), channel_id=1, source_target_pairs={{0,4},{1,5},{2,6},{3,7},{4,0},{5,1},{6,2},{7,3}} | collective-permute-start | bytes 110600 | tf_op jit(solution)/shard_map/ppermute | solution.py:342
  101.6 40.7 %collective-permute-start.8 = (bf16[16,4,96,128]{3,2,1,0:T(8,128)(2,1)}, bf16[16,4,96,128]{3,2,1,0:T(8,128)(2,1)}, u32[]{:S(2)}, u32[]{:S(2)}) collective-permute-start(bf16[16,4,96,128]{3,2,1,0:T(8,128)(2,1)} %get-tuple-element.41), channel_id=1, source_target_pairs={{0,4},{1,5},{2,6},{3,7},{4,0},{5,1},{6,2},{7,3}} | collective-permute-start | bytes 4718600 | tf_op jit(solution)/shard_map/ppermute | solution.py:342
  125.2 44.4 %collective-permute-start.10 = (bf16[128,32,384]{2,1,0:T(8,128)(2,1)}, bf16[128,32,384]{2,1,0:T(8,128)(2,1)}, u32[]{:S(2)}, u32[]{:S(2)}) collective-permute-start(bf16[128,32,384]{2,1,0:T(8,128)(2,1)} %get-tuple-element.27.refs_4_.refs_2_), channel_id=1, source_target_pairs={{0,1},{1,0},{2,3},{3,2},{4,5},{5,4},{6,7},{7,6}} | collective-permute-start | bytes 9437192 | tf_op jit(solution)/shard_map/ppermute | solution.py:342
  125.2 44.3 %collective-permute-start.9 = (bf16[128,32,384]{2,1,0:T(8,128)(2,1)}, bf16[128,32,384]{2,1,0:T(8,128)(2,1)}, u32[]{:S(2)}, u32[]{:S(2)}) collective-permute-start(bf16[128,32,384]{2,1,0:T(8,128)(2,1)} %get-tuple-element.25.refs_3_.refs_1_), channel_id=1, source_target_pairs={{0,1},{1,0},{2,3},{3,2},{4,5},{5,4},{6,7},{7,6}} | collective-permute-start | bytes 9437192 | tf_op jit(solution)/shard_map/ppermute | solution.py:342
  125.7 36.7 %collective-permute-start.7 = (bf16[16,4,96,128]{3,2,1,0:T(8,128)(2,1)}, bf16[16,4,96,128]{3,2,1,0:T(8,128)(2,1)}, u32[]{:S(2)}, u32[]{:S(2)}) collective-permute-start(bf16[16,4,96,128]{3,2,1,0:T(8,128)(2,1)} %get-tuple-element.41), channel_id=1, source_target_pairs={{0,2},{1,3},{2,0},{3,1},{4,6},{5,7},{6,4},{7,5}} | collective-permute-start | bytes 4718600 | tf_op jit(solution)/shard_map/ppermute | solution.py:342
  149.2 20.4 %collective-permute-start.12 = (bf16[128,16,384]{2,1,0:T(8,128)(2,1)}, bf16[128,16,384]{2,1,0:T(8,128)(2,1)}, u32[]{:S(2)}, u32[]{:S(2)}) collective-permute-start(bf16[128,16,384]{2,1,0:T(8,128)(2,1)} %get-tuple-element.33.refs_5_.refs_3_), channel_id=1, source_target_pairs={{0,1},{1,0},{2,3},{3,2},{4,5},{5,4},{6,7},{7,6}} | collective-permute-start | bytes 4718600 | tf_op jit(solution)/shard_map/ppermute | solution.py:342
  169.5 13.1 %collective-permute-start.11 = (bf16[128,16,384]{2,1,0:T(8,128)(2,1)}, bf16[128,16,384]{2,1,0:T(8,128)(2,1)}, u32[]{:S(2)}, u32[]{:S(2)}) collective-permute-start(bf16[128,16,384]{2,1,0:T(8,128)(2,1)} %get-tuple-element.31.refs_3_), channel_id=1, source_target_pairs={{0,1},{1,0},{2,3},{3,2},{4,5},{5,4},{6,7},{7,6}} | collective-permute-start | bytes 4718600 | tf_op jit(solution)/shard_map/ppermute | solution.py:342
  180.6 29.2 %collective-permute-start.13 = (bf16[48,1,96,128]{3,2,1,0:T(8,128)(2,1)}, bf16[48,1,96,128]{3,2,1,0:T(8,128)(2,1)}, u32[]{:S(2)}, u32[]{:S(2)}) collective-permute-start(bf16[48,1,96,128]{3,2,1,0:T(8,128)(2,1)} %triangle.10.refs_14_.refs_2_.refs_5_), channel_id=1, source_target_pairs={{0,2},{1,3},{2,0},{3,1},{4,6},{5,7},{6,4},{7,5}} | collective-permute-start | bytes 3538952 | tf_op jit(solution)/shard_map/ppermute | solution.py:342
  182.1 52.9 %collective-permute-start.15 = (bf16[48,1,96,128]{3,2,1,0:T(8,128)(2,1)}, bf16[48,1,96,128]{3,2,1,0:T(8,128)(2,1)}, u32[]{:S(2)}, u32[]{:S(2)}) collective-permute-start(bf16[48,1,96,128]{3,2,1,0:T(8,128)(2,1)} %triangle.8.refs_13_.refs_0_.refs_9_), channel_id=1, source_target_pairs={{0,2},{1,3},{2,0},{3,1},{4,6},{5,7},{6,4},{7,5}} | collective-permute-start | bytes 3538952 | tf_op jit(solution)/shard_map/ppermute | solution.py:342
  204.1 55.7 %collective-permute-start.16 = (bf16[48,1,96,128]{3,2,1,0:T(8,128)(2,1)}, bf16[48,1,96,128]{3,2,1,0:T(8,128)(2,1)}, u32[]{:S(2)}, u32[]{:S(2)}) collective-permute-start(bf16[48,1,96,128]{3,2,1,0:T(8,128)(2,1)} %triangle.12.refs_12_.refs_2_.refs_11_), channel_id=1, source_target_pairs={{0,2},{1,3},{2,0},{3,1},{4,6},{5,7},{6,4},{7,5}} | collective-permute-start | bytes 3538952 | tf_op jit(solution)/shard_map/ppermute | solution.py:342
  205.6 69.1 %collective-permute-start.19 = (bf16[48,1,96,128]{3,2,1,0:T(8,128)(2,1)}, bf16[48,1,96,128]{3,2,1,0:T(8,128)(2,1)}, u32[]{:S(2)}, u32[]{:S(2)}) collective-permute-start(bf16[48,1,96,128]{3,2,1,0:T(8,128)(2,1)} %triangle.8.refs_13_.refs_0_.refs_9_), channel_id=1, source_target_pairs={{0,4},{1,5},{2,6},{3,7},{4,0},{5,1},{6,2},{7,3}} | collective-permute-start | bytes 3538952 | tf_op jit(solution)/shard_map/ppermute | solution.py:342
  206.1 68.6 %collective-permute-start.20 = (bf16[48,1,96,128]{3,2,1,0:T(8,128)(2,1)}, bf16[48,1,96,128]{3,2,1,0:T(8,128)(2,1)}, u32[]{:S(2)}, u32[]{:S(2)}) collective-permute-start(bf16[48,1,96,128]{3,2,1,0:T(8,128)(2,1)} %triangle.11.refs_14_.refs_1_.refs_10_), channel_id=1, source_target_pairs={{0,4},{1,5},{2,6},{3,7},{4,0},{5,1},{6,2},{7,3}} | collective-permute-start | bytes 3538952 | tf_op jit(solution)/shard_map/ppermute | solution.py:342
  209.7 74.2 %collective-permute-start.18 = (bf16[48,1,96,128]{3,2,1,0:T(8,128)(2,1)}, bf16[48,1,96,128]{3,2,1,0:T(8,128)(2,1)}, u32[]{:S(2)}, u32[]{:S(2)}) collective-permute-start(bf16[48,1,96,128]{3,2,1,0:T(8,128)(2,1)} %collective-permute-done.13.refs_3_), channel_id=1, source_target_pairs={{0,4},{1,5},{2,6},{3,7},{4,0},{5,1},{6,2},{7,3}} | collective-permute-start | bytes 3538952 | tf_op jit(solution)/shard_map/ppermute | solution.py:342
  274.2 38.5 %collective-permute-start.17 = (bf16[128,48,384]{2,1,0:T(8,128)(2,1)}, bf16[128,48,384]{2,1,0:T(8,128)(2,1)}, u32[]{:S(2)}, u32[]{:S(2)}) collective-permute-start(bf16[128,48,384]{2,1,0:T(8,128)(2,1)} %get-tuple-element.38.refs_3_), channel_id=1, source_target_pairs={{0,1},{1,0},{2,3},{3,2},{4,5},{5,4},{6,7},{7,6}} | collective-permute-start | bytes 14155784 | tf_op jit(solution)/shard_map/ppermute | solution.py:342
  274.2 38.5 %collective-permute-start.14 = (bf16[128,48,384]{2,1,0:T(8,128)(2,1)}, bf16[128,48,384]{2,1,0:T(8,128)(2,1)}, u32[]{:S(2)}, u32[]{:S(2)}) collective-permute-start(bf16[128,48,384]{2,1,0:T(8,128)(2,1)} %get-tuple-element.37.refs_1_), channel_id=1, source_target_pairs={{0,1},{1,0},{2,3},{3,2},{4,5},{5,4},{6,7},{7,6}} | collective-permute-start | bytes 14155784 | tf_op jit(solution)/shard_map/ppermute | solution.py:342
  292.3 9.4 %collective-permute-start.21 = (bf16[128,32,384]{2,1,0:T(8,128)(2,1)}, bf16[128,32,384]{2,1,0:T(8,128)(2,1)}, u32[]{:S(2)}, u32[]{:S(2)}) collective-permute-start(bf16[128,32,384]{2,1,0:T(8,128)(2,1)} %project.16.refs_8_.refs_1_.refs_5_), channel_id=1, source_target_pairs={{0,1},{1,0},{2,3},{3,2},{4,5},{5,4},{6,7},{7,6}} | collective-permute-start | bytes 9437192 | tf_op jit(solution)/shard_map/ppermute | solution.py:342
  297.8 3.9 %collective-permute-start.22 = (bf16[128,16,384]{2,1,0:T(8,128)(2,1)}, bf16[128,16,384]{2,1,0:T(8,128)(2,1)}, u32[]{:S(2)}, u32[]{:S(2)}) collective-permute-start(bf16[128,16,384]{2,1,0:T(8,128)(2,1)} %project.17.refs_2_.refs_12_.refs_6_), channel_id=1, source_target_pairs={{0,1},{1,0},{2,3},{3,2},{4,5},{5,4},{6,7},{7,6}} | collective-permute-start | bytes 4718600 | tf_op jit(solution)/shard_map/ppermute | solution.py:342
  312.2 28.6 %collective-permute-start.23 = (bf16[48,1,96,128]{3,2,1,0:T(8,128)(2,1)}, bf16[48,1,96,128]{3,2,1,0:T(8,128)(2,1)}, u32[]{:S(2)}, u32[]{:S(2)}) collective-permute-start(bf16[48,1,96,128]{3,2,1,0:T(8,128)(2,1)} %triangle.14.refs_18_), channel_id=1, source_target_pairs={{0,2},{1,3},{2,0},{3,1},{4,6},{5,7},{6,4},{7,5}} | collective-permute-start | bytes 3538952 | tf_op jit(solution)/shard_map/ppermute | solution.py:342

commit v5 on v4

--- a/solution.py
+++ b/solution.py
@@ -162,7 +162,7 @@
     )(*[tile[0] for _, tiles, _, _ in sources for tile in tiles], *[mask for _, _, mask, _ in sources], vectors, w_t, centre, dep)
 
 
-def triangle_kernel(layer, jobs, n_a, n_b, n_z, n_out, n_held, where_ref, *refs):
+def triangle_kernel(layer, chunk, jobs, n_a, n_b, n_z, n_out, n_held, where_ref, *refs):
     a_refs, refs = refs[:n_a], refs[n_a:]
     b_refs, refs = refs[:n_b], refs[n_b:]
     z_refs, refs = refs[:n_z], refs[n_z:]
@@ -191,7 +191,7 @@
 
     def loads(j, q):
         pieces, b_pieces, _ = jobs[j]
-        chans = pl.ds(pl.multiple_of(q * CHUNK, CHUNK), CHUNK)
+        chans = pl.ds(pl.multiple_of(q * chunk, chunk), chunk)
         copies, r0 = [], a_at[j]
         for n, (_, a, blk, count, _, _) in enumerate(pieces if loads_a[j] else ()):
             copies.append(pltpu.make_async_copy(a_refs[a].at[chans, blk * count:blk * count + count], abuf.at[chans, r0:r0 + count], load_sem.at[j, q, n]))
@@ -215,7 +215,7 @@
                 copy.start()
             return carry
 
-        lax.fori_loop(0, CH // CHUNK, start_loads, 0)
+        lax.fori_loop(0, CH // chunk, start_loads, 0)
         for copy in z_loads(j) + (params if j == 0 else []):
             copy.start()
     tri[:, 96:CH] = jnp.zeros((tri.shape[0], 32), jnp.float32)
@@ -245,13 +245,13 @@
         def some_channels(q, carry, j=j, rows=rows):
             for copy in loads(j, q):
                 copy.wait()
-            for cc in range(CHUNK):
-                c = q * CHUNK + cc
+            for cc in range(chunk):
+                c = q * chunk + cc
                 o = lax.dot_general(bbuf[j, c], abuf[c, a_at[j]:a_at[j] + rows], NT, preferred_element_type=jnp.float32).T
                 tri[pl.ds(c, rows, stride=PITCH), 0:96] = o
             return carry
 
-        lax.fori_loop(0, CH // CHUNK, some_channels, 0)
+        lax.fori_loop(0, CH // chunk, some_channels, 0)
         for copy in z_loads(j) + (params if j == 0 else []):
             copy.wait()
 
@@ -281,7 +281,7 @@
         store(s, r0, i).wait()
 
 
-def triangles(layer, where, jobs, arrays, params, dep):
+def triangles(layer, where, jobs, arrays, params, dep, chunk=CHUNK):
     def place(arr, pool):
         for n, other in enumerate(pool):
             if other is arr:
@@ -310,7 +310,7 @@
     anywhere = pl.BlockSpec(memory_space=pl.ANY)
     in_specs = [anywhere] * (len(a_pool) + len(b_pool) + len(z_pool) + len(params) + len(deps) + len(held))
     return pl.pallas_call(
-        functools.partial(triangle_kernel, layer, static, len(a_pool), len(b_pool), len(z_pool), len(arrays), len(deps) + len(held)),
+        functools.partial(triangle_kernel, layer, chunk, static, len(a_pool), len(b_pool), len(z_pool), len(arrays), len(deps) + len(held)),
         out_shape=[jax.ShapeDtypeStruct((n, width, 96, CH), jnp.bfloat16) for n, width, _ in arrays],
         input_output_aliases=aliases,
         grid_spec=pltpu.PrefetchScalarGridSpec(
@@ -319,7 +319,7 @@
                             pltpu.VMEM((total, 96, CH), jnp.bfloat16), pltpu.VMEM((total, 96, CH), jnp.bfloat16),
                             pltpu.VMEM((96, CH), jnp.bfloat16), pltpu.VMEM((CH, CH), jnp.bfloat16), pltpu.VMEM((CH, CH), jnp.bfloat16), pltpu.VMEM((CH, CH), jnp.bfloat16),
                             pltpu.VMEM((CH, CH), jnp.float32), pltpu.VMEM((CH, CH), jnp.float32), pltpu.VMEM((4, CH), jnp.float32),
-                            pltpu.SemaphoreType.DMA((len(jobs), CH // CHUNK, most_a + most_b)), pltpu.SemaphoreType.DMA((len(z_pool),)), pltpu.SemaphoreType.DMA((7,)), pltpu.SemaphoreType.DMA((total // GROUP,))]),
+                            pltpu.SemaphoreType.DMA((len(jobs), CH // chunk, most_a + most_b)), pltpu.SemaphoreType.DMA((len(z_pool),)), pltpu.SemaphoreType.DMA((7,)), pltpu.SemaphoreType.DMA((total // GROUP,))]),
         compiler_params=pltpu.CompilerParams(dimension_semantics=('arbitrary',), vmem_limit_bytes=VMEM_BYTES),
         cost_estimate=pl.CostEstimate(flops=total * 96 * CH * 1800, bytes_accessed=(total + 96) * 384 * 256, transcendentals=0),
         name='triangle',
@@ -404,11 +404,11 @@
         x0, y0 = triangle(0, where, [[piece(2, k, 0)] for k in range(2)], own, tri, o2, [(OWN, 1, 32, None, x0), (OWN, 1, 32, None, y0)])
 
         tiles = lambda row, *arrs: [(arr, 0, row) for arr in arrs]
-        a_o, b_o = project(1, [(OWN, tiles(0, o0, o1, o2, o3), rel, 0)], vectors, w_t, centre, 2, x0, 8)
+        a_o, b_o = project(1, [(OWN, tiles(0, o0, o1, o2, o3), rel, 0)], vectors, w_t, centre, 2, x0)
         b_o2 = swap(b_o, 1)
         a_x, b_x = project(1, [(OWN, tiles(0, x0, x1, x2, x3), rel, OWN)], vectors, w_t, centre, 2, a_o, 8)
         b_x2 = swap(b_x, 1)
-        b_ya, = project(1, [(32, tiles(0, y0, y1, y2, y3), rel, 96)], vectors, w_t, centre, 1, a_x)
+        b_ya, = project(1, [(32, tiles(0, y0, y1, y2, y3), rel, 96)], vectors, w_t, centre, 1, a_x, 8)
         b_ya2 = swap(b_ya, 1)
         b_yb, = project(1, [(16, tiles(32, y0, y1, y2, y3), rel, CH)], vectors, w_t, centre, 1, b_ya)
         b_yb2 = swap(b_yb, 1)

time: 344 us -> 344 us (level)
  transfers between devices with their start and end apart: 24 -> 24, of which waited for: 8 -> 8; matrix products, arithmetic and copies ran while one was open for 3% -> 3% of each run, Pallas kernels for 52% -> 53%
where the time goes in v5:
time: 344 us; the launch traced here: 343 us
  Pallas kernels  195 us (57%)
  waiting for transfers between devices  105 us (31%)
  starting transfers between devices  20.3 us (6%)
  local copies, waits for them, and re-layouts  11.8 us (3%)
  other arithmetic  10.6 us (3%)
    ppermute x24, waiting for transfers between devices, swap(): return lax.ppermute(x, 'dap', [(i, i ^ bit) for i in range(8)])  105 us
    pallas_call x8, Pallas kernels, triangles(): pl.pallas_call(functools.partial(triangle_kernel, layer, chunk, static, l...  101 us
    pallas_call x9, Pallas kernels, project(): pl.pallas_call(functools.partial(project_kernel, layer, sides, team, [(n,...  93.6 us
    ppermute x24, starting transfers between devices, swap(): return lax.ppermute(x, 'dap', [(i, i ^ bit) for i in range(8)])  20.3 us
  transfers between devices with their start and end apart: 24, of which 8 were waited for; matrix products, arithmetic and copies ran while one was open for 3% of the time, Pallas kernels for 53%

profile of v5, /device:TPU:0, one launch (start us, length us, event | category | flops | bytes accessed | tf_op | source)
XLA Modules:
  0.0 343.0 jit_solution(9714122100179881737)
XLA Ops:
  0.0 0.6 add_convert_fusion.refs_7_.refs_5_.refs_12_.refs_9_.refs_13_
  0.6 0.7 fusion.refs_8_.refs_4_.refs_12_.refs_6_
  1.3 0.7 constant_dynamic-update-slice_fusion.4
  2.0 1.1 copy.15
  3.1 0.7 multiply_bitcast_fusion.refs_6_.refs_11_
  3.8 1.5 convert_element_type.97.refs_4_
  5.3 0.7 constant_dynamic-update-slice_fusion.3
  6.0 0.7 constant_dynamic-update-slice_fusion.2
  6.7 0.7 constant_dynamic-update-slice_fusion.1
  7.3 0.7 constant_dynamic-update-slice_fusion
  8.0 1.3 broadcast_in_dim.2.refs_5_.refs_8_.refs_10_.refs_12_.refs_16_
  9.3 14.8 %project.9 = (bf16[128,48,384]{2,1,0:T(8,128)(2,1)}, bf16[128,48,384]{2,1,0:T(8,128)(2,1)}) custom-call(bf16[48,4,96,128]{3,2,1,0:T(8,128)(2,1)} %bitcast.10, bf16[48,4,96,128]{3,2,1,0:T(8,128)(2,1)} %bitcast.11, bf16[48,4,96,128]{3,2,1,0:T(8,128)(2,1)} %bitcast.12, bf16[48,4,96,128]{3,2,1,0:T(8,128)(2,1)} %bitcast.13, ...), custom_call_target="tpu_custom_call" | custom-call | flops 2415919104 | bytes 14155776 | tf_op jit(solution)/shard_map/project/pallas_call | solution.py:149
  24.1 0.9 collective-permute-start
  25.0 2.5 collective-permute-start.3
  27.5 2.7 slice.30
  30.3 2.0 collective-permute-start.2
  32.3 4.0 %fusion.1 = (bf16[16,4,96,128]{3,2,1,0:T(8,128)(2,1)}, bf16[16,4,96,128]{3,2,1,0:T(8,128)(2,1)}) fusion(bf16[48,4,96,128]{3,2,1,0:T(8,128)(2,1)} %bitcast.14), kind=kLoop, calls=%fused_computation.19 | loop fusion | bytes 6291456 | tf_op jit(solution)/shard_map/slice | solution.py:351
  36.3 1.5 collective-permute-start.5
  37.8 0.5 collective-permute-start.6
  38.3 0.6 pad_maximum_fusion.1.refs_9_.refs_13_.refs_17_.refs_11_
  38.9 0.6 broadcast_multiply_fusion.refs_7_.refs_11_.refs_15_.refs_9_
  39.6 1.5 collective-permute-start.4
  41.1 10.4 %triangle.8.refs_13_.refs_0_.refs_9_ = bf16[48,1,96,128]{3,2,1,0:T(8,128)(2,1)} custom-call(s32[1]{0:T(128)} %bitcast.where_ref, bf16[128,48,384]{2,1,0:T(8,128)(2,1)} %get-tuple-element.23.refs_0_.refs_10_, bf16[128,48,384]{2,1,0:T(8,128)(2,1)} %get-tuple-element.24.refs_1_.refs_2_, bf16[128,48,384]{2,1,0:T(8,128)(2,1)} %collective-permute-done.refs_2_.refs_3_, ...), custom_call_target="tpu_custom_call" | custom-call | flops 1061683200 | bytes 14155776 | tf_op jit(solution)/shard_map/triangle/pallas_call | solution.py:312
  51.5 50.1 %collective-permute-done.4.refs_9_.refs_4_ = bf16[48,384]{1,0:T(8,128)(2,1)} collective-permute-done((bf16[48,384]{1,0:T(8,128)(2,1)}, bf16[48,384]{1,0:T(8,128)(2,1)}, u32[]{:S(2)}, u32[]{:S(2)}) %collective-permute-start.4) | collective-permute-done | bytes 36896 | tf_op jit(solution)/shard_map/ppermute | solution.py:342
  101.6 1.7 collective-permute-start.8
  103.3 10.9 %project.10 = (bf16[128,32,384]{2,1,0:T(8,128)(2,1)}, bf16[128,32,384]{2,1,0:T(8,128)(2,1)}) custom-call(bf16[16,4,96,128]{3,2,1,0:T(8,128)(2,1)} %collective-permute-done.1.refs_0_.refs_1_.refs_2_.refs_3_.refs_4_.refs_9_, bf16[16,4,96,128]{3,2,1,0:T(8,128)(2,1)} %collective-permute-done.1.refs_0_.refs_1_.refs_2_.refs_3_.refs_4_.refs_9_, ...), custom_call_target="tpu_custom_call" | custom-call | flops 1610612736 | bytes 9437184 | tf_op jit(solution)/shard_map/project/pallas_call | solution.py:149
  114.3 10.9 %project.11 = (bf16[128,32,384]{2,1,0:T(8,128)(2,1)}, bf16[128,32,384]{2,1,0:T(8,128)(2,1)}) custom-call(bf16[16,4,96,128]{3,2,1,0:T(8,128)(2,1)} %collective-permute-done.5.refs_0_.refs_1_.refs_2_.refs_3_.refs_5_.refs_10_, bf16[16,4,96,128]{3,2,1,0:T(8,128)(2,1)} %collective-permute-done.5.refs_0_.refs_1_.refs_2_.refs_3_.refs_5_.refs_10_, ...), custom_call_target="tpu_custom_call" | custom-call | flops 1610612736 | bytes 9437184 | tf_op jit(solution)/shard_map/project/pallas_call | solution.py:149
  125.2 0.5 collective-permute-start.9
  125.7 1.5 collective-permute-start.7
  127.2 0.8 pad_maximum_fusion
  128.1 0.1 fusion.3
  128.1 0.9 maximum_select_fusion
  129.1 0.1 fusion.2
  129.2 0.8 maximum_select_fusion.1.refs_15_.refs_4_
  129.9 12.4 %triangle.9 = (bf16[48,1,96,128]{3,2,1,0:T(8,128)(2,1)}, bf16[48,1,96,128]{3,2,1,0:T(8,128)(2,1)}) custom-call(s32[1]{0:T(128)} %bitcast.where_ref, bf16[128,32,384]{2,1,0:T(8,128)(2,1)} %get-tuple-element.26.refs_13_.refs_0_, bf16[128,32,384]{2,1,0:T(8,128)(2,1)} %get-tuple-element.28.refs_1_.refs_14_, ...), custom_call_target="tpu_custom_call" | custom-call | flops 1415577600 | bytes 15728640 | tf_op jit(solution)/shard_map/triangle/pallas_call | solution.py:312
  142.3 6.8 %project.12 = (bf16[128,16,384]{2,1,0:T(8,128)(2,1)}, bf16[128,16,384]{2,1,0:T(8,128)(2,1)}) custom-call(bf16[16,4,96,128]{3,2,1,0:T(8,128)(2,1)} %collective-permute-done.8.refs_0_.refs_1_.refs_2_.refs_3_.refs_5_, bf16[16,4,96,128]{3,2,1,0:T(8,128)(2,1)} %collective-permute-done.8.refs_0_.refs_1_.refs_2_.refs_3_.refs_5_, ...), custom_call_target="tpu_custom_call" | custom-call | flops 805306368 | bytes 4718592 | tf_op jit(solution)/shard_map/project/pallas_call | solution.py:149
  149.2 13.2 %collective-permute-done.7.refs_0_.refs_1_.refs_2_.refs_3_.refs_11_.refs_4_ = bf16[16,4,96,128]{3,2,1,0:T(8,128)(2,1)} collective-permute-done((bf16[16,4,96,128]{3,2,1,0:T(8,128)(2,1)}, bf16[16,4,96,128]{3,2,1,0:T(8,128)(2,1)}, u32[]{:S(2)}, u32[]{:S(2)}) %collective-permute-start.7) | collective-permute-done | bytes 1572896 | tf_op jit(solution)/shard_map/ppermute | solution.py:342
  162.4 7.1 %project.13 = (bf16[128,16,384]{2,1,0:T(8,128)(2,1)}, bf16[128,16,384]{2,1,0:T(8,128)(2,1)}) custom-call(bf16[16,4,96,128]{3,2,1,0:T(8,128)(2,1)} %collective-permute-done.7.refs_0_.refs_1_.refs_2_.refs_3_.refs_11_.refs_4_, bf16[16,4,96,128]{3,2,1,0:T(8,128)(2,1)} %collective-permute-done.7.refs_0_.refs_1_.refs_2_.refs_3_.refs_11_.refs_4_, ...), custom_call_target="tpu_custom_call" | custom-call | flops 805306368 | bytes 4718592 | tf_op jit(solution)/shard_map/project/pallas_call | solution.py:149
  169.6 11.0 %triangle.10.refs_14_.refs_2_.refs_5_ = bf16[48,1,96,128]{3,2,1,0:T(8,128)(2,1)} custom-call(s32[1]{0:T(128)} %bitcast.where_ref, bf16[128,32,384]{2,1,0:T(8,128)(2,1)} %get-tuple-element.26.refs_13_.refs_0_, bf16[128,32,384]{2,1,0:T(8,128)(2,1)} %get-tuple-element.28.refs_1_.refs_14_, bf16[128,16,384]{2,1,0:T(8,128)(2,1)} %get-tuple-element.32.refs_2_.refs_18_.refs_0_, ...), custom_call_target="tpu_custom_call" | custom-call | flops 1061683200 | bytes 14155776 | tf_op jit(solution)/shard_map/triangle/pallas_call | solution.py:312
  180.6 1.5 collective-permute-start.13
  182.1 0.5 collective-permute-start.15
  182.6 10.7 %triangle.11.refs_14_.refs_1_.refs_10_ = bf16[48,1,96,128]{3,2,1,0:T(8,128)(2,1)} custom-call(s32[1]{0:T(128)} %bitcast.where_ref, bf16[128,48,384]{2,1,0:T(8,128)(2,1)} %get-tuple-element.23.refs_0_.refs_10_, bf16[128,32,384]{2,1,0:T(8,128)(2,1)} %get-tuple-element.25.refs_3_.refs_1_, bf16[128,32,384]{2,1,0:T(8,128)(2,1)} %get-tuple-element.27.refs_4_.refs_2_, ...), custom_call_target="tpu_custom_call" | custom-call | flops 1061683200 | bytes 14155776 | tf_op jit(solution)/shard_map/triangle/pallas_call | solution.py:312
  193.3 10.8 %triangle.12.refs_12_.refs_2_.refs_11_ = bf16[48,1,96,128]{3,2,1,0:T(8,128)(2,1)} custom-call(s32[1]{0:T(128)} %bitcast.where_ref, bf16[128,48,384]{2,1,0:T(8,128)(2,1)} %get-tuple-element.23.refs_0_.refs_10_, bf16[128,32,384]{2,1,0:T(8,128)(2,1)} %get-tuple-element.25.refs_3_.refs_1_, bf16[128,32,384]{2,1,0:T(8,128)(2,1)} %get-tuple-element.27.refs_4_.refs_2_, ...), custom_call_target="tpu_custom_call" | custom-call | flops 1061683200 | bytes 14155776 | tf_op jit(solution)/shard_map/triangle/pallas_call | solution.py:312
  204.1 1.5 collective-permute-start.16
  205.6 0.5 collective-permute-start.19
  206.1 1.5 collective-permute-start.20
  207.6 2.1 collective-permute-done.13.refs_3_
  209.7 0.3 collective-permute-start.18
  210.1 8.9 %triangle.13 = (bf16[48,1,96,128]{3,2,1,0:T(8,128)(2,1)}, bf16[48,1,96,128]{3,2,1,0:T(8,128)(2,1)}) custom-call(s32[1]{0:T(128)} %bitcast.where_ref, bf16[128,16,384]{2,1,0:T(8,128)(2,1)} %get-tuple-element.32.refs_2_.refs_18_.refs_0_, bf16[128,16,384]{2,1,0:T(8,128)(2,1)} %get-tuple-element.30.refs_8_.refs_1_, ...), custom_call_target="tpu_custom_call", output_to_operand_aliasing={{0}: (14, {}), {1}: (15, {})} | custom-call | flops 707788800 | bytes 12582912 | tf_op jit(solution)/shard_map/triangle/pallas_call | solution.py:312
  218.9 14.9 %project.14 = (bf16[128,48,384]{2,1,0:T(8,128)(2,1)}, bf16[128,48,384]{2,1,0:T(8,128)(2,1)}) custom-call(bf16[48,1,96,128]{3,2,1,0:T(8,128)(2,1)} %triangle.8.refs_13_.refs_0_.refs_9_, bf16[48,1,96,128]{3,2,1,0:T(8,128)(2,1)} %triangle.11.refs_14_.refs_1_.refs_10_, bf16[48,1,96,128]{3,2,1,0:T(8,128)(2,1)} %triangle.12.refs_12_.refs_2_.refs_11_, ...), custom_call_target="tpu_custom_call" | custom-call | flops 2415919104 | bytes 14155776 | tf_op jit(solution)/shard_map/project/pallas_call | solution.py:149
  233.8 1.2 collective-permute-done.15.refs_1_
  235.0 24.8 %collective-permute-done.16.refs_3_ = bf16[48,1,96,128]{3,2,1,0:T(8,128)(2,1)} collective-permute-done((bf16[48,1,96,128]{3,2,1,0:T(8,128)(2,1)}, bf16[48,1,96,128]{3,2,1,0:T(8,128)(2,1)}, u32[]{:S(2)}, u32[]{:S(2)}) %collective-permute-start.16) | collective-permute-done | bytes 1179680 | tf_op jit(solution)/shard_map/ppermute | solution.py:342
  259.8 14.6 %project.15 = (bf16[128,48,384]{2,1,0:T(8,128)(2,1)}, bf16[128,48,384]{2,1,0:T(8,128)(2,1)}) custom-call(bf16[48,1,96,128]{3,2,1,0:T(8,128)(2,1)} %get-tuple-element.35.refs_8_.refs_0_, bf16[48,1,96,128]{3,2,1,0:T(8,128)(2,1)} %collective-permute-done.15.refs_1_, bf16[48,1,96,128]{3,2,1,0:T(8,128)(2,1)} %triangle.10.refs_14_.refs_2_.refs_5_, ...), custom_call_target="tpu_custom_call" | custom-call | flops 2415919104 | bytes 14155776 | tf_op jit(solution)/shard_map/project/pallas_call | solution.py:149
  274.4 0.5 collective-permute-start.14
  274.9 9.1 %collective-permute-done.18.refs_1_ = bf16[48,1,96,128]{3,2,1,0:T(8,128)(2,1)} collective-permute-done((bf16[48,1,96,128]{3,2,1,0:T(8,128)(2,1)}, bf16[48,1,96,128]{3,2,1,0:T(8,128)(2,1)}, u32[]{:S(2)}, u32[]{:S(2)}) %collective-permute-start.18) | collective-permute-done | bytes 1179680 | tf_op jit(solution)/shard_map/ppermute | solution.py:342
  284.0 8.1 %project.16.refs_8_.refs_1_.refs_5_ = bf16[128,32,384]{2,1,0:T(8,128)(2,1)} custom-call(bf16[48,1,96,128]{3,2,1,0:T(8,128)(2,1)} %get-tuple-element.39.refs_0_, bf16[48,1,96,128]{3,2,1,0:T(8,128)(2,1)} %collective-permute-done.18.refs_1_, bf16[48,1,96,128]{3,2,1,0:T(8,128)(2,1)} %collective-permute-done.19.refs_2_, ...), custom_call_target="tpu_custom_call" | custom-call | flops 805306368 | bytes 6291456 | tf_op jit(solution)/shard_map/project/pallas_call | solution.py:149
  292.2 5.4 %project.17.refs_2_.refs_12_.refs_6_ = bf16[128,16,384]{2,1,0:T(8,128)(2,1)} custom-call(bf16[48,1,96,128]{3,2,1,0:T(8,128)(2,1)} %get-tuple-element.39.refs_0_, bf16[48,1,96,128]{3,2,1,0:T(8,128)(2,1)} %collective-permute-done.18.refs_1_, bf16[48,1,96,128]{3,2,1,0:T(8,128)(2,1)} %collective-permute-done.19.refs_2_, ...), custom_call_target="tpu_custom_call" | custom-call | flops 402653184 | bytes 3145728 | tf_op jit(solution)/shard_map/project/pallas_call | solution.py:149
  297.6 0.5 collective-permute-start.22
  298.1 3.4 collective-permute-done.22.refs_4_.refs_8_
  301.5 10.5 %triangle.14.refs_18_ = bf16[48,1,96,128]{3,2,1,0:T(8,128)(2,1)} custom-call(s32[1]{0:T(128)} %bitcast.where_ref, bf16[128,48,384]{2,1,0:T(8,128)(2,1)} %get-tuple-element.40.refs_8_.refs_0_, bf16[128,32,384]{2,1,0:T(8,128)(2,1)} %project.16.refs_8_.refs_1_.refs_5_, bf16[128,16,384]{2,1,0:T(8,128)(2,1)} %project.17.refs_2_.refs_12_.refs_6_, ...), custom_call_target="tpu_custom_call" | custom-call | flops 1061683200 | bytes 14155776 | tf_op jit(solution)/shard_map/triangle/pallas_call | solution.py:312
  312.0 0.6 collective-permute-start.23
  312.5 27.0 %triangle.15 = bf16[48,4,96,128]{3,2,1,0:T(8,128)(2,1)} custom-call(s32[1]{0:T(128)} %bitcast.where_ref, bf16[128,48,384]{2,1,0:T(8,128)(2,1)} %get-tuple-element.36.refs_8_.refs_0_, bf16[128,48,384]{2,1,0:T(8,128)(2,1)} %get-tuple-element.37.refs_1_, bf16[128,48,384]{2,1,0:T(8,128)(2,1)} %collective-permute-done.14.refs_2_, ...), custom_call_target="tpu_custom_call" | custom-call | flops 3185049600 | bytes 23592960 | tf_op jit(solution)/shard_map/triangle/pallas_call | solution.py:312
  339.5 1.0 collective-permute-done.23
  340.5 2.5 constant_dynamic-update-slice_fusion.5
  (37 shorter events, 0.3 us)
Async XLA Ops:
  24.1 15.5 %collective-permute-start = (bf16[128,48,384]{2,1,0:T(8,128)(2,1)}, bf16[128,48,384]{2,1,0:T(8,128)(2,1)}, u32[]{:S(2)}, u32[]{:S(2)}) collective-permute-start(bf16[128,48,384]{2,1,0:T(8,128)(2,1)} %get-tuple-element.24.refs_1_.refs_2_), channel_id=1, source_target_pairs={{0,1},{1,0},{2,3},{3,2},{4,5},{5,4},{6,7},{7,6}} | collective-permute-start | bytes 14155784 | tf_op jit(solution)/shard_map/ppermute | solution.py:342
  25.0 12.8 %collective-permute-start.3 = (bf16[48,384]{1,0:T(8,128)(2,1)}, bf16[48,384]{1,0:T(8,128)(2,1)}, u32[]{:S(2)}, u32[]{:S(2)}) collective-permute-start(bf16[48,384]{1,0:T(8,128)(2,1)} %convert_element_type.97.refs_4_), channel_id=1, source_target_pairs={{0,2},{1,3},{2,0},{3,1},{4,6},{5,7},{6,4},{7,5}} | collective-permute-start | bytes 110600 | tf_op jit(solution)/shard_map/ppermute | solution.py:342
  30.2 8.1 %copy-start.1 = (bf16[2,128]{1,0:T(2,128)(2,1)S(1)}, bf16[2,128]{1,0:T(2,128)(2,1)}, u32[]{:S(2)}) copy-start(bf16[2,128]{1,0:T(2,128)(2,1)} %param.14) | copy-start | bytes 1540
  30.2 8.1 %copy-start.2 = (bf16[2,128]{1,0:T(2,128)(2,1)S(1)}, bf16[2,128]{1,0:T(2,128)(2,1)}, u32[]{:S(2)}) copy-start(bf16[2,128]{1,0:T(2,128)(2,1)} %param.15) | copy-start | bytes 1540
  30.2 8.1 %copy-start.3 = (bf16[2,128]{1,0:T(2,128)(2,1)S(1)}, bf16[2,128]{1,0:T(2,128)(2,1)}, u32[]{:S(2)}) copy-start(bf16[2,128]{1,0:T(2,128)(2,1)} %param.23) | copy-start | bytes 1540
  30.2 8.1 %copy-start.4 = (bf16[2,128]{1,0:T(2,128)(2,1)S(1)}, bf16[2,128]{1,0:T(2,128)(2,1)}, u32[]{:S(2)}) copy-start(bf16[2,128]{1,0:T(2,128)(2,1)} %param.19) | copy-start | bytes 1540
  30.2 8.7 %copy-start = (bf16[2,128,128]{2,1,0:T(8,128)(2,1)S(1)}, bf16[2,128,128]{2,1,0:T(8,128)(2,1)}, u32[]{:S(2)}) copy-start(bf16[2,128,128]{2,1,0:T(8,128)(2,1)} %param.18) | copy-start | bytes 196612
  30.2 73.1 %collective-permute-start.1 = (bf16[16,4,96,128]{3,2,1,0:T(8,128)(2,1)}, bf16[16,4,96,128]{3,2,1,0:T(8,128)(2,1)}, u32[]{:S(2)}, u32[]{:S(2)}) collective-permute-start(bf16[16,4,96,128]{3,2,1,0:T(8,128)(2,1)} %bitcast.7), channel_id=1, source_target_pairs={{0,2},{1,3},{2,0},{3,1},{4,6},{5,7},{6,4},{7,5}} | collective-permute-start | bytes 4718600 | tf_op jit(solution)/shard_map/ppermute | solution.py:342
  30.3 73.1 %collective-permute-start.2 = (bf16[16,4,96,128]{3,2,1,0:T(8,128)(2,1)}, bf16[16,4,96,128]{3,2,1,0:T(8,128)(2,1)}, u32[]{:S(2)}, u32[]{:S(2)}) collective-permute-start(bf16[16,4,96,128]{3,2,1,0:T(8,128)(2,1)} %bitcast.7), channel_id=1, source_target_pairs={{0,4},{1,5},{2,6},{3,7},{4,0},{5,1},{6,2},{7,3}} | collective-permute-start | bytes 4718600 | tf_op jit(solution)/shard_map/ppermute | solution.py:342
  36.3 78.0 %collective-permute-start.5 = (bf16[16,4,96,128]{3,2,1,0:T(8,128)(2,1)}, bf16[16,4,96,128]{3,2,1,0:T(8,128)(2,1)}, u32[]{:S(2)}, u32[]{:S(2)}) collective-permute-start(bf16[16,4,96,128]{3,2,1,0:T(8,128)(2,1)} %get-tuple-element.42), channel_id=1, source_target_pairs={{0,2},{1,3},{2,0},{3,1},{4,6},{5,7},{6,4},{7,5}} | collective-permute-start | bytes 4718600 | tf_op jit(solution)/shard_map/ppermute | solution.py:342
  37.8 76.5 %collective-permute-start.6 = (bf16[16,4,96,128]{3,2,1,0:T(8,128)(2,1)}, bf16[16,4,96,128]{3,2,1,0:T(8,128)(2,1)}, u32[]{:S(2)}, u32[]{:S(2)}) collective-permute-start(bf16[16,4,96,128]{3,2,1,0:T(8,128)(2,1)} %get-tuple-element.42), channel_id=1, source_target_pairs={{0,4},{1,5},{2,6},{3,7},{4,0},{5,1},{6,2},{7,3}} | collective-permute-start | bytes 4718600 | tf_op jit(solution)/shard_map/ppermute | solution.py:342
  39.6 62.0 %collective-permute-start.4 = (bf16[48,384]{1,0:T(8,128)(2,1)}, bf16[48,384]{1,0:T(8,128)(2,1)}, u32[]{:S(2)}, u32[]{:S(2)}) collective-permute-start(bf16[48,384]{1,0:T(8,128)(2,1)} %convert_element_type.97.refs_4_), channel_id=1, source_target_pairs={{0,4},{1,5},{2,6},{3,7},{4,0},{5,1},{6,2},{7,3}} | collective-permute-start | bytes 110600 | tf_op jit(solution)/shard_map/ppermute | solution.py:342
  101.6 40.7 %collective-permute-start.8 = (bf16[16,4,96,128]{3,2,1,0:T(8,128)(2,1)}, bf16[16,4,96,128]{3,2,1,0:T(8,128)(2,1)}, u32[]{:S(2)}, u32[]{:S(2)}) collective-permute-start(bf16[16,4,96,128]{3,2,1,0:T(8,128)(2,1)} %get-tuple-element.41), channel_id=1, source_target_pairs={{0,4},{1,5},{2,6},{3,7},{4,0},{5,1},{6,2},{7,3}} | collective-permute-start | bytes 4718600 | tf_op jit(solution)/shard_map/ppermute | solution.py:342
  125.2 44.4 %collective-permute-start.10 = (bf16[128,32,384]{2,1,0:T(8,128)(2,1)}, bf16[128,32,384]{2,1,0:T(8,128)(2,1)}, u32[]{:S(2)}, u32[]{:S(2)}) collective-permute-start(bf16[128,32,384]{2,1,0:T(8,128)(2,1)} %get-tuple-element.27.refs_4_.refs_2_), channel_id=1, source_target_pairs={{0,1},{1,0},{2,3},{3,2},{4,5},{5,4},{6,7},{7,6}} | collective-permute-start | bytes 9437192 | tf_op jit(solution)/shard_map/ppermute | solution.py:342
  125.2 44.3 %collective-permute-start.9 = (bf16[128,32,384]{2,1,0:T(8,128)(2,1)}, bf16[128,32,384]{2,1,0:T(8,128)(2,1)}, u32[]{:S(2)}, u32[]{:S(2)}) collective-permute-start(bf16[128,32,384]{2,1,0:T(8,128)(2,1)} %get-tuple-element.25.refs_3_.refs_1_), channel_id=1, source_target_pairs={{0,1},{1,0},{2,3},{3,2},{4,5},{5,4},{6,7},{7,6}} | collective-permute-start | bytes 9437192 | tf_op jit(solution)/shard_map/ppermute | solution.py:342
  125.7 36.7 %collective-permute-start.7 = (bf16[16,4,96,128]{3,2,1,0:T(8,128)(2,1)}, bf16[16,4,96,128]{3,2,1,0:T(8,128)(2,1)}, u32[]{:S(2)}, u32[]{:S(2)}) collective-permute-start(bf16[16,4,96,128]{3,2,1,0:T(8,128)(2,1)} %get-tuple-element.41), channel_id=1, source_target_pairs={{0,2},{1,3},{2,0},{3,1},{4,6},{5,7},{6,4},{7,5}} | collective-permute-start | bytes 4718600 | tf_op jit(solution)/shard_map/ppermute | solution.py:342
  149.2 20.4 %collective-permute-start.12 = (bf16[128,16,384]{2,1,0:T(8,128)(2,1)}, bf16[128,16,384]{2,1,0:T(8,128)(2,1)}, u32[]{:S(2)}, u32[]{:S(2)}) collective-permute-start(bf16[128,16,384]{2,1,0:T(8,128)(2,1)} %get-tuple-element.33.refs_5_.refs_3_), channel_id=1, source_target_pairs={{0,1},{1,0},{2,3},{3,2},{4,5},{5,4},{6,7},{7,6}} | collective-permute-start | bytes 4718600 | tf_op jit(solution)/shard_map/ppermute | solution.py:342
  169.5 13.1 %collective-permute-start.11 = (bf16[128,16,384]{2,1,0:T(8,128)(2,1)}, bf16[128,16,384]{2,1,0:T(8,128)(2,1)}, u32[]{:S(2)}, u32[]{:S(2)}) collective-permute-start(bf16[128,16,384]{2,1,0:T(8,128)(2,1)} %get-tuple-element.31.refs_3_), channel_id=1, source_target_pairs={{0,1},{1,0},{2,3},{3,2},{4,5},{5,4},{6,7},{7,6}} | collective-permute-start | bytes 4718600 | tf_op jit(solution)/shard_map/ppermute | solution.py:342
  180.6 29.2 %collective-permute-start.13 = (bf16[48,1,96,128]{3,2,1,0:T(8,128)(2,1)}, bf16[48,1,96,128]{3,2,1,0:T(8,128)(2,1)}, u32[]{:S(2)}, u32[]{:S(2)}) collective-permute-start(bf16[48,1,96,128]{3,2,1,0:T(8,128)(2,1)} %triangle.10.refs_14_.refs_2_.refs_5_), channel_id=1, source_target_pairs={{0,2},{1,3},{2,0},{3,1},{4,6},{5,7},{6,4},{7,5}} | collective-permute-start | bytes 3538952 | tf_op jit(solution)/shard_map/ppermute | solution.py:342
  182.1 52.9 %collective-permute-start.15 = (bf16[48,1,96,128]{3,2,1,0:T(8,128)(2,1)}, bf16[48,1,96,128]{3,2,1,0:T(8,128)(2,1)}, u32[]{:S(2)}, u32[]{:S(2)}) collective-permute-start(bf16[48,1,96,128]{3,2,1,0:T(8,128)(2,1)} %triangle.8.refs_13_.refs_0_.refs_9_), channel_id=1, source_target_pairs={{0,2},{1,3},{2,0},{3,1},{4,6},{5,7},{6,4},{7,5}} | collective-permute-start | bytes 3538952 | tf_op jit(solution)/shard_map/ppermute | solution.py:342
  204.1 55.7 %collective-permute-start.16 = (bf16[48,1,96,128]{3,2,1,0:T(8,128)(2,1)}, bf16[48,1,96,128]{3,2,1,0:T(8,128)(2,1)}, u32[]{:S(2)}, u32[]{:S(2)}) collective-permute-start(bf16[48,1,96,128]{3,2,1,0:T(8,128)(2,1)} %triangle.12.refs_12_.refs_2_.refs_11_), channel_id=1, source_target_pairs={{0,2},{1,3},{2,0},{3,1},{4,6},{5,7},{6,4},{7,5}} | collective-permute-start | bytes 3538952 | tf_op jit(solution)/shard_map/ppermute | solution.py:342
  205.6 69.3 %collective-permute-start.19 = (bf16[48,1,96,128]{3,2,1,0:T(8,128)(2,1)}, bf16[48,1,96,128]{3,2,1,0:T(8,128)(2,1)}, u32[]{:S(2)}, u32[]{:S(2)}) collective-permute-start(bf16[48,1,96,128]{3,2,1,0:T(8,128)(2,1)} %triangle.8.refs_13_.refs_0_.refs_9_), channel_id=1, source_target_pairs={{0,4},{1,5},{2,6},{3,7},{4,0},{5,1},{6,2},{7,3}} | collective-permute-start | bytes 3538952 | tf_op jit(solution)/shard_map/ppermute | solution.py:342
  206.1 68.8 %collective-permute-start.20 = (bf16[48,1,96,128]{3,2,1,0:T(8,128)(2,1)}, bf16[48,1,96,128]{3,2,1,0:T(8,128)(2,1)}, u32[]{:S(2)}, u32[]{:S(2)}) collective-permute-start(bf16[48,1,96,128]{3,2,1,0:T(8,128)(2,1)} %triangle.11.refs_14_.refs_1_.refs_10_), channel_id=1, source_target_pairs={{0,4},{1,5},{2,6},{3,7},{4,0},{5,1},{6,2},{7,3}} | collective-permute-start | bytes 3538952 | tf_op jit(solution)/shard_map/ppermute | solution.py:342
  209.7 74.2 %collective-permute-start.18 = (bf16[48,1,96,128]{3,2,1,0:T(8,128)(2,1)}, bf16[48,1,96,128]{3,2,1,0:T(8,128)(2,1)}, u32[]{:S(2)}, u32[]{:S(2)}) collective-permute-start(bf16[48,1,96,128]{3,2,1,0:T(8,128)(2,1)} %collective-permute-done.13.refs_3_), channel_id=1, source_target_pairs={{0,4},{1,5},{2,6},{3,7},{4,0},{5,1},{6,2},{7,3}} | collective-permute-start | bytes 3538952 | tf_op jit(solution)/shard_map/ppermute | solution.py:342
  274.4 38.1 %collective-permute-start.17 = (bf16[128,48,384]{2,1,0:T(8,128)(2,1)}, bf16[128,48,384]{2,1,0:T(8,128)(2,1)}, u32[]{:S(2)}, u32[]{:S(2)}) collective-permute-start(bf16[128,48,384]{2,1,0:T(8,128)(2,1)} %get-tuple-element.38.refs_3_), channel_id=1, source_target_pairs={{0,1},{1,0},{2,3},{3,2},{4,5},{5,4},{6,7},{7,6}} | collective-permute-start | bytes 14155784 | tf_op jit(solution)/shard_map/ppermute | solution.py:342
  274.4 38.1 %collective-permute-start.14 = (bf16[128,48,384]{2,1,0:T(8,128)(2,1)}, bf16[128,48,384]{2,1,0:T(8,128)(2,1)}, u32[]{:S(2)}, u32[]{:S(2)}) collective-permute-start(bf16[128,48,384]{2,1,0:T(8,128)(2,1)} %get-tuple-element.37.refs_1_), channel_id=1, source_target_pairs={{0,1},{1,0},{2,3},{3,2},{4,5},{5,4},{6,7},{7,6}} | collective-permute-start | bytes 14155784 | tf_op jit(solution)/shard_map/ppermute | solution.py:342
  292.1 9.4 %collective-permute-start.21 = (bf16[128,32,384]{2,1,0:T(8,128)(2,1)}, bf16[128,32,384]{2,1,0:T(8,128)(2,1)}, u32[]{:S(2)}, u32[]{:S(2)}) collective-permute-start(bf16[128,32,384]{2,1,0:T(8,128)(2,1)} %project.16.refs_8_.refs_1_.refs_5_), channel_id=1, source_target_pairs={{0,1},{1,0},{2,3},{3,2},{4,5},{5,4},{6,7},{7,6}} | collective-permute-start | bytes 9437192 | tf_op jit(solution)/shard_map/ppermute | solution.py:342
  297.6 3.9 %collective-permute-start.22 = (bf16[128,16,384]{2,1,0:T(8,128)(2,1)}, bf16[128,16,384]{2,1,0:T(8,128)(2,1)}, u32[]{:S(2)}, u32[]{:S(2)}) collective-permute-start(bf16[128,16,384]{2,1,0:T(8,128)(2,1)} %project.17.refs_2_.refs_12_.refs_6_), channel_id=1, source_target_pairs={{0,1},{1,0},{2,3},{3,2},{4,5},{5,4},{6,7},{7,6}} | collective-permute-start | bytes 4718600 | tf_op jit(solution)/shard_map/ppermute | solution.py:342
  312.0 28.6 %collective-permute-start.23 = (bf16[48,1,96,128]{3,2,1,0:T(8,128)(2,1)}, bf16[48,1,96,128]{3,2,1,0:T(8,128)(2,1)}, u32[]{:S(2)}, u32[]{:S(2)}) collective-permute-start(bf16[48,1,96,128]{3,2,1,0:T(8,128)(2,1)} %triangle.14.refs_18_), channel_id=1, source_target_pairs={{0,2},{1,3},{2,0},{3,1},{4,6},{5,7},{6,4},{7,5}} | collective-permute-start | bytes 3538952 | tf_op jit(solution)/shard_map/ppermute | solution.py:342
